TPU v7x, 32 devices: a whole 2x2x4 slice. The times are simulated.
32 devices in a mesh: dp: 8 (over z, y), tensor: 4 (over x, core).
Axes of the slice: x: 2, y: 2, z: 4, core: 2. Of those that a mesh axis runs over, the one named last changes fastest.
Arguments:
- acts: bfloat16 [8192, 5120], P('dp', 'tensor'), may hold values from -6 to 6
- out_grad: bfloat16 [8192, 2048], P(('dp', 'tensor')), may hold values from -0.1875 to 0.1875
- momentum: float32 [40960, 2048], P(('dp', 'tensor')), may hold values from -100 to 100
- q_basis: float32 [2048, 256], P('tensor'), may hold values from -0.125 to 0.125
Outputs:
- new_momentum: float32 [40960, 2048], P(('dp', 'tensor'))
- ortho: float32 [5120, 256], P('tensor')
- new_q: float32 [2048, 256], P('tensor')
All inputs are finite; a program needn't handle non-finite values.
Results may differ from a plain program's by a relative error of at most 0.0003.
Values may be sent and summed in bfloat16 or wider, within the bound.
No kernel may reach another device: no remote copies, remote signals or barrier semaphores. Data moves between devices by JAX's collectives and lax.ppermute only.
A program may use at most 64 MiB of HBM per device.

v0:
```python
import jax
import jax.numpy as jnp
from jax import lax
from jax.sharding import PartitionSpec as P

HIGH = lax.Precision.HIGHEST


def contract_rows(first, second):
    return lax.dot_general(
        first, second, (((0,), (0,)), ((), ())), precision=HIGH, preferred_element_type=jnp.float32
    )


def orthonormal(left, gram):
    chol = jnp.linalg.cholesky(gram)
    return lax.linalg.triangular_solve(chol, left, left_side=False, lower=True, transpose_a=True)


def body(acts, out_grad, momentum, q_basis):
    replicas = lax.axis_size("dp")
    grad = lax.dot_general(
        acts,
        lax.all_gather(out_grad, "tensor", axis=0, tiled=True),
        (((0,), (0,)), ((), ())),
        preferred_element_type=jnp.float32,
    )
    buffer = 0.95 * momentum + grad
    columns = buffer
    left_local = jnp.dot(
        columns,
        lax.all_gather(q_basis, "tensor", axis=0, tiled=True),
        precision=HIGH,
        preferred_element_type=jnp.float32,
    )
    left = lax.psum(left_local, "dp") / replicas
    gram = lax.psum(contract_rows(left, left), "tensor")
    ortho = orthonormal(left, gram)
    columns = buffer
    right_share = lax.psum_scatter(
        contract_rows(columns, ortho), "tensor", scatter_dimension=0, tiled=True
    )
    right_share = lax.psum(right_share, "dp") / replicas
    col_squares = lax.psum(jnp.sum(right_share * right_share, axis=0, keepdims=True), "tensor")
    new_q = right_share * lax.rsqrt(col_squares + 1e-06)
    columns = buffer
    update = lax.dot_general(
        ortho,
        lax.all_gather(right_share.astype(jnp.bfloat16), "tensor", axis=0, tiled=True).astype(
            jnp.float32
        ),
        (((1,), (1,)), ((), ())),
        precision=HIGH,
        preferred_element_type=jnp.float32,
    )
    new_momentum = columns - 0.05 * update
    return (new_momentum, ortho, new_q)


def solution(mesh):
    in_specs = (
        P("dp", "tensor"),
        P(("dp", "tensor"), None),
        P(("dp", "tensor"), None),
        P("tensor", None),
    )
    out_specs = (P(("dp", "tensor"), None), P("tensor", None), P("tensor", None))
    return jax.shard_map(body, mesh=mesh, in_specs=in_specs, out_specs=out_specs, check_vma=False)
```

profile of v0, /device:TPU:0, one launch (start us, length us, event | category | flops | bytes accessed | tf_op | source)
XLA Modules:
  0.0 450.7 jit_solution(18422451597590470659)
XLA Ops:
  7.2 0.0 all-gather.4.cloned.1.call-start
  7.2 0.7 all-gather.4.cloned.1.call-update
  7.9 0.0 all-gather.6.cloned.1.call-start
  8.0 0.7 all-gather.6.cloned.1.call-update
  8.7 0.0 all-reduce.5.cloned.1.call-start
  8.7 38.0 %all-gather.4.cloned.1.call-done = bf16[1024,2048]{1,0:T(8,128)(2,1)} async-done(((bf16[256,2048]{1,0:T(8,128)(2,1)}), bf16[1024,2048]{1,0:T(8,128)(2,1)}) %all-gather.4.cloned.1.call-update) | async-done | bytes 4194320 | tf_op jit(solution)/shard_map/all_gather | solution.py:24
  46.8 12.2 %multiply_add_fusion = f32[1280,2048]{1,0:T(8,128)} fusion(f32[1280,2048]{1,0:T(8,128)} %param.6, bf16[1024,1280]{1,0:T(8,128)(2,1)S(1)} %copy-done, bf16[1024,2048]{1,0:T(8,128)(2,1)} %all-gather.4.cloned.1.call-done), kind=kOutput, calls=%fused_computation.3 | convolution fusion | flops 5373952000 | bytes 27787264 | tf_op jit(solution)/shard_map/dot_general | solution.py:22
  58.9 12.0 %all-gather.6.cloned.1.call-done = f32[2048,256]{1,0:T(8,128)} async-done(((f32[512,256]{1,0:T(8,128)}), f32[2048,256]{1,0:T(8,128)}) %all-gather.6.cloned.1.call-update) | async-done | bytes 2097168 | tf_op jit(solution)/shard_map/all_gather | solution.py:32
  70.9 12.5 %fusion.11 = f32[1280,256]{1,0:T(8,128)} fusion(f32[1280,2048]{1,0:T(8,128)} %multiply_add_fusion, f32[2048,256]{1,0:T(8,128)} %all-gather.6.cloned.1.call-done), kind=kOutput, calls=%fused_computation.38 | convolution fusion | flops 8053063680 | bytes 13893632 | tf_op jit(solution)/shard_map/dot_general | solution.py:30
  83.4 0.0 all-reduce.5.cloned.1.call-update
  83.4 0.0 all-reduce.7.cloned.1.call-start
  83.5 83.7 %all-reduce.5.cloned.1.call-done = f32[1280,256]{1,0:T(8,128)} async-done(((f32[1280,256]{1,0:T(8,128)}), f32[1280,256]{1,0:T(8,128)}) %all-reduce.5.cloned.1.call-update) | async-done | bytes 1310736 | tf_op jit(solution)/shard_map/psum | solution.py:36
  167.2 4.8 %fusion.8 = f32[256,256]{0,1:T(8,128)} fusion(f32[1280,256]{1,0:T(8,128)} %all-reduce.5.cloned.1.call-done), kind=kOutput, calls=%fused_computation.35 | convolution fusion | flops 1006960640 | bytes 1572864 | tf_op jit(solution)/shard_map/dot_general | solution.py:10
  172.0 0.0 all-reduce.7.cloned.1.call-update
  172.0 0.2 reduce-scatter.2.cloned.1.call-start
  172.2 2.5 broadcast_multiply_fusion
  174.7 28.8 %all-reduce.7.cloned.1.call-done = f32[256,256]{0,1:T(8,128)} async-done(((f32[256,256]{0,1:T(8,128)}), f32[256,256]{0,1:T(8,128)}) %all-reduce.7.cloned.1.call-update) | async-done | bytes 262160 | tf_op jit(solution)/shard_map/psum | solution.py:37
  203.5 1.1 copy.8
  204.6 1.0 fusion.2
  205.6 11.7 %cholesky.50 = f32[128,128]{1,0:T(8,128)S(1)} custom-call(f32[128,128]{1,0:T(8,128)S(1)} %cholesky.118), custom_call_target="Cholesky" | custom-call | tf_op jit(solution)/shard_map/jit(cholesky)/cholesky | solution.py:16
  217.3 9.8 %custom-call.14 = f32[1,128,128]{1,2,0:T(8,128)S(1)} custom-call(f32[1,128,128]{2,1,0:T(8,128)S(1)} %get-tuple-element.29), custom_call_target="InvertDiagBlocksLowerTriangular" | custom-call | tf_op jit(solution)/shard_map/jit(cholesky)/cholesky | solution.py:16
  227.1 0.2 constant_dynamic-update-slice_fusion.1
  227.4 0.3 convolution_subtract_fusion.1
  227.6 11.7 %cholesky.105 = f32[128,128]{1,0:T(8,128)S(1)} custom-call(f32[128,128]{1,0:T(8,128)S(1)} %convolution_subtract_fusion.1), custom_call_target="Cholesky" | custom-call | tf_op jit(solution)/shard_map/jit(cholesky)/cholesky | solution.py:16
  239.4 0.7 compare_reduce_fusion
  241.4 0.1 triangular_solve.58
  241.4 5.4 %while.1 = (s32[]{:T(128)}, f32[256,256]{1,0:T(8,128)S(1)}, s32[2,2]{1,0:T(2,128)S(1)}, f32[2,128,128]{2,1,0:T(8,128)}, s32[]{:T(128)}) while((s32[]{:T(128)}, f32[256,256]{1,0:T(8,128)S(1)}, s32[2,2]{1,0:T(2,128)S(1)}, f32[2,128,128]{2,1,0:T(8,128)}, s32[]{:T(128)}) %tuple.29), condition=%wide.while_cond, body=%wide.while_body.sunk | while | flops 2 | bytes 132205 | solution.py:17
  241.7 0.6 fusion.23
  242.2 2.0 bitcast_dynamic-update-slice_fusion.2
  244.2 0.6 fusion.23
  244.8 2.0 bitcast_dynamic-update-slice_fusion.2
  246.8 21.1 %custom-call.15 = f32[2,128,128]{1,2,0:T(8,128)} custom-call(f32[2,128,128]{2,1,0:T(8,128)} %get-tuple-element.10), custom_call_target="InvertDiagBlocksLowerTriangular" | custom-call | tf_op jit(solution)/shard_map/triangular_solve | solution.py:17
  267.9 1.8 fusion
  269.8 2.3 convolution_subtract_fusion
  272.1 0.7 fusion.3
  272.8 0.8 copy-done.1
  273.7 20.1 %fusion.9 = f32[2048,256]{1,0:T(8,128)} fusion(f32[1280,2048]{1,0:T(8,128)} %multiply_add_fusion, f32[1280,128]{0,1:T(8,128)S(1)} %fusion.3, f32[1280,128]{0,1:T(8,128)S(1)} %fusion), kind=kOutput, calls=%fused_computation.36 | convolution fusion | flops 8053391360 | bytes 13893632 | tf_op jit(solution)/shard_map/dot_general | solution.py:10
  293.8 0.0 all-reduce.9.cloned.1.call-start
  293.8 31.3 %reduce-scatter.2.cloned.1.call-done = f32[512,256]{1,0:T(8,128)} async-done(((f32[2048,256]{1,0:T(8,128)}), f32[512,256]{1,0:T(8,128)}) %reduce-scatter.2.cloned.1.call-update) | async-done | bytes 524304 | tf_op jit(solution)/shard_map/reduce_scatter | solution.py:40
  325.1 0.0 all-gather.8.cloned.1.call-start
  325.2 75.9 %all-reduce.9.cloned.1.call-done = f32[512,256]{1,0:T(8,128)} async-done(((f32[512,256]{1,0:T(8,128)}), f32[512,256]{1,0:T(8,128)}) %all-reduce.9.cloned.1.call-update) | async-done | bytes 524304 | tf_op jit(solution)/shard_map/psum | solution.py:43
  401.1 1.1 multiply_reduce_fusion
  402.2 5.9 %psum.31 = f32[1,256]{1,0:T(1,128)S(1)} all-reduce(f32[1,256]{1,0:T(1,128)S(1)} %bitcast.39), channel_id=1, replica_groups=mesh['dp'=8,'tensor'=4] {'tensor'}, use_global_device_ids=true, to_apply=%region_9.10 | all-reduce | flops 256 | bytes 2048 | tf_op jit(solution)/shard_map/psum | solution.py:44
  408.1 2.0 broadcast_multiply_fusion.1
  410.2 2.2 pad_maximum_fusion
  412.4 2.8 copy.9
  415.2 11.3 %all-gather.8.cloned.1.call-done = bf16[2048,256]{1,0:T(8,128)(2,1)} async-done(((bf16[512,256]{1,0:T(8,128)(2,1)}), bf16[2048,256]{1,0:T(8,128)(2,1)}) %all-gather.8.cloned.1.call-update) | async-done | bytes 1048592 | tf_op jit(solution)/shard_map/all_gather | solution.py:49
  426.4 17.0 %multiply_subtract_fusion = f32[1280,2048]{1,0:T(8,128)} fusion(f32[1280,2048]{1,0:T(8,128)} %multiply_add_fusion, bf16[2048,256]{1,0:T(8,128)(2,1)} %all-gather.8.cloned.1.call-done, f32[1280,128]{0,1:T(8,128)} %copy-done.1, f32[1280,128]{0,1:T(8,128)S(1)} %fusion), kind=kOutput, calls=%fused_computation.2 | convolution fusion | flops 8058634240 | bytes 23330816 | tf_op jit(solution)/shard_map/dot_general | solution.py:47
  (18 shorter events, 0.2 us)
Async XLA Ops:
  7.2 39.6 %copy-start = (bf16[1024,1280]{1,0:T(8,128)(2,1)S(1)}, bf16[1024,1280]{1,0:T(8,128)(2,1)}, u32[]{:S(2)}) copy-start(bf16[1024,1280]{1,0:T(8,128)(2,1)} %param.4) | copy-start | bytes 7864324
  7.2 39.6 %all-gather.4.cloned.1.call-start = ((), (), s32[]{:S(2)}) async-start(), calls=%async_computation.1 | async-start | bytes 5242880 | tf_op jit(solution)/shard_map/all_gather | solution.py:24
  7.9 63.0 %all-gather.6.cloned.1.call-start = ((), (), s32[]{:S(2)}) async-start(), calls=%async_computation.2 | async-start | bytes 2621440 | tf_op jit(solution)/shard_map/all_gather | solution.py:32
  8.7 158.5 %all-reduce.5.cloned.1.call-start = ((), (), s32[]{:S(2)}) async-start(), calls=%async_computation.3 | async-start | bytes 2621440 | tf_op jit(solution)/shard_map/psum | solution.py:36
  83.4 120.1 %all-reduce.7.cloned.1.call-start = ((), (), s32[]{:S(2)}) async-start(), calls=%async_computation.4 | async-start | bytes 524288 | tf_op jit(solution)/shard_map/psum | solution.py:37
  172.0 153.1 %reduce-scatter.2.cloned.1.call-start = ((), (), s32[]{:S(2)}) async-start(), calls=%async_computation.5 | async-start | bytes 2621440 | tf_op jit(solution)/shard_map/reduce_scatter | solution.py:40
  267.9 4.1 copy-start.2
  272.8 0.8 copy-start.1
  293.8 107.3 %all-reduce.9.cloned.1.call-start = ((), (), s32[]{:S(2)}) async-start(), calls=%async_computation.6 | async-start | bytes 1048576 | tf_op jit(solution)/shard_map/psum | solution.py:43
  325.1 101.3 %all-gather.8.cloned.1.call-start = ((), (), s32[]{:S(2)}) async-start(), calls=%async_computation.7 | async-start | bytes 1310720 | tf_op jit(solution)/shard_map/all_gather | solution.py:49
Sparse Core Ops, SparseCore 0:
  9.5 37.1 all-gather.3
  48.3 22.5 all-gather.5
  83.5 83.6 all-reduce.4
  172.1 31.3 all-reduce.6
  293.9 31.1 reduce-scatter.1
  328.4 72.6 all-reduce.8
  410.3 16.1 all-gather.7
where the time goes:
time: 458 us; the launch traced here: 451 us
  waiting for transfers between devices  282 us (62%)
  matrix products  71.8 us (16%)
  other arithmetic  63.9 us (14%)
  between operations  16 us (3%)
  local copies, waits for them, and re-layouts  9.95 us (2%)
  blocking collectives  5.91 us (1%)
    psum x1, waiting for transfers between devices, body(): left = lax.psum(left_local, 'dp') / replicas  83.7 us
    psum x1, waiting for transfers between devices, body(): right_share = lax.psum(right_share, 'dp') / replicas  75.9 us
    all_gather x1, waiting for transfers between devices, body(): lax.all_gather(out_grad, 'tensor', axis=0, tiled=True)  38 us
    another operation x6, other arithmetic, orthonormal(): chol = jnp.linalg.cholesky(gram)  34 us
    reduce_scatter x1, waiting for transfers between devices, body(): lax.psum_scatter(contract_rows(columns, ortho), 'tensor', scatter_dimensi...  31.3 us
    psum x1, waiting for transfers between devices, body(): gram = lax.psum(contract_rows(left, left), 'tensor')  28.8 us
    dot_general x2, matrix products, contract_rows(): lax.dot_general(first, second, (((0,), (0,)), ((), ())), precision=HIGH,...  24.9 us
    another operation x4, other arithmetic, orthonormal(): lax.linalg.triangular_solve(chol, left, left_side=False, lower=True, tran...  23.4 us
  transfers between devices with their start and end apart: 7, of which 7 were waited for; matrix products, arithmetic and copies ran while one was open for 4% of the time, Pallas kernels for 0%

commit v1 on v0

v1 whole, which is shorter than its diff:
```python
import functools

import jax
import jax.numpy as jnp
from jax import lax
from jax.experimental import pallas as pl
from jax.experimental.pallas import tpu as pltpu
from jax.sharding import PartitionSpec as P

F32 = jnp.float32
BF16 = jnp.bfloat16
HIGHEST = lax.Precision.HIGHEST
BLOCK = 32
GROUP = 8
LANES = 128


def split3(value):
    high = value.astype(BF16)
    rest = value - high.astype(F32)
    mid = rest.astype(BF16)
    low = (rest - mid.astype(F32)).astype(BF16)
    return high, mid, low


def chol_inverse_kernel(gram_ref, out_ref):
    n = gram_ref.shape[0]
    out_ref[...] = gram_ref[...]
    lane = lax.broadcasted_iota(jnp.int32, (GROUP, n), 1)
    sub = lax.broadcasted_iota(jnp.int32, (GROUP, LANES), 0)

    def wide(v):
        return jnp.concatenate([v] * (n // LANES), axis=1)

    groups = BLOCK // GROUP
    for block in range(n // BLOCK):
        base = block * BLOCK
        tile = [out_ref[pl.ds(base + g * GROUP, GROUP), :] for g in range(groups)]
        for g in range(groups):
            start = base + g * GROUP
            cols = [
                [
                    jnp.broadcast_to(tile[h][:, start + s : start + s + 1], (GROUP, LANES))
                    for h in range(g, groups)
                ]
                for s in range(GROUP)
            ]
            for s in range(GROUP):
                col = start + s
                scale = lax.rsqrt(jnp.broadcast_to(cols[s][0][s : s + 1, :], (GROUP, LANES)))
                factor = [c * scale for c in cols[s]]
                factor[0] = jnp.where(sub > s, factor[0], 0.0)
                pivot = jnp.broadcast_to(tile[g][s : s + 1, :], (GROUP, n)) * wide(scale)
                pivot = jnp.where(lane == col, wide(scale), pivot)
                for later in range(s + 1, GROUP):
                    entry = jnp.broadcast_to(cols[later][0][s : s + 1, :], (GROUP, LANES)) * scale
                    cols[later] = [c - f * entry for c, f in zip(cols[later], factor)]
                for h in range(g, groups):
                    if h == g:
                        kept = jnp.where((lane == col) & (wide(sub) > s), 0.0, tile[h])
                        new = kept - wide(factor[0]) * pivot
                        tile[h] = jnp.where(wide(sub) == s, pivot, new)
                    else:
                        kept = jnp.where(lane == col, 0.0, tile[h])
                        tile[h] = kept - wide(factor[h - g]) * pivot
        for g in range(groups):
            out_ref[pl.ds(base + g * GROUP, GROUP), :] = tile[g]
        rest = base + BLOCK
        if rest < n:
            rows = jnp.concatenate(tile, axis=0)
            lane_b = lax.broadcasted_iota(jnp.int32, (BLOCK, n), 1)
            row_b = lax.broadcasted_iota(jnp.int32, (BLOCK, n), 0) + base
            lower = jnp.where((lane_b > row_b) & (lane_b < rest), 0.0, rows)
            ah, am, al = split3(rows)
            bh, bm, bl = split3(lower)
            first = jnp.concatenate([ah, ah, ah, am, am, al], axis=0)
            second = jnp.concatenate([bh, bm, bl, bh, bm, bh], axis=0)
            change = lax.dot_general(
                first, second, (((0,), (0,)), ((), ())), preferred_element_type=F32
            )
            lane_r = lax.broadcasted_iota(jnp.int32, (n - rest, n), 1)
            old = out_ref[pl.ds(rest, n - rest), :]
            old = jnp.where((lane_r >= base) & (lane_r < rest), 0.0, old)
            out_ref[pl.ds(rest, n - rest), :] = old - change[rest:, :]
    lane_n = lax.broadcasted_iota(jnp.int32, (n, n), 1)
    row_n = lax.broadcasted_iota(jnp.int32, (n, n), 0)
    out_ref[...] = jnp.where(row_n >= lane_n, out_ref[...], 0.0)


def dot(a, b, contract, precision=None):
    return lax.dot_general(
        a, b, (contract, ((), ())), precision=precision, preferred_element_type=F32
    )


NN = ((1,), (0,))
NT = ((1,), (1,))
TN = ((0,), (0,))


def struct(shape, dtype=F32):
    return jax.ShapeDtypeStruct(shape, dtype)


def kernel_call(kernel, name, out, flops, *args, grid=(), in_specs=None, out_specs=None, scratch=()):
    whole = pl.BlockSpec(memory_space=pltpu.VMEM)
    many = isinstance(out, (tuple, list))
    if in_specs is None:
        in_specs = [None] * len(args)
    specs = []
    for spec, arg in zip(in_specs, args):
        if spec is None:
            spec = pl.BlockSpec(memory_space=pltpu.SMEM) if arg.dtype == jnp.int32 else whole
        specs.append(spec)
    if out_specs is None:
        out_specs = type(out)([whole] * len(out)) if many else whole
    moved = sum(a.size * a.dtype.itemsize for a in list(args) + list(out if many else [out]))
    return pl.pallas_call(
        kernel,
        out_shape=out,
        grid=grid,
        in_specs=specs,
        out_specs=out_specs,
        scratch_shapes=list(scratch),
        cost_estimate=pl.CostEstimate(flops=flops, bytes_accessed=moved, transcendentals=0),
        compiler_params=pltpu.CompilerParams(vmem_limit_bytes=34 * 1024 * 1024),
        name=name,
    )(*args)


def split2(value):
    high = value.astype(BF16)
    return high, (value - high.astype(F32)).astype(BF16)


def rows_at(index, rows):
    return pl.ds(pl.multiple_of(index * rows, rows), rows)


def chol_inverse(gram):
    n = gram.shape[0]
    return kernel_call(chol_inverse_kernel, "chol_inverse", struct((n, n)), 150_000_000, gram)


def basis_kernel(count, where_ref, grads_ref, *refs):
    pieces, (pair_ref, out_ref) = refs[:count], refs[count:]
    rows, rank = pieces[0].shape
    for m, piece in enumerate(pieces):
        high, low = split2(piece[...])
        at = rows_at(where_ref[0] ^ m, rows)
        pair_ref[at, :rank] = high
        pair_ref[at, rank:] = low
    both = dot(grads_ref[...], pair_ref[...], NN)
    out_ref[...] = both[:, :rank] + both[:, rank:]


def momentum_kernel(momentum_ref, pair_ref, out_ref):
    rank = out_ref.shape[1]
    high, low = split2(momentum_ref[...])
    both = dot(high, pair_ref[...], NN)
    out_ref[...] = 0.95 * (both[:, :rank] + both[:, rank:] + dot(low, pair_ref[:, :rank], NN))


def left_kernel(count, scale, where_ref, acts_ref, base_ref, *refs):
    pieces, (out_ref, pair_ref) = refs[:count], refs[count:]
    rows, rank = pieces[0].shape

    @pl.when(pl.program_id(0) == 0)
    def _():
        for m, piece in enumerate(pieces):
            high, low = split2(piece[...])
            at = rows_at(where_ref[0] ^ m, rows)
            pair_ref[at, :rank] = high
            pair_ref[at, rank:] = low

    both = dot(acts_ref[...], pair_ref[...], TN)
    out_ref[...] = scale * (base_ref[...] + (both[:, :rank] + both[:, rank:]))


def buffer_kernel(count, where_ref, acts_ref, momentum_ref, *refs):
    pieces, (high_ref, low_ref) = refs[:count], refs[count:]
    rows, columns = pieces[0].shape
    step = 512
    lhs = [acts_ref[rows_at(where_ref[0] ^ m, rows), :] for m in range(count)]
    for start in range(0, columns, step):
        at = slice(start, start + step)
        total = 0.95 * momentum_ref[:, at]
        for m in range(count):
            total = total + dot(lhs[m], pieces[m][:, at], TN)
        high_ref[:, at], low_ref[:, at] = split2(total)


def gram_kernel(*refs):
    pieces, out_ref = refs[:-1], refs[-1]
    total = None
    for piece in pieces:
        value = piece[...]
        term = dot(value, value, TN, HIGHEST)
        total = term if total is None else total + term
    out_ref[...] = total


def share_kernel(count, scale, where_ref, high_ref, low_ref, *refs):
    pieces, (out_ref, pair_ref) = refs[:count], refs[count:]
    rows, rank = pieces[0].shape

    @pl.when(pl.program_id(0) == 0)
    def _():
        for m, piece in enumerate(pieces):
            high, low = split2(piece[...] * scale)
            at = rows_at(where_ref[1] ^ m, rows)
            pair_ref[at, :rank] = high
            pair_ref[at, rank:] = low

    both = dot(pair_ref[...], high_ref[...], TN)
    total = both[:rank] + both[rank:] + dot(pair_ref[:, :rank], low_ref[...], TN)
    out_ref[...] = total.T


def right_kernel(part_ref, inverse_ref, right_ref, narrow_ref):
    right = dot(part_ref[...], inverse_ref[...], NT, HIGHEST)
    right_ref[...] = right
    narrow_ref[...] = right.astype(BF16)


def ortho_kernel(count, where_ref, inverse_ref, *refs):
    pieces, out_ref = refs[:count], refs[count]
    rows = pieces[0].shape[0]
    for m, piece in enumerate(pieces):
        out_ref[rows_at(where_ref[1] ^ m, rows), :] = dot(piece[...], inverse_ref[...], NT, HIGHEST)


def collect_kernel(xs, quad, where_ref, *refs):
    exact, narrow = refs[:quad], refs[quad : quad + (xs - 1) * quad]
    own_ref, side_ref, squares_ref = refs[-3:]
    rows = exact[0].shape[0]
    squares = None
    for m in range(quad):
        value = exact[m][...]
        at = rows_at(where_ref[1] ^ m, rows)
        own_ref[at, :] = value
        side_ref[0, at, :] = value.astype(BF16)
        term = jnp.sum(value * value, axis=0, keepdims=True)
        squares = term if squares is None else squares + term
        for x in range(1, xs):
            side_ref[x, at, :] = narrow[(x - 1) * quad + m][...]
    squares_ref[...] = jnp.broadcast_to(squares, squares_ref.shape)


def update_kernel(xs, where_ref, high_ref, low_ref, ortho_ref, side_ref, other_ref, out_ref, full_ref):
    rows = side_ref.shape[1]
    columns = out_ref.shape[1]

    @pl.when(pl.program_id(0) == 0)
    def _():
        for x in range(xs):
            full_ref[rows_at(where_ref[0] ^ (2 * x), rows), :] = side_ref[x]
            full_ref[rows_at(where_ref[0] ^ (2 * x + 1), rows), :] = other_ref[x]

    ortho = ortho_ref[...].astype(BF16)
    step = 512
    for start in range(0, columns, step):
        at = slice(start, start + step)
        change = dot(ortho, full_ref[at, :], NT)
        value = high_ref[:, at].astype(F32) + low_ref[:, at].astype(F32)
        out_ref[:, at] = value - 0.05 * change


class Exchange:
    def __init__(self, replicas, parts):
        self.replicas, self.parts = replicas, parts
        self.quad = min(4, replicas)
        self.xs = parts // 2
        self.higher = []
        bit = self.quad
        while bit < replicas:
            self.higher.append(bit | (bit >> 1))
            bit *= 2
        d, self.t = lax.axis_index("dp"), lax.axis_index("tensor")
        bits, k, above = [], replicas.bit_length() - 2, 0
        while k >= 0:
            own = (d >> k) & 1
            if k >= 1 and (1 << (k + 1)) < replicas:
                own = own ^ above
            bits.append((k, own))
            above = own
            k -= 1
        self.q = sum(own << k for k, own in bits if (1 << k) < self.quad)
        self.x, self.core = self.t // 2, self.t % 2

    def swap(self, value, dp=0, tensor=0):
        n, m = self.parts, self.replicas
        if dp == 0:
            return lax.ppermute(value, "tensor", [(i, i ^ tensor) for i in range(n)])
        if tensor == 0:
            return lax.ppermute(value, "dp", [(i, i ^ dp) for i in range(m)])
        pairs = [((i // n), i % n) for i in range(m * n)]
        perm = [(d * n + t, (d ^ dp) * n + (t ^ tensor)) for d, t in pairs]
        return lax.ppermute(value, ("dp", "tensor"), perm)

    def gather_tensor(self, value):
        pieces = {0: value, 1: self.swap(value, tensor=1)}
        for m in range(2, self.parts, 2):
            pieces[m] = self.swap(value, tensor=m)
            pieces[m + 1] = self.swap(pieces[m], tensor=1)
        return [pieces[m] for m in range(self.parts)]


def block(value, index, count):
    rows = value.shape[0] // count
    return lax.dynamic_slice_in_dim(value, index * rows, rows, axis=0)


def body(acts, out_grad, momentum, q_basis):
    replicas, parts = lax.axis_size("dp"), lax.axis_size("tensor")
    ex = Exchange(replicas, parts)
    rows, columns = momentum.shape
    tokens = acts.shape[0]
    rank = q_basis.shape[1]
    tile = 256 if rows % 256 == 0 else 128
    steps = rows // tile
    where = jnp.stack([ex.t, ex.q]).astype(jnp.int32)
    wide_spec = pl.BlockSpec((tile, columns), lambda i: (i, 0))
    rank_spec = pl.BlockSpec((tile, rank), lambda i: (i, 0))
    acts_spec = pl.BlockSpec((tokens, tile), lambda i: (0, i))

    basis = ex.gather_tensor(q_basis)
    pair, grad_q = kernel_call(
        functools.partial(basis_kernel, parts), "basis",
        (struct((columns, 2 * rank), BF16), struct((out_grad.shape[0], rank))),
        4 * out_grad.shape[0] * columns * rank, where, out_grad, *basis,
    )
    grads_q = ex.gather_tensor(grad_q)
    base = kernel_call(
        momentum_kernel, "momentum_q", struct((rows, rank)), 6 * rows * columns * rank,
        momentum, pair, grid=(steps,), in_specs=[wide_spec, None], out_specs=rank_spec,
    )
    left = kernel_call(
        functools.partial(left_kernel, parts, 1.0 / replicas), "left", struct((rows, rank)),
        4 * rows * tokens * rank, where, acts, base, *grads_q, grid=(steps,),
        in_specs=[None, acts_spec, rank_spec] + [None] * parts, out_specs=rank_spec,
        scratch=[pltpu.VMEM((tokens, 2 * rank), BF16)],
    )

    held, _ = lax.optimization_barrier((out_grad, grads_q[2 % parts]))
    grads = ex.gather_tensor(held)
    high, low = kernel_call(
        functools.partial(buffer_kernel, parts), "buffer",
        (struct((rows, columns), BF16), struct((rows, columns), BF16)),
        2 * rows * tokens * columns, where, acts, momentum, *grads, grid=(steps,),
        in_specs=[None, acts_spec, wide_spec] + [None] * parts, out_specs=(wide_spec, wide_spec),
    )

    quad = range(1, ex.quad)
    part = block(left, ex.q, ex.quad)
    for piece in [ex.swap(block(left, ex.q ^ m, ex.quad), dp=m) for m in quad]:
        part = part + piece
    for mask in ex.higher:
        part = part + ex.swap(part, dp=mask)
    lefts = [part] + [ex.swap(part, dp=m) for m in quad]

    gram = kernel_call(gram_kernel, "gram", struct((rank, rank)), 12 * rows * rank * rank, *lefts)
    gram = gram + ex.swap(gram, tensor=1)
    total = gram
    for m in range(1, ex.xs):
        total = total + ex.swap(gram, tensor=2 * m)
    inverse = chol_inverse(total)

    step = 512
    half_spec = pl.BlockSpec((rows, step), lambda i: (0, i))
    share = kernel_call(
        functools.partial(share_kernel, ex.quad, 1.0 / replicas), "share", struct((columns, rank)),
        6 * rows * columns * rank, where, high, low, *lefts, grid=(columns // step,),
        in_specs=[None, half_spec, half_spec] + [None] * ex.quad,
        out_specs=pl.BlockSpec((step, rank), lambda i: (i, 0)),
        scratch=[pltpu.VMEM((rows, 2 * rank), BF16)],
    )
    share = share.reshape(ex.xs, 2, -1, rank)
    keep = lax.dynamic_index_in_dim(share, ex.core, 1, keepdims=False)
    send = lax.dynamic_index_in_dim(share, 1 - ex.core, 1, keepdims=False)
    share = (keep + ex.swap(send, tensor=1)).reshape(-1, rank)
    count = ex.xs * ex.quad
    mine = ex.x * ex.quad + ex.q
    part = block(share, mine, count)
    for piece in [
        ex.swap(block(share, mine ^ m, count), dp=m % ex.quad, tensor=2 * (m // ex.quad))
        for m in range(1, count)
    ]:
        part = part + piece
    for mask in ex.higher:
        part = part + ex.swap(part, dp=mask)

    right, narrow = kernel_call(
        right_kernel, "right", (struct(part.shape), struct(part.shape, BF16)),
        12 * part.shape[0] * rank * rank, part, inverse,
    )
    exact = [right] + [ex.swap(right, dp=m) for m in quad]
    across = [
        ex.swap(narrow, dp=m % ex.quad, tensor=2 * (m // ex.quad)) for m in range(ex.quad, count)
    ]
    local = columns // parts
    own, side, squares = kernel_call(
        functools.partial(collect_kernel, ex.xs, ex.quad), "collect",
        (struct((local, rank)), struct((ex.xs, local, rank), BF16), struct((8, rank))),
        2 * local * rank, where, *exact, *across,
    )
    other = ex.swap(side, tensor=1)
    squares = squares + ex.swap(squares, tensor=1)
    col_squares = squares
    for m in range(1, ex.xs):
        col_squares = col_squares + ex.swap(squares, tensor=2 * m)
    new_q = own * lax.rsqrt(col_squares[:1] + 1e-06)

    ortho = kernel_call(
        functools.partial(ortho_kernel, ex.quad), "ortho", struct((rows, rank)),
        12 * rows * rank * rank, where, inverse, *lefts,
    )
    new_momentum = kernel_call(
        functools.partial(update_kernel, ex.xs), "update", struct((rows, columns)),
        2 * rows * columns * rank, where, high, low, ortho, side, other, grid=(steps,),
        in_specs=[None, wide_spec, wide_spec, rank_spec, None, None], out_specs=wide_spec,
        scratch=[pltpu.VMEM((columns, rank), BF16)],
    )
    return (new_momentum, ortho, new_q)


def solution(mesh):
    in_specs = (
        P("dp", "tensor"),
        P(("dp", "tensor"), None),
        P(("dp", "tensor"), None),
        P("tensor", None),
    )
    out_specs = (P(("dp", "tensor"), None), P("tensor", None), P("tensor", None))
    return jax.shard_map(body, mesh=mesh, in_specs=in_specs, out_specs=out_specs, check_vma=False)
```

time: 458 us -> 182 us (0.40); the launches traced: 451 us -> 181 us
  waiting for transfers between devices: 282 us -> 65.2 us
  matrix products: 71.8 us -> 0 us
  other arithmetic: 63.9 us -> 6.24 us
  Pallas kernels: 0 us -> 47.8 us
  starting transfers between devices: 0.45 us -> 47.4 us
  between operations: 16 us -> 0.96 us
  blocking collectives: 5.91 us -> 0 us
    psum x3 -> x0, waiting for transfers between devices: 188 us -> none  [the longest x1 83.7 us: body(): left = lax.psum(left_local, 'dp') / replicas]
    dot_general x5 -> x0, matrix products: 66.5 us -> none  [the longest x2 24.9 us: contract_rows(): lax.dot_general(first, second, (((0,), (0,)), ((), ())), precision=HIGH,...]
    ppermute x0 -> x37, waiting for transfers between devices: none -> 65.2 us  [the longest x17 36.2 us: swap(): return lax.ppermute(value, 'tensor', [(i, i ^ tensor) for i in range(n)])]
    all_gather x3 -> x0, waiting for transfers between devices: 61.3 us -> none  [the longest x1 38 us: body(): lax.all_gather(out_grad, 'tensor', axis=0, tiled=True)]
    another operation x10 -> x1, other arithmetic: 57.4 us -> 0.07 us  [body(): where = jnp.stack([ex.t, ex.q]).astype(jnp.int32)]
    pallas_call x0 -> x11, Pallas kernels: none -> 47.8 us  [kernel_call(): pl.pallas_call(kernel, out_shape=out, grid=grid, in_specs=specs, out_spec...]
    ppermute x0 -> x37, starting transfers between devices: none -> 47.4 us  [the longest x14 24.4 us: swap(): return lax.ppermute(value, 'dp', [(i, i ^ dp) for i in range(m)])]
    reduce_scatter x1 -> x0, waiting for transfers between devices: 31.3 us -> none  [body(): lax.psum_scatter(contract_rows(columns, ortho), 'tensor', scatter_dimensi...]
  transfers between devices with their start and end apart: 7 -> 37, of which waited for: 7 -> 18; matrix products, arithmetic and copies ran while one was open for 4% -> 4% of each run, Pallas kernels for 0% -> 17%
where the time goes in v1:
time: 182 us; the launch traced here: 181 us
  waiting for transfers between devices  65.2 us (36%)
  Pallas kernels  47.8 us (26%)
  starting transfers between devices  47.4 us (26%)
  local copies, waits for them, and re-layouts  13.6 us (7%)
  other arithmetic  6.24 us (3%)
    pallas_call x11, Pallas kernels, kernel_call(): pl.pallas_call(kernel, out_shape=out, grid=grid, in_specs=specs, out_spec...  47.8 us
    ppermute x17, waiting for transfers between devices, swap(): return lax.ppermute(value, 'tensor', [(i, i ^ tensor) for i in range(n)])  36.2 us
    ppermute x14, waiting for transfers between devices, swap(): return lax.ppermute(value, 'dp', [(i, i ^ dp) for i in range(m)])  26.1 us
    ppermute x14, starting transfers between devices, swap(): return lax.ppermute(value, 'dp', [(i, i ^ dp) for i in range(m)])  24.4 us
    ppermute x17, starting transfers between devices, swap(): return lax.ppermute(value, 'tensor', [(i, i ^ tensor) for i in range(n)])  12.5 us
    unnamed x42, local copies, waits for them, and re-layouts  11 us
    ppermute x6, starting transfers between devices, swap(): return lax.ppermute(value, ('dp', 'tensor'), perm)  10.4 us
  transfers between devices with their start and end apart: 37, of which 18 were waited for; matrix products, arithmetic and copies ran while one was open for 4% of the time, Pallas kernels for 17%

profile of v1, /device:TPU:0, one launch (start us, length us, event | category | flops | bytes accessed | tf_op | source)
XLA Modules:
  0.0 181.1 jit_solution(12084651174391959015)
XLA Ops:
  0.6 3.0 %collective-permute-start.1 = (f32[512,256]{1,0:T(8,128)}, f32[512,256]{1,0:T(8,128)S(1)}, u32[]{:S(2)}, u32[]{:S(2)}) collective-permute-start(f32[512,256]{1,0:T(8,128)} %refs_0_.1), channel_id=1, source_target_pairs={{0,2},{1,3},{2,0},{3,1},{4,6},{5,7},{6,4},{7,5},{8,10},{9,11},{10,... | collective-permute-start | bytes 1572872 | tf_op jit(solution)/shard_map/ppermute | solution.py:294
  3.7 12.1 %collective-permute-done.1.refs_2_ = f32[512,256]{1,0:T(8,128)S(1)} collective-permute-done((f32[512,256]{1,0:T(8,128)}, f32[512,256]{1,0:T(8,128)S(1)}, u32[]{:S(2)}, u32[]{:S(2)}) %collective-permute-start.1) | collective-permute-done | bytes 524320 | tf_op jit(solution)/shard_map/ppermute | solution.py:294
  15.9 1.8 %collective-permute-done.2.refs_3_ = f32[512,256]{1,0:T(8,128)S(1)} collective-permute-done((f32[512,256]{1,0:T(8,128)S(1)}, f32[512,256]{1,0:T(8,128)S(1)}, u32[]{:S(2)}, u32[]{:S(2)}) %collective-permute-start.2) | collective-permute-done | bytes 524320 | tf_op jit(solution)/shard_map/ppermute | solution.py:294
  18.8 2.5 %basis.1 = (bf16[2048,512]{1,0:T(8,128)(2,1)S(1)}, f32[256,256]{1,0:T(8,128)S(1)}) custom-call(s32[2]{0:T(128)S(1)} %pad_add_fusion.where_ref, bf16[256,2048]{1,0:T(8,128)(2,1)} %refs_0_.2, f32[512,256]{1,0:T(8,128)S(1)} %copy-done.6, f32[512,256]{1,0:T(8,128)S(1)} %collective-permute-done.refs_1_, f32[512,256]{1,0:T(8,128)S(1)} %collective-permute-done.1.refs_2_, ...), custom_call_target="tpu_custom_call" | custom-call | flops 536870912 | bytes 5505032 | tf_op jit(solution)/shard_map/basis/pallas_call | solution.py:118
  21.3 1.3 copy-done.9
  22.6 1.7 collective-permute-start.3
  24.3 6.6 %collective-permute-done.3.refs_2_ = f32[256,256]{1,0:T(8,128)S(1)} collective-permute-done((f32[256,256]{1,0:T(8,128)S(1)}, f32[256,256]{1,0:T(8,128)S(1)}, u32[]{:S(2)}, u32[]{:S(2)}) %collective-permute-start.3) | collective-permute-done | bytes 262176 | tf_op jit(solution)/shard_map/ppermute | solution.py:294
  30.9 1.7 collective-permute-start.5
  33.2 4.0 %copy-done.8 = f32[1280,2048]{1,0:T(8,128)S(1)} copy-done((f32[1280,2048]{1,0:T(8,128)S(1)}, f32[1280,2048]{1,0:T(8,128)}, u32[]{:S(2)}) %copy-start.8) | copy-done | bytes 10485784
  37.1 1.6 copy-done.10
  38.7 5.0 %momentum_q.1.base_ref = f32[1280,256]{1,0:T(8,128)S(1)} custom-call(f32[1280,2048]{1,0:T(8,128)S(1)} %copy-done.8, bf16[2048,512]{1,0:T(8,128)(2,1)S(1)} %copy-done.10), custom_call_target="tpu_custom_call" | custom-call | flops 4026531840 | bytes 13893632 | tf_op jit(solution)/shard_map/momentum_q/pallas_call | solution.py:118
  43.9 3.3 %left.1 = f32[1280,256]{1,0:T(8,128)S(1)} custom-call(s32[2]{0:T(128)S(1)} %pad_add_fusion.where_ref, bf16[1024,1280]{1,0:T(8,128)(2,1)S(1)} %copy-done.3, f32[1280,256]{1,0:T(8,128)S(1)} %momentum_q.1.base_ref, f32[256,256]{1,0:T(8,128)S(1)} %get-tuple-element.13.refs_0_, f32[256,256]{1,0:T(8,128)S(1)} %collective-permute-done.7.refs_1_, ...), custom_call_target="tpu_custom_call" | custom-call | flops 1342177280 | bytes 6291464 | tf_op jit(solution)/shard_map/left/pallas_call | solution.py:118
  47.2 8.3 %collective-permute-done.5.refs_2_ = bf16[256,2048]{1,0:T(8,128)(2,1)S(1)} collective-permute-done((bf16[256,2048]{1,0:T(8,128)(2,1)}, bf16[256,2048]{1,0:T(8,128)(2,1)S(1)}, u32[]{:S(2)}, u32[]{:S(2)}) %collective-permute-start.5) | collective-permute-done | bytes 1048608 | tf_op jit(solution)/shard_map/ppermute | solution.py:294
  56.3 1.8 collective-permute-start.9
  58.0 1.5 collective-permute-start.11
  59.8 14.0 %collective-permute-done.9 = f32[320,256]{1,0:T(8,128)} collective-permute-done((f32[320,256]{1,0:T(8,128)}, f32[320,256]{1,0:T(8,128)}, u32[]{:S(2)}, u32[]{:S(2)}) %collective-permute-start.9) | collective-permute-done | bytes 327712 | tf_op jit(solution)/shard_map/ppermute | solution.py:296
  73.8 1.1 collective-permute-done.10
  74.9 1.3 add_add_fusion
  76.2 3.8 %collective-permute-start.12 = (f32[320,256]{1,0:T(8,128)S(1)}, f32[320,256]{1,0:T(8,128)S(1)}, u32[]{:S(2)}, u32[]{:S(2)}) collective-permute-start(f32[320,256]{1,0:T(8,128)S(1)} %add_add_fusion), channel_id=1, source_target_pairs={{0,24},{4,28},{8,16},{12,20},{16,8},{20,12},{24,0},{28,4},{1,25},{... | collective-permute-start | bytes 983048 | tf_op jit(solution)/shard_map/ppermute | solution.py:296
  79.9 7.3 %collective-permute-done.12 = f32[320,256]{1,0:T(8,128)S(1)} collective-permute-done((f32[320,256]{1,0:T(8,128)S(1)}, f32[320,256]{1,0:T(8,128)S(1)}, u32[]{:S(2)}, u32[]{:S(2)}) %collective-permute-start.12) | collective-permute-done | bytes 327712 | tf_op jit(solution)/shard_map/ppermute | solution.py:296
  87.3 7.7 %collective-permute-start.15 = (f32[320,256]{1,0:T(8,128)S(1)}, f32[320,256]{1,0:T(8,128)S(1)}, u32[]{:S(2)}, u32[]{:S(2)}) collective-permute-start(f32[320,256]{1,0:T(8,128)S(1)} %add.120.refs_0_), channel_id=1, source_target_pairs={{0,12},{4,8},{8,4},{12,0},{16,28},{20,24},{24,20},{28,16},{1,13},{... | collective-permute-start | bytes 983048 | tf_op jit(solution)/shard_map/ppermute | solution.py:296
  95.6 1.7 copy-done.4
  97.4 10.0 %buffer.1 = (bf16[1280,2048]{1,0:T(8,128)(2,1)S(1)}, bf16[1280,2048]{1,0:T(8,128)(2,1)S(1)}) custom-call(s32[2]{0:T(128)S(1)} %pad_add_fusion.where_ref, bf16[1024,1280]{1,0:T(8,128)(2,1)S(1)} %copy-done.4, f32[1280,2048]{1,0:T(8,128)} %momentum_ref.3, bf16[256,2048]{1,0:T(8,128)(2,1)} %refs_0_.2, bf16[256,2048]{1,0:T(8,128)(2,1)} %collective-permute-done.4.refs_1_, ...), custom_call_target="tpu_custom_call" | custom-call | flops 5368709120 | bytes 27787272 | tf_op jit(solution)/shard_map/buffer/pallas_call | solution.py:118
  109.0 7.1 %share.1 = f32[2048,256]{1,0:T(8,128)S(1)} custom-call(s32[2]{0:T(128)S(1)} %pad_add_fusion.where_ref, bf16[1280,2048]{1,0:T(8,128)(2,1)S(1)} %get-tuple-element.15.high_ref, bf16[1280,2048]{1,0:T(8,128)(2,1)S(1)} %get-tuple-element.16.low_ref, f32[320,256]{1,0:T(8,128)S(1)} %add.120.refs_0_, f32[320,256]{1,0:T(8,128)S(1)} %collective-permute-done.13.refs_1_, ...), custom_call_target="tpu_custom_call" | custom-call | flops 4026531840 | bytes 13893640 | tf_op jit(solution)/shard_map/share/pallas_call | solution.py:118
  116.2 1.0 dynamic-slice_bitcast_fusion
  117.3 1.9 %gram.1 = f32[256,256]{1,0:T(8,128)S(1)} custom-call(f32[320,256]{1,0:T(8,128)S(1)} %add.120.refs_0_, f32[320,256]{1,0:T(8,128)S(1)} %collective-permute-done.13.refs_1_, f32[320,256]{1,0:T(8,128)S(1)} %collective-permute-done.14.refs_2_, f32[320,256]{1,0:T(8,128)S(1)} %collective-permute-done.15.refs_3_), custom_call_target="tpu_custom_call" | custom-call | flops 1006632960 | bytes 1572864 | tf_op jit(solution)/shard_map/gram/pallas_call | solution.py:118
  120.3 1.4 bitcast_add_fusion
  123.1 3.6 %collective-permute-start.25 = (f32[128,256]{1,0:T(8,128)S(1)}, f32[128,256]{1,0:T(8,128)S(1)}, u32[]{:S(2)}, u32[]{:S(2)}) collective-permute-start(f32[128,256]{1,0:T(8,128)S(1)} %get-tuple-element.27), channel_id=1, source_target_pairs={{0,14},{1,15},{2,12},{3,13},{4,10},{5,11},{6,8},{7,9},{8,6},{9,7},... | collective-permute-start | bytes 393224 | tf_op jit(solution)/shard_map/ppermute | solution.py:299
  126.9 1.5 collective-permute-start.23
  128.4 1.1 collective-permute-start.22
  129.6 1.6 collective-permute-done.19
  131.2 1.8 %collective-permute-start.21 = (f32[128,256]{1,0:T(8,128)S(1)}, f32[128,256]{1,0:T(8,128)}, u32[]{:S(2)}, u32[]{:S(2)}) collective-permute-start(f32[128,256]{1,0:T(8,128)S(1)} %get-tuple-element.31), channel_id=1, source_target_pairs={{0,12},{4,8},{8,4},{12,0},{16,28},{20,24},{24,20},{28,16},{1,13},{... | collective-permute-start | bytes 393224 | tf_op jit(solution)/shard_map/ppermute | solution.py:296
  134.0 1.2 add.121
  135.2 1.6 collective-permute-start.17
  136.8 2.6 %collective-permute-done.22 = f32[128,256]{1,0:T(8,128)} collective-permute-done((f32[128,256]{1,0:T(8,128)S(1)}, f32[128,256]{1,0:T(8,128)}, u32[]{:S(2)}, u32[]{:S(2)}) %collective-permute-start.22) | collective-permute-done | bytes 131104 | tf_op jit(solution)/shard_map/ppermute | solution.py:294
  139.4 1.3 add_add_fusion.1
  140.7 1.9 %collective-permute-start.26 = (f32[128,256]{1,0:T(8,128)S(1)}, f32[128,256]{1,0:T(8,128)S(1)}, u32[]{:S(2)}, u32[]{:S(2)}) collective-permute-start(f32[128,256]{1,0:T(8,128)S(1)} %add_add_fusion.1), channel_id=1, source_target_pairs={{0,24},{4,28},{8,16},{12,20},{16,8},{20,12},{24,0},{28,4},{1,25},{... | collective-permute-start | bytes 393224 | tf_op jit(solution)/shard_map/ppermute | solution.py:296
  142.6 2.2 %collective-permute-done.17 = f32[256,256]{1,0:T(8,128)S(1)} collective-permute-done((f32[256,256]{1,0:T(8,128)S(1)}, f32[256,256]{1,0:T(8,128)S(1)}, u32[]{:S(2)}, u32[]{:S(2)}) %collective-permute-start.17) | collective-permute-done | bytes 262176 | tf_op jit(solution)/shard_map/ppermute | solution.py:294
  144.9 7.8 %chol_inverse.1.inverse_ref = f32[256,256]{1,0:T(8,128)S(1)} custom-call(f32[256,256]{1,0:T(8,128)S(1)} %add.122.gram_ref), custom_call_target="tpu_custom_call" | custom-call | flops 150000000 | bytes 524288 | tf_op jit(solution)/shard_map/chol_inverse/pallas_call | solution.py:118
  153.1 3.5 %collective-permute-start.33 = (bf16[128,256]{1,0:T(8,128)(2,1)S(1)}, bf16[128,256]{1,0:T(8,128)(2,1)S(1)}, u32[]{:S(2)}, u32[]{:S(2)}) collective-permute-start(bf16[128,256]{1,0:T(8,128)(2,1)S(1)} %get-tuple-element.19), channel_id=1, source_target_pairs={{0,14},{1,15},{2,12},{3,13},{4,10},{5,11},{6,8},{7,9},{8,6},{9,7},... | collective-permute-start | bytes 196616 | tf_op jit(solution)/shard_map/ppermute | solution.py:299
  156.6 1.9 %collective-permute-start.29 = (f32[128,256]{1,0:T(8,128)S(1)}, f32[128,256]{1,0:T(8,128)S(1)}, u32[]{:S(2)}, u32[]{:S(2)}) collective-permute-start(f32[128,256]{1,0:T(8,128)S(1)} %get-tuple-element.18.refs_0_), channel_id=1, source_target_pairs={{0,12},{4,8},{8,4},{12,0},{16,28},{20,24},{24,20},{28,16},{1,13},{... | collective-permute-start | bytes 393224 | tf_op jit(solution)/shard_map/ppermute | solution.py:296
  159.0 1.2 collective-permute-start.27
  160.2 1.6 collective-permute-start.31
  163.1 2.2 %collective-permute-done.31.refs_5_ = bf16[128,256]{1,0:T(8,128)(2,1)S(1)} collective-permute-done((bf16[128,256]{1,0:T(8,128)(2,1)S(1)}, bf16[128,256]{1,0:T(8,128)(2,1)S(1)}, u32[]{:S(2)}, u32[]{:S(2)}) %collective-permute-start.31) | collective-permute-done | bytes 65568 | tf_op jit(solution)/shard_map/ppermute | solution.py:299
  165.4 1.4 collective-permute-done.30.refs_4_
  169.9 2.9 %ortho.1.ortho_ref = f32[1280,256]{1,0:T(8,128)} custom-call(s32[2]{0:T(128)S(1)} %pad_add_fusion.where_ref, f32[256,256]{1,0:T(8,128)S(1)} %chol_inverse.1.inverse_ref, f32[320,256]{1,0:T(8,128)S(1)} %add.120.refs_0_, f32[320,256]{1,0:T(8,128)S(1)} %copy-done.16, f32[320,256]{1,0:T(8,128)S(1)} %copy-done.14, f32[320,256]{1,0:T(8,128)S(1)} %copy-done.12), custom_call_target="tpu_custom_call" | custom-call | flops 1006632960 | bytes 2883592 | tf_op jit(solution)/shard_map/ortho/pallas_call | solution.py:118
  173.7 1.3 copy-done.5
  175.0 6.1 %update.1 = f32[1280,2048]{1,0:T(8,128)} custom-call(s32[2]{0:T(128)S(1)} %pad_add_fusion.where_ref, bf16[1280,2048]{1,0:T(8,128)(2,1)S(1)} %bitcast.10, bf16[1280,2048]{1,0:T(8,128)(2,1)S(1)} %copy-done.2, f32[1280,256]{1,0:T(8,128)S(1)} %copy-done.5, bf16[2,512,256]{2,1,0:T(8,128)(2,1)S(1)} %get-tuple-element.20.side_ref, ...), custom_call_target="tpu_custom_call" | custom-call | flops 1342177280 | bytes 23330824 | tf_op jit(solution)/shard_map/update/pallas_call | solution.py:118
  (94 shorter events, 14.9 us)
Async XLA Ops:
  0.6 15.2 %collective-permute-start.1 = (f32[512,256]{1,0:T(8,128)}, f32[512,256]{1,0:T(8,128)S(1)}, u32[]{:S(2)}, u32[]{:S(2)}) collective-permute-start(f32[512,256]{1,0:T(8,128)} %refs_0_.1), channel_id=1, source_target_pairs={{0,2},{1,3},{2,0},{3,1},{4,6},{5,7},{6,4},{7,5},{8,10},{9,11},{10,... | collective-permute-start | bytes 1572872 | tf_op jit(solution)/shard_map/ppermute | solution.py:294
  3.7 12.2 %collective-permute-start = (f32[512,256]{1,0:T(8,128)}, f32[512,256]{1,0:T(8,128)S(1)}, u32[]{:S(2)}, u32[]{:S(2)}) collective-permute-start(f32[512,256]{1,0:T(8,128)} %refs_0_.1), channel_id=1, source_target_pairs={{0,1},{1,0},{2,3},{3,2},{4,5},{5,4},{6,7},{7,6},{8,9},{9,8},{10,11... | collective-permute-start | bytes 1572872 | tf_op jit(solution)/shard_map/ppermute | solution.py:294
  15.8 1.9 %collective-permute-start.2 = (f32[512,256]{1,0:T(8,128)S(1)}, f32[512,256]{1,0:T(8,128)S(1)}, u32[]{:S(2)}, u32[]{:S(2)}) collective-permute-start(f32[512,256]{1,0:T(8,128)S(1)} %collective-permute-done.1.refs_2_), channel_id=1, source_target_pairs={{0,1},{1,0},{2,3},{3,2},{4,5},{5,4},{6,7},{7,6},{8,9},{9,8},{10,11... | collective-permute-start | bytes 1572872 | tf_op jit(solution)/shard_map/ppermute | solution.py:294
  22.6 8.3 %collective-permute-start.3 = (f32[256,256]{1,0:T(8,128)S(1)}, f32[256,256]{1,0:T(8,128)S(1)}, u32[]{:S(2)}, u32[]{:S(2)}) collective-permute-start(f32[256,256]{1,0:T(8,128)S(1)} %get-tuple-element.13.refs_0_), channel_id=1, source_target_pairs={{0,2},{1,3},{2,0},{3,1},{4,6},{5,7},{6,4},{7,5},{8,10},{9,11},{10,... | collective-permute-start | bytes 786440 | tf_op jit(solution)/shard_map/ppermute | solution.py:294
  30.9 24.6 %collective-permute-start.5 = (bf16[256,2048]{1,0:T(8,128)(2,1)}, bf16[256,2048]{1,0:T(8,128)(2,1)S(1)}, u32[]{:S(2)}, u32[]{:S(2)}) collective-permute-start(bf16[256,2048]{1,0:T(8,128)(2,1)} %refs_0_.2), channel_id=1, source_target_pairs={{0,2},{1,3},{2,0},{3,1},{4,6},{5,7},{6,4},{7,5},{8,10},{9,11},{10,... | collective-permute-start | bytes 3145736 | tf_op jit(solution)/shard_map/ppermute | solution.py:294
  32.7 11.2 %collective-permute-start.7 = (f32[256,256]{1,0:T(8,128)S(1)}, f32[256,256]{1,0:T(8,128)S(1)}, u32[]{:S(2)}, u32[]{:S(2)}) collective-permute-start(f32[256,256]{1,0:T(8,128)S(1)} %get-tuple-element.13.refs_0_), channel_id=1, source_target_pairs={{0,1},{1,0},{2,3},{3,2},{4,5},{5,4},{6,7},{7,6},{8,9},{9,8},{10,11... | collective-permute-start | bytes 786440 | tf_op jit(solution)/shard_map/ppermute | solution.py:294
  32.7 11.2 %collective-permute-start.8 = (f32[256,256]{1,0:T(8,128)S(1)}, f32[256,256]{1,0:T(8,128)S(1)}, u32[]{:S(2)}, u32[]{:S(2)}) collective-permute-start(f32[256,256]{1,0:T(8,128)S(1)} %collective-permute-done.3.refs_2_), channel_id=1, source_target_pairs={{0,1},{1,0},{2,3},{3,2},{4,5},{5,4},{6,7},{7,6},{8,9},{9,8},{10,11... | collective-permute-start | bytes 786440 | tf_op jit(solution)/shard_map/ppermute | solution.py:294
  43.7 51.9 %collective-permute-start.4 = (bf16[256,2048]{1,0:T(8,128)(2,1)}, bf16[256,2048]{1,0:T(8,128)(2,1)}, u32[]{:S(2)}, u32[]{:S(2)}) collective-permute-start(bf16[256,2048]{1,0:T(8,128)(2,1)} %refs_0_.2), channel_id=1, source_target_pairs={{0,1},{1,0},{2,3},{3,2},{4,5},{5,4},{6,7},{7,6},{8,9},{9,8},{10,11... | collective-permute-start | bytes 3145736 | tf_op jit(solution)/shard_map/ppermute | solution.py:294
  55.5 40.2 %collective-permute-start.6 = (bf16[256,2048]{1,0:T(8,128)(2,1)S(1)}, bf16[256,2048]{1,0:T(8,128)(2,1)}, u32[]{:S(2)}, u32[]{:S(2)}) collective-permute-start(bf16[256,2048]{1,0:T(8,128)(2,1)S(1)} %collective-permute-done.5.refs_2_), channel_id=1, source_target_pairs={{0,1},{1,0},{2,3},{3,2},{4,5},{5,4},{6,7},{7,6},{8,9},{9,8},{10,11... | collective-permute-start | bytes 3145736 | tf_op jit(solution)/shard_map/ppermute | solution.py:294
  56.3 17.5 %collective-permute-start.9 = (f32[320,256]{1,0:T(8,128)}, f32[320,256]{1,0:T(8,128)}, u32[]{:S(2)}, u32[]{:S(2)}) collective-permute-start(f32[320,256]{1,0:T(8,128)} %get-tuple-element.23), channel_id=1, source_target_pairs={{0,4},{4,0},{8,12},{12,8},{16,20},{20,16},{24,28},{28,24},{1,5},{5... | collective-permute-start | bytes 983048 | tf_op jit(solution)/shard_map/ppermute | solution.py:296
  58.0 15.7 %collective-permute-start.11 = (f32[320,256]{1,0:T(8,128)S(1)}, f32[320,256]{1,0:T(8,128)}, u32[]{:S(2)}, u32[]{:S(2)}) collective-permute-start(f32[320,256]{1,0:T(8,128)S(1)} %get-tuple-element.24), channel_id=1, source_target_pairs={{0,12},{4,8},{8,4},{12,0},{16,28},{20,24},{24,20},{28,16},{1,13},{... | collective-permute-start | bytes 983048 | tf_op jit(solution)/shard_map/ppermute | solution.py:296
  59.6 15.3 %collective-permute-start.10 = (f32[320,256]{1,0:T(8,128)S(1)}, f32[320,256]{1,0:T(8,128)}, u32[]{:S(2)}, u32[]{:S(2)}) collective-permute-start(f32[320,256]{1,0:T(8,128)S(1)} %get-tuple-element.25), channel_id=1, source_target_pairs={{0,8},{4,12},{8,0},{12,4},{16,24},{20,28},{24,16},{28,20},{1,9},{5... | collective-permute-start | bytes 983048 | tf_op jit(solution)/shard_map/ppermute | solution.py:296
  76.2 11.1 %collective-permute-start.12 = (f32[320,256]{1,0:T(8,128)S(1)}, f32[320,256]{1,0:T(8,128)S(1)}, u32[]{:S(2)}, u32[]{:S(2)}) collective-permute-start(f32[320,256]{1,0:T(8,128)S(1)} %add_add_fusion), channel_id=1, source_target_pairs={{0,24},{4,28},{8,16},{12,20},{16,8},{20,12},{24,0},{28,4},{1,25},{... | collective-permute-start | bytes 983048 | tf_op jit(solution)/shard_map/ppermute | solution.py:296
  87.3 20.1 %collective-permute-start.15 = (f32[320,256]{1,0:T(8,128)S(1)}, f32[320,256]{1,0:T(8,128)S(1)}, u32[]{:S(2)}, u32[]{:S(2)}) collective-permute-start(f32[320,256]{1,0:T(8,128)S(1)} %add.120.refs_0_), channel_id=1, source_target_pairs={{0,12},{4,8},{8,4},{12,0},{16,28},{20,24},{24,20},{28,16},{1,13},{... | collective-permute-start | bytes 983048 | tf_op jit(solution)/shard_map/ppermute | solution.py:296
  95.0 13.4 %collective-permute-start.14 = (f32[320,256]{1,0:T(8,128)S(1)}, f32[320,256]{1,0:T(8,128)S(1)}, u32[]{:S(2)}, u32[]{:S(2)}) collective-permute-start(f32[320,256]{1,0:T(8,128)S(1)} %add.120.refs_0_), channel_id=1, source_target_pairs={{0,8},{4,12},{8,0},{12,4},{16,24},{20,28},{24,16},{28,20},{1,9},{5... | collective-permute-start | bytes 983048 | tf_op jit(solution)/shard_map/ppermute | solution.py:296
  95.0 14.1 %collective-permute-start.13 = (f32[320,256]{1,0:T(8,128)S(1)}, f32[320,256]{1,0:T(8,128)S(1)}, u32[]{:S(2)}, u32[]{:S(2)}) collective-permute-start(f32[320,256]{1,0:T(8,128)S(1)} %add.120.refs_0_), channel_id=1, source_target_pairs={{0,4},{4,0},{8,12},{12,8},{16,20},{20,16},{24,28},{28,24},{1,5},{5... | collective-permute-start | bytes 983048 | tf_op jit(solution)/shard_map/ppermute | solution.py:296
  107.4 8.8 %copy-start = (bf16[1280,2048]{1,0:T(8,128)(2,1)}, bf16[1280,2048]{1,0:T(8,128)(2,1)S(1)}, u32[]{:S(2)}) copy-start(bf16[1280,2048]{1,0:T(8,128)(2,1)S(1)} %get-tuple-element.15.high_ref) | copy-start | bytes 15728644
  107.4 8.8 %copy-start.1 = (bf16[1280,2048]{1,0:T(8,128)(2,1)}, bf16[1280,2048]{1,0:T(8,128)(2,1)S(1)}, u32[]{:S(2)}) copy-start(bf16[1280,2048]{1,0:T(8,128)(2,1)S(1)} %get-tuple-element.16.low_ref) | copy-start | bytes 15728644
  107.4 9.8 %copy-start.11 = (f32[320,256]{1,0:T(8,128)}, f32[320,256]{1,0:T(8,128)S(1)}, u32[]{:S(2)}) copy-start(f32[320,256]{1,0:T(8,128)S(1)} %collective-permute-done.15.refs_3_) | copy-start | bytes 983044
  108.3 8.9 %copy-start.13 = (f32[320,256]{1,0:T(8,128)}, f32[320,256]{1,0:T(8,128)S(1)}, u32[]{:S(2)}) copy-start(f32[320,256]{1,0:T(8,128)S(1)} %collective-permute-done.14.refs_2_) | copy-start | bytes 983044
  109.0 8.2 %copy-start.15 = (f32[320,256]{1,0:T(8,128)}, f32[320,256]{1,0:T(8,128)S(1)}, u32[]{:S(2)}) copy-start(f32[320,256]{1,0:T(8,128)S(1)} %collective-permute-done.13.refs_1_) | copy-start | bytes 983044
  117.3 3.0 %collective-permute-start.18 = (f32[2,512,256]{2,1,0:T(8,128)}, f32[2,512,256]{2,1,0:T(8,128)}, u32[]{:S(2)}, u32[]{:S(2)}) collective-permute-start(f32[2,512,256]{2,1,0:T(8,128)} %dynamic-slice_bitcast_fusion), channel_id=1, source_target_pairs={{0,1},{1,0},{2,3},{3,2},{4,5},{5,4},{6,7},{7,6},{8,9},{9,8},{10,11... | collective-permute-start | bytes 3145736 | tf_op jit(solution)/shard_map/ppermute | solution.py:294
  119.2 9.2 %collective-permute-start.16 = (f32[256,256]{1,0:T(8,128)S(1)}, f32[256,256]{1,0:T(8,128)}, u32[]{:S(2)}, u32[]{:S(2)}) collective-permute-start(f32[256,256]{1,0:T(8,128)S(1)} %gram.1), channel_id=1, source_target_pairs={{0,1},{1,0},{2,3},{3,2},{4,5},{5,4},{6,7},{7,6},{8,9},{9,8},{10,11... | collective-permute-start | bytes 786440 | tf_op jit(solution)/shard_map/ppermute | solution.py:294
  120.3 53.4 %slice-start = ((s8[5242880]{0:T(1024)(128)(4,1)}), s8[1048576]{0:T(1024)(128)(4,1)S(1)}, s32[]{:S(2)}) async-start(s8[5242880]{0:T(1024)(128)(4,1)} %bitcast.9), calls=%async_computation | async-start | bytes 2097152
  121.7 48.2 %copy-start.12 = (f32[320,256]{1,0:T(8,128)S(1)}, f32[320,256]{1,0:T(8,128)}, u32[]{:S(2)}) copy-start(f32[320,256]{1,0:T(8,128)} %copy-done.11) | copy-start | bytes 983044
  121.7 48.2 %copy-start.14 = (f32[320,256]{1,0:T(8,128)S(1)}, f32[320,256]{1,0:T(8,128)}, u32[]{:S(2)}) copy-start(f32[320,256]{1,0:T(8,128)} %copy-done.13) | copy-start | bytes 983044
  121.8 48.2 %copy-start.16 = (f32[320,256]{1,0:T(8,128)S(1)}, f32[320,256]{1,0:T(8,128)}, u32[]{:S(2)}) copy-start(f32[320,256]{1,0:T(8,128)} %copy-done.15) | copy-start | bytes 983044
  122.5 8.7 %collective-permute-start.19 = (f32[128,256]{1,0:T(8,128)S(1)}, f32[128,256]{1,0:T(8,128)S(1)}, u32[]{:S(2)}, u32[]{:S(2)}) collective-permute-start(f32[128,256]{1,0:T(8,128)S(1)} %get-tuple-element.26), channel_id=1, source_target_pairs={{0,4},{4,0},{8,12},{12,8},{16,20},{20,16},{24,28},{28,24},{1,5},{5... | collective-permute-start | bytes 393224 | tf_op jit(solution)/shard_map/ppermute | solution.py:296
  123.1 9.9 %collective-permute-start.25 = (f32[128,256]{1,0:T(8,128)S(1)}, f32[128,256]{1,0:T(8,128)S(1)}, u32[]{:S(2)}, u32[]{:S(2)}) collective-permute-start(f32[128,256]{1,0:T(8,128)S(1)} %get-tuple-element.27), channel_id=1, source_target_pairs={{0,14},{1,15},{2,12},{3,13},{4,10},{5,11},{6,8},{7,9},{8,6},{9,7},... | collective-permute-start | bytes 393224 | tf_op jit(solution)/shard_map/ppermute | solution.py:299
  126.7 8.5 %collective-permute-start.24 = (f32[128,256]{1,0:T(8,128)S(1)}, f32[128,256]{1,0:T(8,128)}, u32[]{:S(2)}, u32[]{:S(2)}) collective-permute-start(f32[128,256]{1,0:T(8,128)S(1)} %get-tuple-element.28), channel_id=1, source_target_pairs={{0,10},{1,11},{2,8},{3,9},{4,14},{5,15},{6,12},{7,13},{8,2},{9,3},... | collective-permute-start | bytes 393224 | tf_op jit(solution)/shard_map/ppermute | solution.py:299
  126.9 9.9 %collective-permute-start.23 = (f32[128,256]{1,0:T(8,128)}, f32[128,256]{1,0:T(8,128)}, u32[]{:S(2)}, u32[]{:S(2)}) collective-permute-start(f32[128,256]{1,0:T(8,128)} %get-tuple-element.29), channel_id=1, source_target_pairs={{0,6},{1,7},{2,4},{3,5},{4,2},{5,3},{6,0},{7,1},{8,14},{9,15},{10,... | collective-permute-start | bytes 393224 | tf_op jit(solution)/shard_map/ppermute | solution.py:299
  128.4 11.0 %collective-permute-start.22 = (f32[128,256]{1,0:T(8,128)S(1)}, f32[128,256]{1,0:T(8,128)}, u32[]{:S(2)}, u32[]{:S(2)}) collective-permute-start(f32[128,256]{1,0:T(8,128)S(1)} %get-tuple-element.30), channel_id=1, source_target_pairs={{0,2},{1,3},{2,0},{3,1},{4,6},{5,7},{6,4},{7,5},{8,10},{9,11},{10,... | collective-permute-start | bytes 393224 | tf_op jit(solution)/shard_map/ppermute | solution.py:294
  131.2 8.2 %collective-permute-start.21 = (f32[128,256]{1,0:T(8,128)S(1)}, f32[128,256]{1,0:T(8,128)}, u32[]{:S(2)}, u32[]{:S(2)}) collective-permute-start(f32[128,256]{1,0:T(8,128)S(1)} %get-tuple-element.31), channel_id=1, source_target_pairs={{0,12},{4,8},{8,4},{12,0},{16,28},{20,24},{24,20},{28,16},{1,13},{... | collective-permute-start | bytes 393224 | tf_op jit(solution)/shard_map/ppermute | solution.py:296
  133.1 6.4 %collective-permute-start.20 = (f32[128,256]{1,0:T(8,128)S(1)}, f32[128,256]{1,0:T(8,128)}, u32[]{:S(2)}, u32[]{:S(2)}) collective-permute-start(f32[128,256]{1,0:T(8,128)S(1)} %get-tuple-element.32), channel_id=1, source_target_pairs={{0,8},{4,12},{8,0},{12,4},{16,24},{20,28},{24,16},{28,20},{1,9},{5... | collective-permute-start | bytes 393224 | tf_op jit(solution)/shard_map/ppermute | solution.py:296
  134.0 39.7 %copy-start.2 = (bf16[1280,2048]{1,0:T(8,128)(2,1)S(1)}, bf16[1280,2048]{1,0:T(8,128)(2,1)}, u32[]{:S(2)}) copy-start(bf16[1280,2048]{1,0:T(8,128)(2,1)} %copy-done.1) | copy-start | bytes 15728644
  135.2 9.6 %collective-permute-start.17 = (f32[256,256]{1,0:T(8,128)S(1)}, f32[256,256]{1,0:T(8,128)S(1)}, u32[]{:S(2)}, u32[]{:S(2)}) collective-permute-start(f32[256,256]{1,0:T(8,128)S(1)} %add.121), channel_id=1, source_target_pairs={{0,2},{1,3},{2,0},{3,1},{4,6},{5,7},{6,4},{7,5},{8,10},{9,11},{10,... | collective-permute-start | bytes 786440 | tf_op jit(solution)/shard_map/ppermute | solution.py:294
  140.7 32.9 %slice-start.1 = ((s8[5242880]{0:T(1024)(128)(4,1)}), s8[4194304]{0:T(1024)(128)(4,1)S(1)}, s32[]{:S(2)}) async-start(s8[5242880]{0:T(1024)(128)(4,1)} %bitcast.9), calls=%async_computation.1 | async-start | bytes 8388608
  140.7 11.9 %collective-permute-start.26 = (f32[128,256]{1,0:T(8,128)S(1)}, f32[128,256]{1,0:T(8,128)S(1)}, u32[]{:S(2)}, u32[]{:S(2)}) collective-permute-start(f32[128,256]{1,0:T(8,128)S(1)} %add_add_fusion.1), channel_id=1, source_target_pairs={{0,24},{4,28},{8,16},{12,20},{16,8},{20,12},{24,0},{28,4},{1,25},{... | collective-permute-start | bytes 393224 | tf_op jit(solution)/shard_map/ppermute | solution.py:296
  153.1 7.1 %collective-permute-start.33 = (bf16[128,256]{1,0:T(8,128)(2,1)S(1)}, bf16[128,256]{1,0:T(8,128)(2,1)S(1)}, u32[]{:S(2)}, u32[]{:S(2)}) collective-permute-start(bf16[128,256]{1,0:T(8,128)(2,1)S(1)} %get-tuple-element.19), channel_id=1, source_target_pairs={{0,14},{1,15},{2,12},{3,13},{4,10},{5,11},{6,8},{7,9},{8,6},{9,7},... | collective-permute-start | bytes 196616 | tf_op jit(solution)/shard_map/ppermute | solution.py:299
  156.6 5.9 %collective-permute-start.32 = (bf16[128,256]{1,0:T(8,128)(2,1)S(1)}, bf16[128,256]{1,0:T(8,128)(2,1)S(1)}, u32[]{:S(2)}, u32[]{:S(2)}) collective-permute-start(bf16[128,256]{1,0:T(8,128)(2,1)S(1)} %get-tuple-element.19), channel_id=1, source_target_pairs={{0,10},{1,11},{2,8},{3,9},{4,14},{5,15},{6,12},{7,13},{8,2},{9,3},... | collective-permute-start | bytes 196616 | tf_op jit(solution)/shard_map/ppermute | solution.py:299
  156.6 10.1 %collective-permute-start.29 = (f32[128,256]{1,0:T(8,128)S(1)}, f32[128,256]{1,0:T(8,128)S(1)}, u32[]{:S(2)}, u32[]{:S(2)}) collective-permute-start(f32[128,256]{1,0:T(8,128)S(1)} %get-tuple-element.18.refs_0_), channel_id=1, source_target_pairs={{0,12},{4,8},{8,4},{12,0},{16,28},{20,24},{24,20},{28,16},{1,13},{... | collective-permute-start | bytes 393224 | tf_op jit(solution)/shard_map/ppermute | solution.py:296
  158.5 8.2 %collective-permute-start.28 = (f32[128,256]{1,0:T(8,128)S(1)}, f32[128,256]{1,0:T(8,128)S(1)}, u32[]{:S(2)}, u32[]{:S(2)}) collective-permute-start(f32[128,256]{1,0:T(8,128)S(1)} %get-tuple-element.18.refs_0_), channel_id=1, source_target_pairs={{0,8},{4,12},{8,0},{12,4},{16,24},{20,28},{24,16},{28,20},{1,9},{5... | collective-permute-start | bytes 393224 | tf_op jit(solution)/shard_map/ppermute | solution.py:296
  159.0 8.1 %collective-permute-start.27 = (f32[128,256]{1,0:T(8,128)S(1)}, f32[128,256]{1,0:T(8,128)S(1)}, u32[]{:S(2)}, u32[]{:S(2)}) collective-permute-start(f32[128,256]{1,0:T(8,128)S(1)} %get-tuple-element.18.refs_0_), channel_id=1, source_target_pairs={{0,4},{4,0},{8,12},{12,8},{16,20},{20,16},{24,28},{28,24},{1,5},{5... | collective-permute-start | bytes 393224 | tf_op jit(solution)/shard_map/ppermute | solution.py:296
  160.2 5.2 %collective-permute-start.31 = (bf16[128,256]{1,0:T(8,128)(2,1)S(1)}, bf16[128,256]{1,0:T(8,128)(2,1)S(1)}, u32[]{:S(2)}, u32[]{:S(2)}) collective-permute-start(bf16[128,256]{1,0:T(8,128)(2,1)S(1)} %get-tuple-element.19), channel_id=1, source_target_pairs={{0,6},{1,7},{2,4},{3,5},{4,2},{5,3},{6,0},{7,1},{8,14},{9,15},{10,... | collective-permute-start | bytes 196616 | tf_op jit(solution)/shard_map/ppermute | solution.py:299
  162.5 4.3 %collective-permute-start.30 = (bf16[128,256]{1,0:T(8,128)(2,1)S(1)}, bf16[128,256]{1,0:T(8,128)(2,1)S(1)}, u32[]{:S(2)}, u32[]{:S(2)}) collective-permute-start(bf16[128,256]{1,0:T(8,128)(2,1)S(1)} %get-tuple-element.19), channel_id=1, source_target_pairs={{0,2},{1,3},{2,0},{3,1},{4,6},{5,7},{6,4},{7,5},{8,10},{9,11},{10,... | collective-permute-start | bytes 196616 | tf_op jit(solution)/shard_map/ppermute | solution.py:294
  167.7 1.2 collective-permute-start.35
  167.8 5.8 %collective-permute-start.34 = (bf16[2,512,256]{2,1,0:T(8,128)(2,1)S(1)}, bf16[2,512,256]{2,1,0:T(8,128)(2,1)S(1)}, u32[]{:S(2)}, u32[]{:S(2)}) collective-permute-start(bf16[2,512,256]{2,1,0:T(8,128)(2,1)S(1)} %get-tuple-element.20.side_ref), channel_id=1, source_target_pairs={{0,1},{1,0},{2,3},{3,2},{4,5},{5,4},{6,7},{7,6},{8,9},{9,8},{10,11... | collective-permute-start | bytes 1572872 | tf_op jit(solution)/shard_map/ppermute | solution.py:294
  169.0 3.8 %collective-permute-start.36 = (f32[8,256]{1,0:T(8,128)S(1)}, f32[8,256]{1,0:T(8,128)S(1)}, u32[]{:S(2)}, u32[]{:S(2)}) collective-permute-start(f32[8,256]{1,0:T(8,128)S(1)} %add.144), channel_id=1, source_target_pairs={{0,2},{1,3},{2,0},{3,1},{4,6},{5,7},{6,4},{7,5},{8,10},{9,11},{10,... | collective-permute-start | bytes 24584 | tf_op jit(solution)/shard_map/ppermute | solution.py:294
  (10 other events, 27.1 us)

commit v2 on v1

v2 whole, which is shorter than its diff:
```python
import functools

import jax
import jax.numpy as jnp
from jax import lax
from jax.experimental import pallas as pl
from jax.experimental.pallas import tpu as pltpu
from jax.sharding import PartitionSpec as P


F32 = jnp.float32
BF16 = jnp.bfloat16
HIGHEST = lax.Precision.HIGHEST
BLOCK = 32
GROUP = 8
VMEM = 20
LARGE = 54
LEFT = 60
LANES = 128


def split3(value):
    high = value.astype(BF16)
    rest = value - high.astype(F32)
    mid = rest.astype(BF16)
    low = (rest - mid.astype(F32)).astype(BF16)
    return high, mid, low


def chol_inverse_kernel(first, last, gram_ref, out_ref):
    n = gram_ref.shape[0]
    out_ref[...] = gram_ref[...]
    lane = lax.broadcasted_iota(jnp.int32, (GROUP, n), 1)
    sub = lax.broadcasted_iota(jnp.int32, (GROUP, LANES), 0)

    def wide(v):
        return jnp.concatenate([v] * (n // LANES), axis=1)

    groups = BLOCK // GROUP
    for block in range(first, last):
        base = block * BLOCK
        tile = [out_ref[pl.ds(base + g * GROUP, GROUP), :] for g in range(groups)]
        for g in range(groups):
            start = base + g * GROUP
            cols = [
                [
                    jnp.broadcast_to(tile[h][:, start + s : start + s + 1], (GROUP, LANES))
                    for h in range(g, groups)
                ]
                for s in range(GROUP)
            ]
            for s in range(GROUP):
                col = start + s
                scale = lax.rsqrt(jnp.broadcast_to(cols[s][0][s : s + 1, :], (GROUP, LANES)))
                factor = [c * scale for c in cols[s]]
                factor[0] = jnp.where(sub > s, factor[0], 0.0)
                pivot = jnp.broadcast_to(tile[g][s : s + 1, :], (GROUP, n)) * wide(scale)
                pivot = jnp.where(lane == col, wide(scale), pivot)
                for later in range(s + 1, GROUP):
                    entry = jnp.broadcast_to(cols[later][0][s : s + 1, :], (GROUP, LANES)) * scale
                    cols[later] = [c - f * entry for c, f in zip(cols[later], factor)]
                for h in range(g, groups):
                    if h == g:
                        kept = jnp.where((lane == col) & (wide(sub) > s), 0.0, tile[h])
                        new = kept - wide(factor[0]) * pivot
                        tile[h] = jnp.where(wide(sub) == s, pivot, new)
                    else:
                        kept = jnp.where(lane == col, 0.0, tile[h])
                        tile[h] = kept - wide(factor[h - g]) * pivot
        for g in range(groups):
            out_ref[pl.ds(base + g * GROUP, GROUP), :] = tile[g]
        rest = base + BLOCK
        if rest < n:
            rows = jnp.concatenate(tile, axis=0)
            lane_b = lax.broadcasted_iota(jnp.int32, (BLOCK, n), 1)
            row_b = lax.broadcasted_iota(jnp.int32, (BLOCK, n), 0) + base
            lower = jnp.where((lane_b > row_b) & (lane_b < rest), 0.0, rows)
            ah, am, al = split3(rows)
            bh, bm, bl = split3(lower)
            first = jnp.concatenate([ah, ah, ah, am, am, al], axis=0)
            second = jnp.concatenate([bh, bm, bl, bh, bm, bh], axis=0)
            change = lax.dot_general(
                first, second, (((0,), (0,)), ((), ())), preferred_element_type=F32
            )
            lane_r = lax.broadcasted_iota(jnp.int32, (n - rest, n), 1)
            old = out_ref[pl.ds(rest, n - rest), :]
            old = jnp.where((lane_r >= base) & (lane_r < rest), 0.0, old)
            out_ref[pl.ds(rest, n - rest), :] = old - change[rest:, :]
    if last * BLOCK == n:
        lane_n = lax.broadcasted_iota(jnp.int32, (n, n), 1)
        row_n = lax.broadcasted_iota(jnp.int32, (n, n), 0)
        out_ref[...] = jnp.where(row_n >= lane_n, out_ref[...], 0.0)


def dot(a, b, contract, precision=None):
    return lax.dot_general(
        a, b, (contract, ((), ())), precision=precision, preferred_element_type=F32
    )


NN = ((1,), (0,))
NT = ((1,), (1,))
TN = ((0,), (0,))


def struct(shape, dtype=F32):
    return jax.ShapeDtypeStruct(shape, dtype)


def kernel_call(kernel, out, flops, *args, grid=(), in_specs=None, out_specs=None, scratch=(), vmem=VMEM, prefetch=0):
    whole = pl.BlockSpec(memory_space=pltpu.VMEM)
    many = isinstance(out, (tuple, list))
    if in_specs is None:
        in_specs = [None] * len(args)
    specs = []
    for i, (spec, arg) in enumerate(zip(in_specs, args)):
        if i < prefetch:
            continue
        if spec is None:
            spec = pl.BlockSpec(memory_space=pltpu.SMEM) if arg.dtype == jnp.int32 else whole
        specs.append(spec)
    if out_specs is None:
        out_specs = type(out)([whole] * len(out)) if many else whole
    moved = sum(a.size * a.dtype.itemsize for a in list(args) + list(out if many else [out]))
    return pl.pallas_call(
        kernel,
        out_shape=out,
        grid_spec=pltpu.PrefetchScalarGridSpec(
            num_scalar_prefetch=prefetch,
            grid=grid,
            in_specs=specs,
            out_specs=out_specs,
            scratch_shapes=list(scratch),
        ),
        cost_estimate=pl.CostEstimate(flops=flops, bytes_accessed=moved, transcendentals=0),
        compiler_params=pltpu.CompilerParams(vmem_limit_bytes=vmem * 1024 * 1024),
    )(*args)


def split2(value):
    high = value.astype(BF16)
    return high, (value - high.astype(F32)).astype(BF16)


def rows_at(index, rows):
    return pl.ds(pl.multiple_of(index * rows, rows), rows)


def chol_inverse(state, first, last):
    kernel = functools.partial(chol_inverse_kernel, first, last)
    return kernel_call(kernel, struct(state.shape), 2_000_000_000, state)


def tied(values, *others):
    return lax.optimization_barrier((values, others))[0]


def fill_pair(pair_ref, pieces, place, scale=1.0):
    rows, rank = pieces[0].shape
    for m, piece in enumerate(pieces):
        high, low = split2(piece[...] * scale if scale != 1.0 else piece[...])
        at = rows_at(place(m), rows)
        pair_ref[at, :rank] = high
        pair_ref[at, rank:] = low


def basis_kernel(first, count, where_ref, grads_ref, *refs):
    pieces, (pair_ref, out_ref) = refs[: 2 * count], refs[-2:]
    rows, rank = pieces[0].shape
    fill_pair(pair_ref, pieces, lambda m: (m // 2) * 2 + ((where_ref[0] ^ m) & 1))
    total = refs[2 * count][...] if first else None
    for m in range(count):
        block = (where_ref[0] >> 1) ^ (first + m)
        columns = pl.ds(pl.multiple_of(block * (2 * rows), 2 * rows), 2 * rows)
        both = dot(grads_ref[:, columns], pair_ref[m * 2 * rows : (m + 1) * 2 * rows, :], NN)
        term = both[:, :rank] + both[:, rank:]
        total = term if total is None else total + term
    out_ref[...] = total


def momentum_kernel(first, where_ref, momentum_ref, pair_ref, *refs):
    out_ref = refs[-1]
    rank = out_ref.shape[1]
    high, low = split2(momentum_ref[...])
    both = dot(high, pair_ref[...], NN)
    term = 0.95 * (both[:, :rank] + both[:, rank:] + dot(low, pair_ref[:, :rank], NN))

    if first == 0:
        out_ref[...] = term
        return

    @pl.when(pl.program_id(1) == 0)
    def _():
        out_ref[...] = refs[0][...] + term

    @pl.when(pl.program_id(1) != 0)
    def _():
        out_ref[...] = out_ref[...] + term


SPLIT = 2


def chunk_of(q, index):
    return (q ^ (index // SPLIT)) * SPLIT + index % SPLIT


def left_kernel(count, scale, where_ref, acts_ref, base_ref, *refs):
    pieces, outs, (pair_ref, full_ref) = refs[:count], refs[count:-2], refs[-2:]
    rank = pieces[0].shape[1]
    fill_pair(pair_ref, pieces, lambda m: where_ref[0] ^ m)
    both = dot(acts_ref[...], pair_ref[...], TN)
    full_ref[...] = scale * (base_ref[...] + (both[:, :rank] + both[:, rank:]))
    for m, out_ref in enumerate(outs):
        out_ref[...] = full_ref[rows_at(chunk_of(where_ref[1], m), out_ref.shape[0]), :]


def buffer_kernel(count, where_ref, acts_ref, momentum_ref, *refs):
    pieces, (high_ref, low_ref) = refs[:count], refs[count:]
    rows, columns = pieces[0].shape
    step = 512
    lhs = [acts_ref[rows_at(where_ref[0] ^ m, rows), :] for m in range(count)]
    for start in range(0, columns, step):
        at = slice(start, start + step)
        total = 0.95 * momentum_ref[:, at]
        for m in range(count):
            total = total + dot(lhs[m], pieces[m][:, at], TN)
        high_ref[:, at], low_ref[:, at] = split2(total)


def gram_kernel(*refs):
    pieces, out_ref = refs[:-1], refs[-1]
    total = None
    for piece in pieces:
        value = piece[...]
        term = dot(value, value, TN, HIGHEST)
        total = term if total is None else total + term
    out_ref[...] = total


def share_kernel(quad, scale, where_ref, high_ref, low_ref, *refs):
    pieces, (out_ref, pair_ref) = refs[:-2], refs[-2:]
    rank = pieces[0].shape[1]

    @pl.when((pl.program_id(0) == 0) & (pl.program_id(1) == 0))
    def _():
        fill_pair(pair_ref, pieces, lambda m: chunk_of(where_ref[1], m), scale)

    both = dot(pair_ref[...], high_ref[...], TN)
    total = both[:rank] + both[rank:] + dot(pair_ref[:, :rank], low_ref[...], TN)
    total = total.T
    chunk = total.shape[0] // quad
    for c in range(quad):
        out_ref[0, 0, rows_at(where_ref[1] ^ c, chunk), :] = total[c * chunk : (c + 1) * chunk]


EXTRA = 16


def with_squares(ref, start, squares):
    ref[start : start + EXTRA, :] = jnp.zeros((EXTRA, ref.shape[1]), BF16)
    for i, part in enumerate(split3(squares)):
        ref[start + i : start + i + 1, :] = part


def squares_of(ref, start):
    part = ref[start : start + EXTRA, :].astype(F32)
    return part[0:1] + part[1:2] + part[2:3]


def right_kernel(part_ref, inverse_ref, right_ref, narrow_ref):
    right = dot(part_ref[...], inverse_ref[...], NT, HIGHEST)
    rows = right.shape[0]
    right_ref[...] = right
    narrow_ref[:rows, :] = right.astype(BF16)
    with_squares(narrow_ref, rows, jnp.sum(right * right, axis=0, keepdims=True))


def ortho_kernel(where_ref, inverse_ref, *refs):
    pieces, (out_ref, narrow_ref) = refs[:-2], refs[-2:]
    rows = pieces[0].shape[0]
    for m, piece in enumerate(pieces):
        at = rows_at(chunk_of(where_ref[1], m), rows)
        value = dot(piece[...], inverse_ref[...], NT, HIGHEST)
        out_ref[at, :] = value
        narrow_ref[at, :] = value.astype(BF16)


def collect_kernel(xs, quad, where_ref, *refs):
    exact, narrow = refs[:quad], refs[quad : xs * quad]
    own_ref, side_ref = refs[-2:]
    rows = exact[0].shape[0]
    squares = None
    for m in range(quad):
        value = exact[m][...]
        own_ref[rows_at(where_ref[1] ^ m, rows), :] = value
        terms = [jnp.sum(value * value, axis=0, keepdims=True)]
        for x in range(xs):
            at = rows_at(x * quad + (where_ref[1] ^ m), rows)
            if x == 0:
                side_ref[at, :] = value.astype(BF16)
            else:
                piece = narrow[(x - 1) * quad + m]
                side_ref[at, :] = piece[:rows, :]
                terms.append(squares_of(piece, rows))
        for term in terms:
            squares = term if squares is None else squares + term
    with_squares(side_ref, xs * quad * rows, squares)


def update_kernel(xs, where_ref, high_ref, low_ref, ortho_ref, side_ref, other_ref, own_ref, out_ref, new_ref, full_ref):
    rows = own_ref.shape[0]

    @pl.when(pl.program_id(0) == 0)
    def _():
        for x in range(xs):
            at = slice(x * rows, (x + 1) * rows)
            full_ref[rows_at(where_ref[0] ^ (2 * x), rows), :] = side_ref[at, :]
            full_ref[rows_at(where_ref[0] ^ (2 * x + 1), rows), :] = other_ref[at, :]
        squares = squares_of(side_ref, xs * rows) + squares_of(other_ref, xs * rows)
        new_ref[...] = own_ref[...] * lax.rsqrt(squares + 1e-06)

    step = 512
    for start in range(0, out_ref.shape[1], step):
        at = slice(start, start + step)
        change = dot(ortho_ref[...], full_ref[at, :], NT)
        value = high_ref[:, at].astype(F32) + low_ref[:, at].astype(F32)
        out_ref[:, at] = value - 0.05 * change


class Exchange:
    def __init__(self, replicas, parts):
        self.replicas, self.parts = replicas, parts
        self.quad = min(4, replicas)
        self.xs = parts // 2
        self.higher = []
        bit = self.quad
        while bit < replicas:
            self.higher.append(bit | (bit >> 1))
            bit *= 2
        d, self.t = lax.axis_index("dp"), lax.axis_index("tensor")
        bits, k, above = [], replicas.bit_length() - 2, 0
        while k >= 0:
            own = (d >> k) & 1
            if k >= 1 and (1 << (k + 1)) < replicas:
                own = own ^ above
            bits.append((k, own))
            above = own
            k -= 1
        self.q = sum(own << k for k, own in bits if (1 << k) < self.quad)
        self.x, self.core = self.t // 2, self.t % 2

    def swap(self, value, dp=0, tensor=0):
        n, m = self.parts, self.replicas
        if dp == 0:
            return lax.ppermute(value, "tensor", [(i, i ^ tensor) for i in range(n)])
        if tensor == 0:
            return lax.ppermute(value, "dp", [(i, i ^ dp) for i in range(m)])
        pairs = [((i // n), i % n) for i in range(m * n)]
        perm = [(d * n + t, (d ^ dp) * n + (t ^ tensor)) for d, t in pairs]
        return lax.ppermute(value, ("dp", "tensor"), perm)

    def gather_tensor(self, value):
        pieces = {0: value, 1: self.swap(value, tensor=1)}
        for m in range(2, self.parts, 2):
            pieces[m] = self.swap(value, tensor=m)
            pieces[m + 1] = self.swap(pieces[m], tensor=1)
        return [pieces[m] for m in range(self.parts)]


def step(acts, out_grad, momentum, q_basis):
    replicas, parts = lax.axis_size("dp"), lax.axis_size("tensor")
    ex = Exchange(replicas, parts)
    rows, columns = momentum.shape
    tokens = acts.shape[0]
    rank = q_basis.shape[1]
    tile = 256 if rows % 256 == 0 else 128
    large = rows // 2
    steps = rows // tile
    where = jnp.stack([ex.t, ex.q]).astype(jnp.int32)
    wide_spec = pl.BlockSpec((tile, columns), lambda i: (i, 0))
    rank_spec = pl.BlockSpec((tile, rank), lambda i: (i, 0))
    acts_spec = pl.BlockSpec((tokens, tile), lambda i: (0, i))

    xs, local = ex.xs, columns // parts
    half = 2 * local
    where_x = jnp.stack([ex.x, ex.q]).astype(jnp.int32)
    near = [q_basis, ex.swap(q_basis, tensor=1)]
    across = [ex.swap(q_basis, tensor=m) for m in range(2, parts, 2)]

    def basis(first, pieces, *more):
        count = len(pieces) // 2
        return kernel_call(
            functools.partial(basis_kernel, first, count),
            (struct((count * half, 2 * rank), BF16), struct((out_grad.shape[0], rank))),
            4 * out_grad.shape[0] * count * half * rank, where, out_grad, *pieces, *more,
        )

    near_pair, near_grad = basis(0, near)
    base = kernel_call(
        functools.partial(momentum_kernel, 0), struct((rows, rank)),
        6 * rows * half * rank, where_x, momentum, near_pair, grid=(2,), prefetch=1,
        in_specs=[None, pl.BlockSpec((large, half), lambda i, w: (i, w[0])), None],
        out_specs=pl.BlockSpec((large, rank), lambda i, w: (i, 0)), vmem=LARGE,
    )
    far = []
    for piece in tied(across, base):
        far += [piece, ex.swap(piece, tensor=1)]
    pair, grad_q = basis(1, far, near_grad)
    base = kernel_call(
        functools.partial(momentum_kernel, 1), struct((rows, rank)),
        6 * rows * (columns - half) * rank, where_x, momentum, pair, base,
        grid=(2, xs - 1), prefetch=1,
        in_specs=[
            None,
            pl.BlockSpec((large, half), lambda i, j, w: (i, w[0] ^ (j + 1))),
            pl.BlockSpec((half, 2 * rank), lambda i, j, w: (j, 0)),
            pl.BlockSpec((large, rank), lambda i, j, w: (i, 0)),
        ],
        out_specs=pl.BlockSpec((large, rank), lambda i, j, w: (i, 0)), vmem=LARGE,
    )
    near_q = ex.swap(grad_q, tensor=1)
    far_q = tied([ex.swap(grad_q, tensor=m) for m in range(2, parts, 2)], base)
    grads_q = [grad_q, near_q]
    for value in far_q:
        grads_q += [value, ex.swap(value, tensor=1)]
    left = kernel_call(
        functools.partial(left_kernel, parts, 1.0 / replicas),
        [struct((rows // (SPLIT * ex.quad), rank))] * (SPLIT * ex.quad),
        4 * rows * tokens * rank, where, acts, base, *grads_q,
        scratch=[pltpu.VMEM((tokens, 2 * rank), BF16), pltpu.VMEM((rows, rank), F32)], vmem=LEFT,
    )

    quad = range(1, ex.quad)
    received = []
    for h in range(SPLIT):
        received.append([ex.swap(left[m * SPLIT + h], dp=m) for m in quad])
    grads = {0: out_grad, 1: ex.swap(out_grad, tensor=1)}
    sums = []
    for h in range(SPLIT):
        total = left[h]
        for piece in tied(received[h], sums):
            total = total + piece
        sums.append(total)
    held = tied(out_grad, grads_q[1:])
    for m in range(2, parts, 2):
        grads[m] = ex.swap(held, tensor=m)
    for mask in ex.higher:
        others = [ex.swap(value, dp=mask) for value in sums]
        added = []
        for value, other in zip(sums, others):
            added.append(value + tied(other, added))
        sums = added
    for m in range(2, parts, 2):
        grads[m] = tied(grads[m], sums)
        grads[m + 1] = ex.swap(grads[m], tensor=1)
    lefts = list(sums)
    for m in quad:
        lefts += [ex.swap(value, dp=m) for value in sums]
    grads = [grads[m] for m in range(parts)]

    high, low = kernel_call(
        functools.partial(buffer_kernel, parts),
        (struct((rows, columns), BF16), struct((rows, columns), BF16)),
        2 * rows * tokens * columns, where, acts, momentum, *grads, grid=(steps,),
        in_specs=[None, acts_spec, wide_spec] + [None] * parts, out_specs=(wide_spec, wide_spec), vmem=34,
    )

    lefts[SPLIT:] = tied(lefts[SPLIT:], high)
    gram = kernel_call(gram_kernel, struct((rank, rank)), 12 * rows * rank * rank, *lefts)
    lefts_b = tied(lefts, gram)
    near_gram = ex.swap(gram, tensor=1)
    blocks = rank // BLOCK
    count = xs * ex.quad

    def shares(other, first, number):
        core = 1 - ex.core if other else ex.core
        at = jnp.stack([ex.x * 2 + core, ex.q, core]).astype(jnp.int32)
        spec = pl.BlockSpec((rows, local), lambda i, j, w: (0, w[0] ^ (2 * (i + first))))
        return kernel_call(
            functools.partial(share_kernel, ex.quad, 1.0 / replicas),
            struct((number, 1, local, rank)), 6 * rows * number * local * rank,
            at, high, low, *lefts_b, grid=(number, 1), prefetch=1,
            in_specs=[None, spec, spec] + [None] * len(lefts_b),
            out_specs=pl.BlockSpec((1, 1, local, rank), lambda i, j, w: (i, 0, 0, 0)),
            scratch=[pltpu.VMEM((rows, 2 * rank), BF16)], vmem=VMEM,
        ).reshape(number * ex.quad, local // ex.quad, rank)

    send = shares(True, 0, xs)
    got = ex.swap(send, tensor=1)
    gram = gram + tied(near_gram, send)
    grams = [ex.swap(gram, tensor=m) for m in range(2, parts, 2)]
    keep = shares(False, 0, xs)
    share = keep + got
    part = share[0]
    pieces = [
        ex.swap(share[m], dp=m % ex.quad, tensor=2 * (m // ex.quad)) for m in range(1, count)
    ]
    total = gram
    for piece in tied(grams, pieces[-1]):
        total = total + piece
    state = chol_inverse(total, 0, blocks // 2)
    for piece in tied(pieces, state):
        part = part + piece
    inverse = chol_inverse(tied(state, part), blocks // 2, blocks)
    for mask in ex.higher:
        part = part + tied(ex.swap(part, dp=mask), inverse)

    right, narrow = kernel_call(
        right_kernel, (struct(part.shape), struct((part.shape[0] + EXTRA, rank), BF16)),
        12 * part.shape[0] * rank * rank, part, inverse,
    )
    exact = [right] + [ex.swap(right, dp=m) for m in quad]
    across = [
        ex.swap(narrow, dp=m % ex.quad, tensor=2 * (m // ex.quad)) for m in range(ex.quad, count)
    ]
    ortho, narrow = kernel_call(
        ortho_kernel,
        (struct((rows, rank)), struct((rows, rank), BF16)),
        12 * rows * rank * rank, tied(where, right), inverse, *lefts,
    )
    exact[1:], across = tied((exact[1:], across), ortho)
    own, side = kernel_call(
        functools.partial(collect_kernel, xs, ex.quad),
        (struct((local, rank)), struct((xs * local + EXTRA, rank), BF16)),
        2 * local * rank, where, *exact, *across,
    )
    other = ex.swap(side, tensor=1)
    new_momentum, new_q = kernel_call(
        functools.partial(update_kernel, xs),
        (struct((rows, columns)), struct((local, rank))),
        2 * rows * columns * rank, where, high, low, narrow, side, other, own, grid=(steps,),
        in_specs=[None, wide_spec, wide_spec, rank_spec, None, None, None],
        out_specs=(wide_spec, pl.BlockSpec((local, rank), lambda i: (0, 0))),
        scratch=[pltpu.VMEM((columns, rank), BF16)], vmem=VMEM,
    )
    return (new_momentum, ortho, new_q)


def solution(mesh):
    in_specs = (
        P("dp", "tensor"),
        P(("dp", "tensor"), None),
        P(("dp", "tensor"), None),
        P("tensor", None),
    )
    out_specs = (P(("dp", "tensor"), None), P("tensor", None), P("tensor", None))
    return jax.shard_map(step, mesh=mesh, in_specs=in_specs, out_specs=out_specs, check_vma=False)
```

time: 182 us -> 156 us (0.86)
  waiting for transfers between devices: 65.2 us -> 27.1 us
  starting transfers between devices: 47.4 us -> 59.4 us
  Pallas kernels: 47.8 us -> 58.9 us
  local copies, waits for them, and re-layouts: 13.6 us -> 6.1 us
  other arithmetic: 6.24 us -> 3 us
    ppermute x17 -> x15, waiting for transfers between devices: 36.2 us -> 15.4 us  [swap(): return lax.ppermute(value, 'tensor', [(i, i ^ tensor) for i in range(n)])]
    ppermute x14 -> x21, waiting for transfers between devices: 26.1 us -> 11.1 us  [swap(): return lax.ppermute(value, 'dp', [(i, i ^ dp) for i in range(m)])]
    ppermute x14 -> x21, starting transfers between devices: 24.4 us -> 39.3 us  [swap(): return lax.ppermute(value, 'dp', [(i, i ^ dp) for i in range(m)])]
    pallas_call x11 -> x15, Pallas kernels: 47.8 us -> 58.9 us  [kernel_call(): pl.pallas_call(kernel, out_shape=out, grid_spec=pltpu.PrefetchScalarGridS...]
    unnamed x42 -> x24, local copies, waits for them, and re-layouts: 11 us -> 6.02 us
    add x8 -> x9, other arithmetic: 5.32 us -> 2.26 us  [the longest x3 1.95 us: step(): total = total + piece]
    ppermute x17 -> x15, starting transfers between devices: 12.5 us -> 10.2 us  [swap(): return lax.ppermute(value, 'tensor', [(i, i ^ tensor) for i in range(n)])]
    ppermute x6, waiting for transfers between devices: 2.89 us -> 0.58 us  [swap(): return lax.ppermute(value, ('dp', 'tensor'), perm)]
  transfers between devices with their start and end apart: 37 -> 42, of which waited for: 18 -> 13; matrix products, arithmetic and copies ran while one was open for 4% -> 2% of each run, Pallas kernels for 17% -> 28%
where the time goes in v2:
time: 156 us; the launch traced here: 155 us
  starting transfers between devices  59.4 us (38%)
  Pallas kernels  58.9 us (38%)
  waiting for transfers between devices  27.1 us (17%)
  local copies, waits for them, and re-layouts  6.1 us (4%)
  other arithmetic  3 us (2%)
    pallas_call x15, Pallas kernels, kernel_call(): pl.pallas_call(kernel, out_shape=out, grid_spec=pltpu.PrefetchScalarGridS...  58.9 us
    ppermute x21, starting transfers between devices, swap(): return lax.ppermute(value, 'dp', [(i, i ^ dp) for i in range(m)])  39.3 us
    ppermute x15, waiting for transfers between devices, swap(): return lax.ppermute(value, 'tensor', [(i, i ^ tensor) for i in range(n)])  15.4 us
    ppermute x21, waiting for transfers between devices, swap(): return lax.ppermute(value, 'dp', [(i, i ^ dp) for i in range(m)])  11.1 us
    ppermute x15, starting transfers between devices, swap(): return lax.ppermute(value, 'tensor', [(i, i ^ tensor) for i in range(n)])  10.2 us
    ppermute x6, starting transfers between devices, swap(): return lax.ppermute(value, ('dp', 'tensor'), perm)  9.97 us
    unnamed x24, local copies, waits for them, and re-layouts  6.02 us
  transfers between devices with their start and end apart: 42, of which 13 were waited for; matrix products, arithmetic and copies ran while one was open for 2% of the time, Pallas kernels for 28%

profile of v2, /device:TPU:0, one launch (start us, length us, event | category | flops | bytes accessed | tf_op | source)
XLA Modules:
  0.0 155.4 jit_solution(8511022503887182497)
XLA Ops:
  1.2 2.6 %collective-permute-start.1 = (f32[512,256]{1,0:T(8,128)}, f32[512,256]{1,0:T(8,128)S(1)}, u32[]{:S(2)}, u32[]{:S(2)}) collective-permute-start(f32[512,256]{1,0:T(8,128)} %refs_0_.2), channel_id=1, source_target_pairs={{0,2},{1,3},{2,0},{3,1},{4,6},{5,7},{6,4},{7,5},{8,10},{9,11},{10,... | collective-permute-start | bytes 1572872 | tf_op jit(solution)/shard_map/ppermute | solution.py:356
  4.4 1.2 copy-done
  6.7 1.2 shard_map.67
  8.9 6.1 %shard_map.68.refs_0_ = f32[1280,256]{1,0:T(8,128)} custom-call(s32[2]{0:T(128)} %pad_add_fusion.1.where_ref, f32[1280,2048]{1,0:T(8,128)} %momentum_ref.5, bf16[1024,512]{1,0:T(8,128)(2,1)} %copy-done.3), custom_call_target="tpu_custom_call" | custom-call | flops 2013265920 | bytes 12845064 | tf_op jit(solution)/shard_map/pallas_call | solution.py:125
  14.9 1.5 collective-permute-done.1.refs_0_
  16.5 1.9 %collective-permute-done.3.refs_1_ = f32[512,256]{1,0:T(8,128)S(1)} collective-permute-done((f32[512,256]{1,0:T(8,128)S(1)}, f32[512,256]{1,0:T(8,128)S(1)}, u32[]{:S(2)}, u32[]{:S(2)}) %collective-permute-start.3) | collective-permute-done | bytes 524320 | tf_op jit(solution)/shard_map/ppermute | solution.py:356
  18.4 1.2 shard_map.69
  20.6 1.7 %collective-permute-start.5 = (f32[256,256]{1,0:T(8,128)S(1)}, f32[256,256]{1,0:T(8,128)S(1)}, u32[]{:S(2)}, u32[]{:S(2)}) collective-permute-start(f32[256,256]{1,0:T(8,128)S(1)} %get-tuple-element.72.refs_0_), channel_id=1, source_target_pairs={{0,2},{1,3},{2,0},{3,1},{4,6},{5,7},{6,4},{7,5},{8,10},{9,11},{10,... | collective-permute-start | bytes 786440 | tf_op jit(solution)/shard_map/ppermute | solution.py:356
  22.4 6.1 %shard_map.70.base_ref = f32[1280,256]{1,0:T(8,128)} custom-call(s32[2]{0:T(128)} %pad_add_fusion.1.where_ref, f32[1280,2048]{1,0:T(8,128)} %momentum_ref.5, bf16[1024,512]{1,0:T(8,128)(2,1)} %copy-done.4, f32[1280,256]{1,0:T(8,128)} %shard_map.68.refs_0_), custom_call_target="tpu_custom_call" | custom-call | flops 2013265920 | bytes 14155784 | tf_op jit(solution)/shard_map/pallas_call | solution.py:125
  29.1 1.4 collective-permute-done.6.refs_3_
  30.5 1.7 %collective-permute-start.7 = (bf16[256,2048]{1,0:T(8,128)(2,1)S(1)}, bf16[256,2048]{1,0:T(8,128)(2,1)S(1)}, u32[]{:S(2)}, u32[]{:S(2)}) collective-permute-start(bf16[256,2048]{1,0:T(8,128)(2,1)S(1)} %copy-done.1), channel_id=1, source_target_pairs={{0,2},{1,3},{2,0},{3,1},{4,6},{5,7},{6,4},{7,5},{8,10},{9,11},{10,... | collective-permute-start | bytes 3145736 | tf_op jit(solution)/shard_map/ppermute | solution.py:356
  32.3 5.2 %shard_map.71 = (f32[160,256]{1,0:T(8,128)}, f32[160,256]{1,0:T(8,128)}, f32[160,256]{1,0:T(8,128)}, f32[160,256]{1,0:T(8,128)}, f32[160,256]{1,0:T(8,128)}, /*i...) custom-call(s32[2]{0:T(128)} %copy-done.7, bf16[1024,1280]{1,0:T(8,128)(2,1)} %acts_ref.3, ...), custom_call_target="tpu_custom_call" | custom-call | flops 1342177280 | bytes 6291464 | tf_op jit(solution)/shard_map/pallas_call | solution.py:125
  37.5 1.5 collective-permute-start.8
  39.0 1.6 %collective-permute-start.9 = (f32[160,256]{1,0:T(8,128)}, f32[160,256]{1,0:T(8,128)S(1)}, u32[]{:S(2)}, u32[]{:S(2)}) collective-permute-start(f32[160,256]{1,0:T(8,128)} %get-tuple-element.78), channel_id=1, source_target_pairs={{0,8},{4,12},{8,0},{12,4},{16,24},{20,28},{24,16},{28,20},{1,9},{5... | collective-permute-start | bytes 491528 | tf_op jit(solution)/shard_map/ppermute | solution.py:358
  41.0 1.5 collective-permute-start.12
  42.5 3.0 %collective-permute-done.8 = f32[160,256]{1,0:T(8,128)S(1)} collective-permute-done((f32[160,256]{1,0:T(8,128)}, f32[160,256]{1,0:T(8,128)S(1)}, u32[]{:S(2)}, u32[]{:S(2)}) %collective-permute-start.8) | collective-permute-done | bytes 163872 | tf_op jit(solution)/shard_map/ppermute | solution.py:358
  45.5 1.7 %collective-permute-start.13 = (f32[160,256]{1,0:T(8,128)}, f32[160,256]{1,0:T(8,128)S(1)}, u32[]{:S(2)}, u32[]{:S(2)}) collective-permute-start(f32[160,256]{1,0:T(8,128)} %get-tuple-element.85), channel_id=1, source_target_pairs={{0,8},{4,12},{8,0},{12,4},{16,24},{20,28},{24,16},{28,20},{1,9},{5... | collective-permute-start | bytes 491528 | tf_op jit(solution)/shard_map/ppermute | solution.py:358
  47.2 1.4 collective-permute-start.14
  48.6 1.1 collective-permute-done.10
  50.7 3.8 %collective-permute-start.11 = (f32[160,256]{1,0:T(8,128)S(1)}, f32[160,256]{1,0:T(8,128)S(1)}, u32[]{:S(2)}, u32[]{:S(2)}) collective-permute-start(f32[160,256]{1,0:T(8,128)S(1)} %add_add_fusion.1), channel_id=1, source_target_pairs={{0,24},{4,28},{8,16},{12,20},{16,8},{20,12},{24,0},{28,4},{1,25},{... | collective-permute-start | bytes 491528 | tf_op jit(solution)/shard_map/ppermute | solution.py:358
  54.4 1.6 %collective-permute-done.14 = f32[160,256]{1,0:T(8,128)S(1)} collective-permute-done((f32[160,256]{1,0:T(8,128)}, f32[160,256]{1,0:T(8,128)S(1)}, u32[]{:S(2)}, u32[]{:S(2)}) %collective-permute-start.14) | collective-permute-done | bytes 163872 | tf_op jit(solution)/shard_map/ppermute | solution.py:358
  57.0 6.5 %collective-permute-start.15 = (f32[160,256]{1,0:T(8,128)S(1)}, f32[160,256]{1,0:T(8,128)S(1)}, u32[]{:S(2)}, u32[]{:S(2)}) collective-permute-start(f32[160,256]{1,0:T(8,128)S(1)} %add_add_fusion), channel_id=1, source_target_pairs={{0,24},{4,28},{8,16},{12,20},{16,8},{20,12},{24,0},{28,4},{1,25},{... | collective-permute-start | bytes 491528 | tf_op jit(solution)/shard_map/ppermute | solution.py:358
  63.6 3.4 %collective-permute-done.15 = f32[160,256]{1,0:T(8,128)S(1)} collective-permute-done((f32[160,256]{1,0:T(8,128)S(1)}, f32[160,256]{1,0:T(8,128)S(1)}, u32[]{:S(2)}, u32[]{:S(2)}) %collective-permute-start.15) | collective-permute-done | bytes 163872 | tf_op jit(solution)/shard_map/ppermute | solution.py:358
  67.3 4.5 %collective-permute-start.19 = (f32[160,256]{1,0:T(8,128)S(1)}, f32[160,256]{1,0:T(8,128)S(1)}, u32[]{:S(2)}, u32[]{:S(2)}) collective-permute-start(f32[160,256]{1,0:T(8,128)S(1)} %add.75.refs_0_), channel_id=1, source_target_pairs={{0,8},{4,12},{8,0},{12,4},{16,24},{20,28},{24,16},{28,20},{1,9},{5... | collective-permute-start | bytes 491528 | tf_op jit(solution)/shard_map/ppermute | solution.py:358
  71.9 1.5 collective-permute-start.22
  73.4 1.7 %collective-permute-done.21.refs_6_ = f32[160,256]{1,0:T(8,128)S(1)} collective-permute-done((f32[160,256]{1,0:T(8,128)S(1)}, f32[160,256]{1,0:T(8,128)S(1)}, u32[]{:S(2)}, u32[]{:S(2)}) %collective-permute-start.21) | collective-permute-done | bytes 163872 | tf_op jit(solution)/shard_map/ppermute | solution.py:358
  75.1 1.7 %collective-permute-start.20 = (f32[160,256]{1,0:T(8,128)S(1)}, f32[160,256]{1,0:T(8,128)S(1)}, u32[]{:S(2)}, u32[]{:S(2)}) collective-permute-start(f32[160,256]{1,0:T(8,128)S(1)} %add.79.refs_1_), channel_id=1, source_target_pairs={{0,8},{4,12},{8,0},{12,4},{16,24},{20,28},{24,16},{28,20},{1,9},{5... | collective-permute-start | bytes 491528 | tf_op jit(solution)/shard_map/ppermute | solution.py:358
  76.8 1.5 collective-permute-start.18
  78.3 1.7 %copy-done.2 = bf16[1024,1280]{1,0:T(8,128)(2,1)S(1)} copy-done((bf16[1024,1280]{1,0:T(8,128)(2,1)S(1)}, bf16[1024,1280]{1,0:T(8,128)(2,1)}, u32[]{:S(2)}) %copy-start.2) | copy-done | bytes 2621464
  80.1 9.8 %shard_map.72 = (bf16[1280,2048]{1,0:T(8,128)(2,1)S(1)}, bf16[1280,2048]{1,0:T(8,128)(2,1)S(1)}) custom-call(s32[2]{0:T(128)S(1)} %copy-done.8, bf16[1024,1280]{1,0:T(8,128)(2,1)S(1)} %copy-done.2, f32[1280,2048]{1,0:T(8,128)} %momentum_ref.5, bf16[256,2048]{1,0:T(8,128)(2,1)S(1)} %copy-done.1, bf16[256,2048]{1,0:T(8,128)(2,1)} %collective-permute-done.refs_1_, ...), custom_call_target="tpu_custom_call" | custom-call | flops 5368709120 | bytes 27787272 | tf_op jit(solution)/shard_map/pallas_call | solution.py:125
  89.9 2.0 %shard_map.73 = f32[256,256]{1,0:T(8,128)S(1)} custom-call(f32[160,256]{1,0:T(8,128)S(1)} %add.75.refs_0_, f32[160,256]{1,0:T(8,128)S(1)} %add.79.refs_1_, f32[160,256]{1,0:T(8,128)S(1)} %collective-permute-done.17.refs_2_, f32[160,256]{1,0:T(8,128)S(1)} %collective-permute-done.18.refs_3_, f32[160,256]{1,0:T(8,128)S(1)} %collective-permute-done.19.refs_4_, ...), custom_call_target="tpu_custom_call" | custom-call | flops 1006632960 | bytes 1572864 | tf_op jit(solution)/shard_map/pallas_call | solution.py:125
  92.0 4.0 %shard_map.75 = f32[2,1,512,256]{3,2,1,0:T(8,128)S(1)} custom-call(s32[3]{0:T(128)S(1)} %get-tuple-element.143.where_ref, bf16[1280,2048]{1,0:T(8,128)(2,1)S(1)} %get-tuple-element.92.high_ref, bf16[1280,2048]{1,0:T(8,128)(2,1)S(1)} %get-tuple-element.93.low_ref, f32[160,256]{1,0:T(8,128)S(1)} %add.75.refs_0_, f32[160,256]{1,0:T(8,128)S(1)} %add.79.refs_1_, ...), custom_call_target="tpu_custom_call" | custom-call | flops 2013265920 | bytes 12845068 | tf_op jit(solution)/shard_map/pallas_call | solution.py:125
  96.6 4.2 %shard_map.74 = f32[2,1,512,256]{3,2,1,0:T(8,128)S(1)} custom-call(s32[3]{0:T(128)S(1)} %get-tuple-element.142.where_ref, bf16[1280,2048]{1,0:T(8,128)(2,1)S(1)} %get-tuple-element.92.high_ref, bf16[1280,2048]{1,0:T(8,128)(2,1)S(1)} %get-tuple-element.93.low_ref, f32[160,256]{1,0:T(8,128)S(1)} %add.75.refs_0_, f32[160,256]{1,0:T(8,128)S(1)} %add.79.refs_1_, ...), custom_call_target="tpu_custom_call" | custom-call | flops 2013265920 | bytes 12845068 | tf_op jit(solution)/shard_map/pallas_call | solution.py:125
  101.4 2.7 %collective-permute-start.30 = (f32[128,256]{1,0:T(8,128)S(1)}, f32[128,256]{1,0:T(8,128)S(1)}, u32[]{:S(2)}, u32[]{:S(2)}) collective-permute-start(f32[128,256]{1,0:T(8,128)S(1)} %get-tuple-element.135), channel_id=1, source_target_pairs={{0,14},{1,15},{2,12},{3,13},{4,10},{5,11},{6,8},{7,9},{8,6},{9,7},... | collective-permute-start | bytes 393224 | tf_op jit(solution)/shard_map/ppermute | solution.py:361
  105.0 2.0 %collective-permute-start.28 = (f32[128,256]{1,0:T(8,128)S(1)}, f32[128,256]{1,0:T(8,128)S(1)}, u32[]{:S(2)}, u32[]{:S(2)}) collective-permute-start(f32[128,256]{1,0:T(8,128)S(1)} %get-tuple-element.137), channel_id=1, source_target_pairs={{0,6},{1,7},{2,4},{3,5},{4,2},{5,3},{6,0},{7,1},{8,14},{9,15},{10,... | collective-permute-start | bytes 393224 | tf_op jit(solution)/shard_map/ppermute | solution.py:361
  107.6 8.1 %collective-permute-done.32 = f32[256,256]{1,0:T(8,128)S(1)} collective-permute-done((f32[256,256]{1,0:T(8,128)S(1)}, f32[256,256]{1,0:T(8,128)S(1)}, u32[]{:S(2)}, u32[]{:S(2)}) %collective-permute-start.32) | collective-permute-done | bytes 262176 | tf_op jit(solution)/shard_map/ppermute | solution.py:356
  115.7 1.5 collective-permute-start.26
  117.7 1.6 %collective-permute-start.24 = (f32[128,256]{1,0:T(8,128)S(1)}, f32[128,256]{1,0:T(8,128)S(1)}, u32[]{:S(2)}, u32[]{:S(2)}) collective-permute-start(f32[128,256]{1,0:T(8,128)S(1)} %get-tuple-element.141), channel_id=1, source_target_pairs={{0,4},{4,0},{8,12},{12,8},{16,20},{20,16},{24,28},{28,24},{1,5},{5... | collective-permute-start | bytes 393224 | tf_op jit(solution)/shard_map/ppermute | solution.py:358
  119.3 4.0 %shard_map.76.gram_ref = f32[256,256]{1,0:T(8,128)S(1)} custom-call(f32[256,256]{1,0:T(8,128)S(1)} %add.85.gram_ref), custom_call_target="tpu_custom_call" | custom-call | flops 2000000000 | bytes 524288 | tf_op jit(solution)/shard_map/pallas_call | solution.py:125
  123.7 3.9 %collective-permute-start.33 = (f32[128,256]{1,0:T(8,128)S(1)}, f32[128,256]{1,0:T(8,128)S(1)}, u32[]{:S(2)}, u32[]{:S(2)}) collective-permute-start(f32[128,256]{1,0:T(8,128)S(1)} %fusion.6), channel_id=1, source_target_pairs={{0,24},{4,28},{8,16},{12,20},{16,8},{20,12},{24,0},{28,4},{1,25},{... | collective-permute-start | bytes 393224 | tf_op jit(solution)/shard_map/ppermute | solution.py:358
  127.6 3.8 %shard_map.77.inverse_ref = f32[256,256]{1,0:T(8,128)S(1)} custom-call(f32[256,256]{1,0:T(8,128)S(1)} %shard_map.76.gram_ref), custom_call_target="tpu_custom_call" | custom-call | flops 2000000000 | bytes 524288 | tf_op jit(solution)/shard_map/pallas_call | solution.py:125
  131.8 2.8 %collective-permute-start.40 = (bf16[144,256]{1,0:T(8,128)(2,1)S(1)}, bf16[144,256]{1,0:T(8,128)(2,1)S(1)}, u32[]{:S(2)}, u32[]{:S(2)}) collective-permute-start(bf16[144,256]{1,0:T(8,128)(2,1)S(1)} %get-tuple-element.122), channel_id=1, source_target_pairs={{0,14},{1,15},{2,12},{3,13},{4,10},{5,11},{6,8},{7,9},{8,6},{9,7},... | collective-permute-start | bytes 221192 | tf_op jit(solution)/shard_map/ppermute | solution.py:361
  135.5 1.6 %collective-permute-start.36 = (f32[128,256]{1,0:T(8,128)S(1)}, f32[128,256]{1,0:T(8,128)S(1)}, u32[]{:S(2)}, u32[]{:S(2)}) collective-permute-start(f32[128,256]{1,0:T(8,128)S(1)} %get-tuple-element.119.refs_0_), channel_id=1, source_target_pairs={{0,12},{4,8},{8,4},{12,0},{16,28},{20,24},{24,20},{28,16},{1,13},{... | collective-permute-start | bytes 393224 | tf_op jit(solution)/shard_map/ppermute | solution.py:358
  138.0 1.5 collective-permute-start.34
  140.6 1.9 %collective-permute-start.37 = (bf16[144,256]{1,0:T(8,128)(2,1)S(1)}, bf16[144,256]{1,0:T(8,128)(2,1)S(1)}, u32[]{:S(2)}, u32[]{:S(2)}) collective-permute-start(bf16[144,256]{1,0:T(8,128)(2,1)S(1)} %get-tuple-element.122), channel_id=1, source_target_pairs={{0,2},{1,3},{2,0},{3,1},{4,6},{5,7},{6,4},{7,5},{8,10},{9,11},{10,... | collective-permute-start | bytes 221192 | tf_op jit(solution)/shard_map/ppermute | solution.py:356
  142.5 3.9 %shard_map.79 = (f32[1280,256]{1,0:T(8,128)}, bf16[1280,256]{1,0:T(8,128)(2,1)S(1)}) custom-call(s32[2]{0:T(128)S(1)} %copy-done.8, f32[256,256]{1,0:T(8,128)S(1)} %shard_map.77.inverse_ref, f32[160,256]{1,0:T(8,128)S(1)} %add.75.refs_0_, f32[160,256]{1,0:T(8,128)S(1)} %add.79.refs_1_, f32[160,256]{1,0:T(8,128)S(1)} %collective-permute-done.17.refs_2_, ...), custom_call_target="tpu_custom_call" | custom-call | flops 1006632960 | bytes 3538952 | tf_op jit(solution)/shard_map/pallas_call | solution.py:125
  147.2 1.9 %collective-permute-done.41.other_ref = bf16[1040,256]{1,0:T(8,128)(2,1)S(1)} collective-permute-done((bf16[1040,256]{1,0:T(8,128)(2,1)S(1)}, bf16[1040,256]{1,0:T(8,128)(2,1)S(1)}, u32[]{:S(2)}, u32[]{:S(2)}) %collective-permute-start.41) | collective-permute-done | bytes 532512 | tf_op jit(solution)/shard_map/ppermute | solution.py:356
  149.1 6.3 %shard_map.81 = (f32[1280,2048]{1,0:T(8,128)}, f32[512,256]{1,0:T(8,128)}) custom-call(s32[2]{0:T(128)S(1)} %copy-done.8, bf16[1280,2048]{1,0:T(8,128)(2,1)S(1)} %get-tuple-element.92.high_ref, bf16[1280,2048]{1,0:T(8,128)(2,1)S(1)} %get-tuple-element.93.low_ref, bf16[1280,256]{1,0:T(8,128)(2,1)S(1)} %get-tuple-element.121.ortho_ref, ...), custom_call_target="tpu_custom_call" | custom-call | flops 1342177280 | bytes 23740424 | tf_op jit(solution)/shard_map/pallas_call | solution.py:125
  (88 shorter events, 15.3 us)
Async XLA Ops:
  0.6 3.8 %collective-permute-start.2 = (f32[512,256]{1,0:T(8,128)}, f32[512,256]{1,0:T(8,128)S(1)}, u32[]{:S(2)}, u32[]{:S(2)}) collective-permute-start(f32[512,256]{1,0:T(8,128)} %refs_0_.2), channel_id=1, source_target_pairs={{0,1},{1,0},{2,3},{3,2},{4,5},{5,4},{6,7},{7,6},{8,9},{9,8},{10,11... | collective-permute-start | bytes 1572872 | tf_op jit(solution)/shard_map/ppermute | solution.py:356
  1.2 15.3 %collective-permute-start.1 = (f32[512,256]{1,0:T(8,128)}, f32[512,256]{1,0:T(8,128)S(1)}, u32[]{:S(2)}, u32[]{:S(2)}) collective-permute-start(f32[512,256]{1,0:T(8,128)} %refs_0_.2), channel_id=1, source_target_pairs={{0,2},{1,3},{2,0},{3,1},{4,6},{5,7},{6,4},{7,5},{8,10},{9,11},{10,... | collective-permute-start | bytes 1572872 | tf_op jit(solution)/shard_map/ppermute | solution.py:356
  3.8 14.6 %copy-start.7 = (s32[2]{0:T(128)}, s32[2]{0:T(128)S(1)}, u32[]{:S(2)}) copy-start(s32[2]{0:T(128)S(1)} %pad_add_fusion.where_ref) | copy-start | bytes 28
  8.9 9.5 %copy-start.1 = (bf16[256,2048]{1,0:T(8,128)(2,1)S(1)}, bf16[256,2048]{1,0:T(8,128)(2,1)}, u32[]{:S(2)}) copy-start(bf16[256,2048]{1,0:T(8,128)(2,1)} %refs_0_.3) | copy-start | bytes 3145732
  16.5 1.9 %collective-permute-start.3 = (f32[512,256]{1,0:T(8,128)S(1)}, f32[512,256]{1,0:T(8,128)S(1)}, u32[]{:S(2)}, u32[]{:S(2)}) collective-permute-start(f32[512,256]{1,0:T(8,128)S(1)} %collective-permute-done.1.refs_0_), channel_id=1, source_target_pairs={{0,1},{1,0},{2,3},{3,2},{4,5},{5,4},{6,7},{7,6},{8,9},{9,8},{10,11... | collective-permute-start | bytes 1572872 | tf_op jit(solution)/shard_map/ppermute | solution.py:356
  20.6 7.9 %copy-start.6 = (f32[256,256]{1,0:T(8,128)}, f32[256,256]{1,0:T(8,128)S(1)}, u32[]{:S(2)}) copy-start(f32[256,256]{1,0:T(8,128)S(1)} %get-tuple-element.72.refs_0_) | copy-start | bytes 786436
  20.6 8.4 %collective-permute-start.5 = (f32[256,256]{1,0:T(8,128)S(1)}, f32[256,256]{1,0:T(8,128)S(1)}, u32[]{:S(2)}, u32[]{:S(2)}) collective-permute-start(f32[256,256]{1,0:T(8,128)S(1)} %get-tuple-element.72.refs_0_), channel_id=1, source_target_pairs={{0,2},{1,3},{2,0},{3,1},{4,6},{5,7},{6,4},{7,5},{8,10},{9,11},{10,... | collective-permute-start | bytes 786440 | tf_op jit(solution)/shard_map/ppermute | solution.py:356
  22.4 6.7 %collective-permute-start.4 = (f32[256,256]{1,0:T(8,128)S(1)}, f32[256,256]{1,0:T(8,128)S(1)}, u32[]{:S(2)}, u32[]{:S(2)}) collective-permute-start(f32[256,256]{1,0:T(8,128)S(1)} %get-tuple-element.72.refs_0_), channel_id=1, source_target_pairs={{0,1},{1,0},{2,3},{3,2},{4,5},{5,4},{6,7},{7,6},{8,9},{9,8},{10,11... | collective-permute-start | bytes 786440 | tf_op jit(solution)/shard_map/ppermute | solution.py:356
  28.5 49.8 %copy-start.8 = (s32[2]{0:T(128)S(1)}, s32[2]{0:T(128)}, u32[]{:S(2)}) copy-start(s32[2]{0:T(128)} %copy-done.7) | copy-start | bytes 28
  29.0 3.3 %copy-start.9 = (f32[256,256]{1,0:T(8,128)}, f32[256,256]{1,0:T(8,128)S(1)}, u32[]{:S(2)}) copy-start(f32[256,256]{1,0:T(8,128)S(1)} %collective-permute-done.5.refs_2_) | copy-start | bytes 786436
  29.0 1.5 collective-permute-start.6
  29.1 3.2 %copy-start.10 = (f32[256,256]{1,0:T(8,128)}, f32[256,256]{1,0:T(8,128)S(1)}, u32[]{:S(2)}) copy-start(f32[256,256]{1,0:T(8,128)S(1)} %collective-permute-done.4.refs_1_) | copy-start | bytes 786436
  30.5 36.4 %collective-permute-start.7 = (bf16[256,2048]{1,0:T(8,128)(2,1)S(1)}, bf16[256,2048]{1,0:T(8,128)(2,1)S(1)}, u32[]{:S(2)}, u32[]{:S(2)}) collective-permute-start(bf16[256,2048]{1,0:T(8,128)(2,1)S(1)} %copy-done.1), channel_id=1, source_target_pairs={{0,2},{1,3},{2,0},{3,1},{4,6},{5,7},{6,4},{7,5},{8,10},{9,11},{10,... | collective-permute-start | bytes 3145736 | tf_op jit(solution)/shard_map/ppermute | solution.py:356
  37.5 8.0 %collective-permute-start.8 = (f32[160,256]{1,0:T(8,128)}, f32[160,256]{1,0:T(8,128)S(1)}, u32[]{:S(2)}, u32[]{:S(2)}) collective-permute-start(f32[160,256]{1,0:T(8,128)} %get-tuple-element.77), channel_id=1, source_target_pairs={{0,4},{4,0},{8,12},{12,8},{16,20},{20,16},{24,28},{28,24},{1,5},{5... | collective-permute-start | bytes 491528 | tf_op jit(solution)/shard_map/ppermute | solution.py:358
  39.0 8.2 %collective-permute-start.9 = (f32[160,256]{1,0:T(8,128)}, f32[160,256]{1,0:T(8,128)S(1)}, u32[]{:S(2)}, u32[]{:S(2)}) collective-permute-start(f32[160,256]{1,0:T(8,128)} %get-tuple-element.78), channel_id=1, source_target_pairs={{0,8},{4,12},{8,0},{12,4},{16,24},{20,28},{24,16},{28,20},{1,9},{5... | collective-permute-start | bytes 491528 | tf_op jit(solution)/shard_map/ppermute | solution.py:358
  40.6 9.1 %collective-permute-start.10 = (f32[160,256]{1,0:T(8,128)}, f32[160,256]{1,0:T(8,128)S(1)}, u32[]{:S(2)}, u32[]{:S(2)}) collective-permute-start(f32[160,256]{1,0:T(8,128)} %get-tuple-element.79), channel_id=1, source_target_pairs={{0,12},{4,8},{8,4},{12,0},{16,28},{20,24},{24,20},{28,16},{1,13},{... | collective-permute-start | bytes 491528 | tf_op jit(solution)/shard_map/ppermute | solution.py:358
  41.0 13.4 %collective-permute-start.12 = (f32[160,256]{1,0:T(8,128)}, f32[160,256]{1,0:T(8,128)S(1)}, u32[]{:S(2)}, u32[]{:S(2)}) collective-permute-start(f32[160,256]{1,0:T(8,128)} %get-tuple-element.84), channel_id=1, source_target_pairs={{0,4},{4,0},{8,12},{12,8},{16,20},{20,16},{24,28},{28,24},{1,5},{5... | collective-permute-start | bytes 491528 | tf_op jit(solution)/shard_map/ppermute | solution.py:358
  45.5 8.9 %collective-permute-start.13 = (f32[160,256]{1,0:T(8,128)}, f32[160,256]{1,0:T(8,128)S(1)}, u32[]{:S(2)}, u32[]{:S(2)}) collective-permute-start(f32[160,256]{1,0:T(8,128)} %get-tuple-element.85), channel_id=1, source_target_pairs={{0,8},{4,12},{8,0},{12,4},{16,24},{20,28},{24,16},{28,20},{1,9},{5... | collective-permute-start | bytes 491528 | tf_op jit(solution)/shard_map/ppermute | solution.py:358
  47.2 8.9 %collective-permute-start.14 = (f32[160,256]{1,0:T(8,128)}, f32[160,256]{1,0:T(8,128)S(1)}, u32[]{:S(2)}, u32[]{:S(2)}) collective-permute-start(f32[160,256]{1,0:T(8,128)} %get-tuple-element.86), channel_id=1, source_target_pairs={{0,12},{4,8},{8,4},{12,0},{16,28},{20,24},{24,20},{28,16},{1,13},{... | collective-permute-start | bytes 491528 | tf_op jit(solution)/shard_map/ppermute | solution.py:358
  50.7 12.9 %collective-permute-start.11 = (f32[160,256]{1,0:T(8,128)S(1)}, f32[160,256]{1,0:T(8,128)S(1)}, u32[]{:S(2)}, u32[]{:S(2)}) collective-permute-start(f32[160,256]{1,0:T(8,128)S(1)} %add_add_fusion.1), channel_id=1, source_target_pairs={{0,24},{4,28},{8,16},{12,20},{16,8},{20,12},{24,0},{28,4},{1,25},{... | collective-permute-start | bytes 491528 | tf_op jit(solution)/shard_map/ppermute | solution.py:358
  57.0 9.9 %collective-permute-start.15 = (f32[160,256]{1,0:T(8,128)S(1)}, f32[160,256]{1,0:T(8,128)S(1)}, u32[]{:S(2)}, u32[]{:S(2)}) collective-permute-start(f32[160,256]{1,0:T(8,128)S(1)} %add_add_fusion), channel_id=1, source_target_pairs={{0,24},{4,28},{8,16},{12,20},{16,8},{20,12},{24,0},{28,4},{1,25},{... | collective-permute-start | bytes 491528 | tf_op jit(solution)/shard_map/ppermute | solution.py:358
  63.6 8.3 %collective-permute-start = (bf16[256,2048]{1,0:T(8,128)(2,1)S(1)}, bf16[256,2048]{1,0:T(8,128)(2,1)}, u32[]{:S(2)}, u32[]{:S(2)}) collective-permute-start(bf16[256,2048]{1,0:T(8,128)(2,1)S(1)} %copy-done.1), channel_id=1, source_target_pairs={{0,1},{1,0},{2,3},{3,2},{4,5},{5,4},{6,7},{7,6},{8,9},{9,8},{10,11... | collective-permute-start | bytes 3145736 | tf_op jit(solution)/shard_map/ppermute | solution.py:356
  67.0 9.9 %collective-permute-start.16 = (bf16[256,2048]{1,0:T(8,128)(2,1)S(1)}, bf16[256,2048]{1,0:T(8,128)(2,1)}, u32[]{:S(2)}, u32[]{:S(2)}) collective-permute-start(bf16[256,2048]{1,0:T(8,128)(2,1)S(1)} %collective-permute-done.7.refs_2_), channel_id=1, source_target_pairs={{0,1},{1,0},{2,3},{3,2},{4,5},{5,4},{6,7},{7,6},{8,9},{9,8},{10,11... | collective-permute-start | bytes 3145736 | tf_op jit(solution)/shard_map/ppermute | solution.py:356
  67.1 8.0 %collective-permute-start.21 = (f32[160,256]{1,0:T(8,128)S(1)}, f32[160,256]{1,0:T(8,128)S(1)}, u32[]{:S(2)}, u32[]{:S(2)}) collective-permute-start(f32[160,256]{1,0:T(8,128)S(1)} %add.75.refs_0_), channel_id=1, source_target_pairs={{0,12},{4,8},{8,4},{12,0},{16,28},{20,24},{24,20},{28,16},{1,13},{... | collective-permute-start | bytes 491528 | tf_op jit(solution)/shard_map/ppermute | solution.py:358
  67.3 22.6 %collective-permute-start.19 = (f32[160,256]{1,0:T(8,128)S(1)}, f32[160,256]{1,0:T(8,128)S(1)}, u32[]{:S(2)}, u32[]{:S(2)}) collective-permute-start(f32[160,256]{1,0:T(8,128)S(1)} %add.75.refs_0_), channel_id=1, source_target_pairs={{0,8},{4,12},{8,0},{12,4},{16,24},{20,28},{24,16},{28,20},{1,9},{5... | collective-permute-start | bytes 491528 | tf_op jit(solution)/shard_map/ppermute | solution.py:358
  71.9 18.0 %collective-permute-start.17 = (f32[160,256]{1,0:T(8,128)S(1)}, f32[160,256]{1,0:T(8,128)S(1)}, u32[]{:S(2)}, u32[]{:S(2)}) collective-permute-start(f32[160,256]{1,0:T(8,128)S(1)} %add.75.refs_0_), channel_id=1, source_target_pairs={{0,4},{4,0},{8,12},{12,8},{16,20},{20,16},{24,28},{28,24},{1,5},{5... | collective-permute-start | bytes 491528 | tf_op jit(solution)/shard_map/ppermute | solution.py:358
  71.9 18.0 %collective-permute-start.22 = (f32[160,256]{1,0:T(8,128)S(1)}, f32[160,256]{1,0:T(8,128)S(1)}, u32[]{:S(2)}, u32[]{:S(2)}) collective-permute-start(f32[160,256]{1,0:T(8,128)S(1)} %add.79.refs_1_), channel_id=1, source_target_pairs={{0,12},{4,8},{8,4},{12,0},{16,28},{20,24},{24,20},{28,16},{1,13},{... | collective-permute-start | bytes 491528 | tf_op jit(solution)/shard_map/ppermute | solution.py:358
  75.1 14.8 %collective-permute-start.20 = (f32[160,256]{1,0:T(8,128)S(1)}, f32[160,256]{1,0:T(8,128)S(1)}, u32[]{:S(2)}, u32[]{:S(2)}) collective-permute-start(f32[160,256]{1,0:T(8,128)S(1)} %add.79.refs_1_), channel_id=1, source_target_pairs={{0,8},{4,12},{8,0},{12,4},{16,24},{20,28},{24,16},{28,20},{1,9},{5... | collective-permute-start | bytes 491528 | tf_op jit(solution)/shard_map/ppermute | solution.py:358
  76.8 13.1 %collective-permute-start.18 = (f32[160,256]{1,0:T(8,128)S(1)}, f32[160,256]{1,0:T(8,128)S(1)}, u32[]{:S(2)}, u32[]{:S(2)}) collective-permute-start(f32[160,256]{1,0:T(8,128)S(1)} %add.79.refs_1_), channel_id=1, source_target_pairs={{0,4},{4,0},{8,12},{12,8},{16,20},{20,16},{24,28},{28,24},{1,5},{5... | collective-permute-start | bytes 491528 | tf_op jit(solution)/shard_map/ppermute | solution.py:358
  96.0 5.1 %collective-permute-start.23 = (f32[8,128,256]{2,1,0:T(8,128)S(1)}, f32[8,128,256]{2,1,0:T(8,128)S(1)}, u32[]{:S(2)}, u32[]{:S(2)}) collective-permute-start(f32[8,128,256]{2,1,0:T(8,128)S(1)} %bitcast.40), channel_id=1, source_target_pairs={{0,1},{1,0},{2,3},{3,2},{4,5},{5,4},{6,7},{7,6},{8,9},{9,8},{10,11... | collective-permute-start | bytes 3145736 | tf_op jit(solution)/shard_map/ppermute | solution.py:356
  96.1 4.7 %collective-permute-start.31 = (f32[256,256]{1,0:T(8,128)S(1)}, f32[256,256]{1,0:T(8,128)S(1)}, u32[]{:S(2)}, u32[]{:S(2)}) collective-permute-start(f32[256,256]{1,0:T(8,128)S(1)} %shard_map.73), channel_id=1, source_target_pairs={{0,1},{1,0},{2,3},{3,2},{4,5},{5,4},{6,7},{7,6},{8,9},{9,8},{10,11... | collective-permute-start | bytes 786440 | tf_op jit(solution)/shard_map/ppermute | solution.py:356
  100.8 14.9 %collective-permute-start.32 = (f32[256,256]{1,0:T(8,128)S(1)}, f32[256,256]{1,0:T(8,128)S(1)}, u32[]{:S(2)}, u32[]{:S(2)}) collective-permute-start(f32[256,256]{1,0:T(8,128)S(1)} %add.84), channel_id=1, source_target_pairs={{0,2},{1,3},{2,0},{3,1},{4,6},{5,7},{6,4},{7,5},{8,10},{9,11},{10,... | collective-permute-start | bytes 786440 | tf_op jit(solution)/shard_map/ppermute | solution.py:356
  101.4 15.8 %collective-permute-start.30 = (f32[128,256]{1,0:T(8,128)S(1)}, f32[128,256]{1,0:T(8,128)S(1)}, u32[]{:S(2)}, u32[]{:S(2)}) collective-permute-start(f32[128,256]{1,0:T(8,128)S(1)} %get-tuple-element.135), channel_id=1, source_target_pairs={{0,14},{1,15},{2,12},{3,13},{4,10},{5,11},{6,8},{7,9},{8,6},{9,7},... | collective-permute-start | bytes 393224 | tf_op jit(solution)/shard_map/ppermute | solution.py:361
  104.1 13.6 %collective-permute-start.29 = (f32[128,256]{1,0:T(8,128)S(1)}, f32[128,256]{1,0:T(8,128)S(1)}, u32[]{:S(2)}, u32[]{:S(2)}) collective-permute-start(f32[128,256]{1,0:T(8,128)S(1)} %get-tuple-element.136), channel_id=1, source_target_pairs={{0,10},{1,11},{2,8},{3,9},{4,14},{5,15},{6,12},{7,13},{8,2},{9,3},... | collective-permute-start | bytes 393224 | tf_op jit(solution)/shard_map/ppermute | solution.py:361
  105.0 18.2 %collective-permute-start.28 = (f32[128,256]{1,0:T(8,128)S(1)}, f32[128,256]{1,0:T(8,128)S(1)}, u32[]{:S(2)}, u32[]{:S(2)}) collective-permute-start(f32[128,256]{1,0:T(8,128)S(1)} %get-tuple-element.137), channel_id=1, source_target_pairs={{0,6},{1,7},{2,4},{3,5},{4,2},{5,3},{6,0},{7,1},{8,14},{9,15},{10,... | collective-permute-start | bytes 393224 | tf_op jit(solution)/shard_map/ppermute | solution.py:361
  107.0 16.2 %collective-permute-start.27 = (f32[128,256]{1,0:T(8,128)S(1)}, f32[128,256]{1,0:T(8,128)S(1)}, u32[]{:S(2)}, u32[]{:S(2)}) collective-permute-start(f32[128,256]{1,0:T(8,128)S(1)} %get-tuple-element.138), channel_id=1, source_target_pairs={{0,2},{1,3},{2,0},{3,1},{4,6},{5,7},{6,4},{7,5},{8,10},{9,11},{10,... | collective-permute-start | bytes 393224 | tf_op jit(solution)/shard_map/ppermute | solution.py:356
  115.7 7.6 %collective-permute-start.26 = (f32[128,256]{1,0:T(8,128)S(1)}, f32[128,256]{1,0:T(8,128)S(1)}, u32[]{:S(2)}, u32[]{:S(2)}) collective-permute-start(f32[128,256]{1,0:T(8,128)S(1)} %get-tuple-element.139), channel_id=1, source_target_pairs={{0,12},{4,8},{8,4},{12,0},{16,28},{20,24},{24,20},{28,16},{1,13},{... | collective-permute-start | bytes 393224 | tf_op jit(solution)/shard_map/ppermute | solution.py:358
  117.1 6.1 %collective-permute-start.25 = (f32[128,256]{1,0:T(8,128)S(1)}, f32[128,256]{1,0:T(8,128)S(1)}, u32[]{:S(2)}, u32[]{:S(2)}) collective-permute-start(f32[128,256]{1,0:T(8,128)S(1)} %get-tuple-element.140), channel_id=1, source_target_pairs={{0,8},{4,12},{8,0},{12,4},{16,24},{20,28},{24,16},{28,20},{1,9},{5... | collective-permute-start | bytes 393224 | tf_op jit(solution)/shard_map/ppermute | solution.py:358
  117.7 5.9 %collective-permute-start.24 = (f32[128,256]{1,0:T(8,128)S(1)}, f32[128,256]{1,0:T(8,128)S(1)}, u32[]{:S(2)}, u32[]{:S(2)}) collective-permute-start(f32[128,256]{1,0:T(8,128)S(1)} %get-tuple-element.141), channel_id=1, source_target_pairs={{0,4},{4,0},{8,12},{12,8},{16,20},{20,16},{24,28},{28,24},{1,5},{5... | collective-permute-start | bytes 393224 | tf_op jit(solution)/shard_map/ppermute | solution.py:358
  123.7 7.7 %collective-permute-start.33 = (f32[128,256]{1,0:T(8,128)S(1)}, f32[128,256]{1,0:T(8,128)S(1)}, u32[]{:S(2)}, u32[]{:S(2)}) collective-permute-start(f32[128,256]{1,0:T(8,128)S(1)} %fusion.6), channel_id=1, source_target_pairs={{0,24},{4,28},{8,16},{12,20},{16,8},{20,12},{24,0},{28,4},{1,25},{... | collective-permute-start | bytes 393224 | tf_op jit(solution)/shard_map/ppermute | solution.py:358
  131.8 7.6 %collective-permute-start.40 = (bf16[144,256]{1,0:T(8,128)(2,1)S(1)}, bf16[144,256]{1,0:T(8,128)(2,1)S(1)}, u32[]{:S(2)}, u32[]{:S(2)}) collective-permute-start(bf16[144,256]{1,0:T(8,128)(2,1)S(1)} %get-tuple-element.122), channel_id=1, source_target_pairs={{0,14},{1,15},{2,12},{3,13},{4,10},{5,11},{6,8},{7,9},{8,6},{9,7},... | collective-permute-start | bytes 221192 | tf_op jit(solution)/shard_map/ppermute | solution.py:361
  134.6 6.0 %collective-permute-start.39 = (bf16[144,256]{1,0:T(8,128)(2,1)S(1)}, bf16[144,256]{1,0:T(8,128)(2,1)S(1)}, u32[]{:S(2)}, u32[]{:S(2)}) collective-permute-start(bf16[144,256]{1,0:T(8,128)(2,1)S(1)} %get-tuple-element.122), channel_id=1, source_target_pairs={{0,10},{1,11},{2,8},{3,9},{4,14},{5,15},{6,12},{7,13},{8,2},{9,3},... | collective-permute-start | bytes 221192 | tf_op jit(solution)/shard_map/ppermute | solution.py:361
  135.5 11.0 %collective-permute-start.36 = (f32[128,256]{1,0:T(8,128)S(1)}, f32[128,256]{1,0:T(8,128)S(1)}, u32[]{:S(2)}, u32[]{:S(2)}) collective-permute-start(f32[128,256]{1,0:T(8,128)S(1)} %get-tuple-element.119.refs_0_), channel_id=1, source_target_pairs={{0,12},{4,8},{8,4},{12,0},{16,28},{20,24},{24,20},{28,16},{1,13},{... | collective-permute-start | bytes 393224 | tf_op jit(solution)/shard_map/ppermute | solution.py:358
  137.1 9.3 %collective-permute-start.35 = (f32[128,256]{1,0:T(8,128)S(1)}, f32[128,256]{1,0:T(8,128)S(1)}, u32[]{:S(2)}, u32[]{:S(2)}) collective-permute-start(f32[128,256]{1,0:T(8,128)S(1)} %get-tuple-element.119.refs_0_), channel_id=1, source_target_pairs={{0,8},{4,12},{8,0},{12,4},{16,24},{20,28},{24,16},{28,20},{1,9},{5... | collective-permute-start | bytes 393224 | tf_op jit(solution)/shard_map/ppermute | solution.py:358
  138.0 8.5 %collective-permute-start.34 = (f32[128,256]{1,0:T(8,128)S(1)}, f32[128,256]{1,0:T(8,128)S(1)}, u32[]{:S(2)}, u32[]{:S(2)}) collective-permute-start(f32[128,256]{1,0:T(8,128)S(1)} %get-tuple-element.119.refs_0_), channel_id=1, source_target_pairs={{0,4},{4,0},{8,12},{12,8},{16,20},{20,16},{24,28},{28,24},{1,5},{5... | collective-permute-start | bytes 393224 | tf_op jit(solution)/shard_map/ppermute | solution.py:358
  139.4 7.0 %collective-permute-start.38 = (bf16[144,256]{1,0:T(8,128)(2,1)S(1)}, bf16[144,256]{1,0:T(8,128)(2,1)S(1)}, u32[]{:S(2)}, u32[]{:S(2)}) collective-permute-start(bf16[144,256]{1,0:T(8,128)(2,1)S(1)} %get-tuple-element.122), channel_id=1, source_target_pairs={{0,6},{1,7},{2,4},{3,5},{4,2},{5,3},{6,0},{7,1},{8,14},{9,15},{10,... | collective-permute-start | bytes 221192 | tf_op jit(solution)/shard_map/ppermute | solution.py:361
  140.6 5.8 %collective-permute-start.37 = (bf16[144,256]{1,0:T(8,128)(2,1)S(1)}, bf16[144,256]{1,0:T(8,128)(2,1)S(1)}, u32[]{:S(2)}, u32[]{:S(2)}) collective-permute-start(bf16[144,256]{1,0:T(8,128)(2,1)S(1)} %get-tuple-element.122), channel_id=1, source_target_pairs={{0,2},{1,3},{2,0},{3,1},{4,6},{5,7},{6,4},{7,5},{8,10},{9,11},{10,... | collective-permute-start | bytes 221192 | tf_op jit(solution)/shard_map/ppermute | solution.py:356
  147.1 2.0 %collective-permute-start.41 = (bf16[1040,256]{1,0:T(8,128)(2,1)S(1)}, bf16[1040,256]{1,0:T(8,128)(2,1)S(1)}, u32[]{:S(2)}, u32[]{:S(2)}) collective-permute-start(bf16[1040,256]{1,0:T(8,128)(2,1)S(1)} %get-tuple-element.131.side_ref), channel_id=1, source_target_pairs={{0,1},{1,0},{2,3},{3,2},{4,5},{5,4},{6,7},{7,6},{8,9},{9,8},{10,11... | collective-permute-start | bytes 1597448 | tf_op jit(solution)/shard_map/ppermute | solution.py:356
  (6 other events, 7.8 us)

commit v3 on v2

--- a/solution.py
+++ b/solution.py
@@ -14,8 +14,9 @@
 BLOCK = 32
 GROUP = 8
 VMEM = 20
-LARGE = 54
+LARGE = 52
 LEFT = 60
+BUFFER = 34
 LANES = 128
 
 
@@ -456,14 +457,15 @@
         grads[m + 1] = ex.swap(grads[m], tensor=1)
     lefts = list(sums)
     for m in quad:
-        lefts += [ex.swap(value, dp=m) for value in sums]
+        for h in range(SPLIT):
+            lefts.append(ex.swap(sums[h], dp=m))
     grads = [grads[m] for m in range(parts)]
 
     high, low = kernel_call(
         functools.partial(buffer_kernel, parts),
         (struct((rows, columns), BF16), struct((rows, columns), BF16)),
         2 * rows * tokens * columns, where, acts, momentum, *grads, grid=(steps,),
-        in_specs=[None, acts_spec, wide_spec] + [None] * parts, out_specs=(wide_spec, wide_spec), vmem=34,
+        in_specs=[None, acts_spec, wide_spec] + [None] * parts, out_specs=(wide_spec, wide_spec), vmem=BUFFER,
     )
 
     lefts[SPLIT:] = tied(lefts[SPLIT:], high)

time: 156 us -> 155 us (level)
  waiting for transfers between devices: 27.1 us -> 29.7 us
  local copies, waits for them, and re-layouts: 6.1 us -> 4.12 us
    ppermute x15, waiting for transfers between devices: 15.4 us -> 18 us  [swap(): return lax.ppermute(value, 'tensor', [(i, i ^ tensor) for i in range(n)])]
    unnamed x24 -> x20, local copies, waits for them, and re-layouts: 6.02 us -> 4.04 us
where the time goes in v3:
time: 155 us; the launch traced here: 154 us
  starting transfers between devices  59.4 us (38%)
  Pallas kernels  57.8 us (37%)
  waiting for transfers between devices  29.7 us (19%)
  local copies, waits for them, and re-layouts  4.12 us (3%)
  other arithmetic  2.48 us (2%)
    pallas_call x15, Pallas kernels, kernel_call(): pl.pallas_call(kernel, out_shape=out, grid_spec=pltpu.PrefetchScalarGridS...  57.8 us
    ppermute x21, starting transfers between devices, swap(): return lax.ppermute(value, 'dp', [(i, i ^ dp) for i in range(m)])  39.2 us
    ppermute x15, waiting for transfers between devices, swap(): return lax.ppermute(value, 'tensor', [(i, i ^ tensor) for i in range(n)])  18 us
    ppermute x21, waiting for transfers between devices, swap(): return lax.ppermute(value, 'dp', [(i, i ^ dp) for i in range(m)])  11.1 us
    ppermute x15, starting transfers between devices, swap(): return lax.ppermute(value, 'tensor', [(i, i ^ tensor) for i in range(n)])  10.2 us
    ppermute x6, starting transfers between devices, swap(): return lax.ppermute(value, ('dp', 'tensor'), perm)  9.98 us
    unnamed x20, local copies, waits for them, and re-layouts  4.04 us
  transfers between devices with their start and end apart: 42, of which 13 were waited for; matrix products, arithmetic and copies ran while one was open for 2% of the time, Pallas kernels for 28%

profile of v3, /device:TPU:0, one launch (start us, length us, event | category | flops | bytes accessed | tf_op | source)
XLA Modules:
  0.0 154.4 jit_solution(2790651534382453576)
XLA Ops:
  1.2 2.6 %collective-permute-start.1 = (f32[512,256]{1,0:T(8,128)}, f32[512,256]{1,0:T(8,128)S(1)}, u32[]{:S(2)}, u32[]{:S(2)}) collective-permute-start(f32[512,256]{1,0:T(8,128)} %refs_0_.2), channel_id=1, source_target_pairs={{0,2},{1,3},{2,0},{3,1},{4,6},{5,7},{6,4},{7,5},{8,10},{9,11},{10,... | collective-permute-start | bytes 1572872 | tf_op jit(solution)/shard_map/ppermute | solution.py:357
  3.9 1.2 copy-done
  6.2 1.2 shard_map.67
  7.4 5.5 %shard_map.68.refs_0_ = f32[1280,256]{1,0:T(8,128)} custom-call(s32[2]{0:T(128)S(1)} %pad_add_fusion.1.where_ref, f32[1280,2048]{1,0:T(8,128)} %momentum_ref.5, bf16[1024,512]{1,0:T(8,128)(2,1)S(1)} %get-tuple-element.69.pair_ref), custom_call_target="tpu_custom_call" | custom-call | flops 2013265920 | bytes 12845064 | tf_op jit(solution)/shard_map/pallas_call | solution.py:126
  12.9 3.6 %collective-permute-done.1.refs_0_ = f32[512,256]{1,0:T(8,128)S(1)} collective-permute-done((f32[512,256]{1,0:T(8,128)}, f32[512,256]{1,0:T(8,128)S(1)}, u32[]{:S(2)}, u32[]{:S(2)}) %collective-permute-start.1) | collective-permute-done | bytes 524320 | tf_op jit(solution)/shard_map/ppermute | solution.py:357
  16.5 1.9 %collective-permute-done.3.refs_1_ = f32[512,256]{1,0:T(8,128)S(1)} collective-permute-done((f32[512,256]{1,0:T(8,128)S(1)}, f32[512,256]{1,0:T(8,128)S(1)}, u32[]{:S(2)}, u32[]{:S(2)}) %collective-permute-start.3) | collective-permute-done | bytes 524320 | tf_op jit(solution)/shard_map/ppermute | solution.py:357
  18.4 1.2 shard_map.69
  19.6 1.8 %collective-permute-start.5 = (f32[256,256]{1,0:T(8,128)S(1)}, f32[256,256]{1,0:T(8,128)S(1)}, u32[]{:S(2)}, u32[]{:S(2)}) collective-permute-start(f32[256,256]{1,0:T(8,128)S(1)} %get-tuple-element.72.refs_0_), channel_id=1, source_target_pairs={{0,2},{1,3},{2,0},{3,1},{4,6},{5,7},{6,4},{7,5},{8,10},{9,11},{10,... | collective-permute-start | bytes 786440 | tf_op jit(solution)/shard_map/ppermute | solution.py:357
  21.4 5.6 %shard_map.70.base_ref = f32[1280,256]{1,0:T(8,128)} custom-call(s32[2]{0:T(128)S(1)} %pad_add_fusion.1.where_ref, f32[1280,2048]{1,0:T(8,128)} %momentum_ref.5, bf16[1024,512]{1,0:T(8,128)(2,1)S(1)} %get-tuple-element.73.pair_ref, f32[1280,256]{1,0:T(8,128)} %shard_map.68.refs_0_), custom_call_target="tpu_custom_call" | custom-call | flops 2013265920 | bytes 14155784 | tf_op jit(solution)/shard_map/pallas_call | solution.py:126
  28.1 1.5 collective-permute-done.6.refs_3_
  29.6 1.7 %collective-permute-start.7 = (bf16[256,2048]{1,0:T(8,128)(2,1)S(1)}, bf16[256,2048]{1,0:T(8,128)(2,1)S(1)}, u32[]{:S(2)}, u32[]{:S(2)}) collective-permute-start(bf16[256,2048]{1,0:T(8,128)(2,1)S(1)} %copy-done.1), channel_id=1, source_target_pairs={{0,2},{1,3},{2,0},{3,1},{4,6},{5,7},{6,4},{7,5},{8,10},{9,11},{10,... | collective-permute-start | bytes 3145736 | tf_op jit(solution)/shard_map/ppermute | solution.py:357
  31.3 5.2 %shard_map.71 = (f32[160,256]{1,0:T(8,128)}, f32[160,256]{1,0:T(8,128)}, f32[160,256]{1,0:T(8,128)}, f32[160,256]{1,0:T(8,128)}, f32[160,256]{1,0:T(8,128)}, /*i...) custom-call(s32[2]{0:T(128)} %copy-done.5, bf16[1024,1280]{1,0:T(8,128)(2,1)} %acts_ref.3, ...), custom_call_target="tpu_custom_call" | custom-call | flops 1342177280 | bytes 6291464 | tf_op jit(solution)/shard_map/pallas_call | solution.py:126
  36.5 1.5 collective-permute-start.8
  38.1 1.6 %collective-permute-start.9 = (f32[160,256]{1,0:T(8,128)}, f32[160,256]{1,0:T(8,128)S(1)}, u32[]{:S(2)}, u32[]{:S(2)}) collective-permute-start(f32[160,256]{1,0:T(8,128)} %get-tuple-element.78), channel_id=1, source_target_pairs={{0,8},{4,12},{8,0},{12,4},{16,24},{20,28},{24,16},{28,20},{1,9},{5... | collective-permute-start | bytes 491528 | tf_op jit(solution)/shard_map/ppermute | solution.py:359
  40.0 1.5 collective-permute-start.12
  41.5 3.0 %collective-permute-done.8 = f32[160,256]{1,0:T(8,128)S(1)} collective-permute-done((f32[160,256]{1,0:T(8,128)}, f32[160,256]{1,0:T(8,128)S(1)}, u32[]{:S(2)}, u32[]{:S(2)}) %collective-permute-start.8) | collective-permute-done | bytes 163872 | tf_op jit(solution)/shard_map/ppermute | solution.py:359
  44.5 1.7 %collective-permute-start.13 = (f32[160,256]{1,0:T(8,128)}, f32[160,256]{1,0:T(8,128)S(1)}, u32[]{:S(2)}, u32[]{:S(2)}) collective-permute-start(f32[160,256]{1,0:T(8,128)} %get-tuple-element.85), channel_id=1, source_target_pairs={{0,8},{4,12},{8,0},{12,4},{16,24},{20,28},{24,16},{28,20},{1,9},{5... | collective-permute-start | bytes 491528 | tf_op jit(solution)/shard_map/ppermute | solution.py:359
  46.2 1.4 collective-permute-start.14
  47.6 1.1 collective-permute-done.10
  49.7 3.8 %collective-permute-start.11 = (f32[160,256]{1,0:T(8,128)S(1)}, f32[160,256]{1,0:T(8,128)S(1)}, u32[]{:S(2)}, u32[]{:S(2)}) collective-permute-start(f32[160,256]{1,0:T(8,128)S(1)} %add_add_fusion.1), channel_id=1, source_target_pairs={{0,24},{4,28},{8,16},{12,20},{16,8},{20,12},{24,0},{28,4},{1,25},{... | collective-permute-start | bytes 491528 | tf_op jit(solution)/shard_map/ppermute | solution.py:359
  53.4 1.6 %collective-permute-done.14 = f32[160,256]{1,0:T(8,128)S(1)} collective-permute-done((f32[160,256]{1,0:T(8,128)}, f32[160,256]{1,0:T(8,128)S(1)}, u32[]{:S(2)}, u32[]{:S(2)}) %collective-permute-start.14) | collective-permute-done | bytes 163872 | tf_op jit(solution)/shard_map/ppermute | solution.py:359
  56.0 6.5 %collective-permute-start.15 = (f32[160,256]{1,0:T(8,128)S(1)}, f32[160,256]{1,0:T(8,128)S(1)}, u32[]{:S(2)}, u32[]{:S(2)}) collective-permute-start(f32[160,256]{1,0:T(8,128)S(1)} %add_add_fusion), channel_id=1, source_target_pairs={{0,24},{4,28},{8,16},{12,20},{16,8},{20,12},{24,0},{28,4},{1,25},{... | collective-permute-start | bytes 491528 | tf_op jit(solution)/shard_map/ppermute | solution.py:359
  62.6 3.4 %collective-permute-done.15 = f32[160,256]{1,0:T(8,128)S(1)} collective-permute-done((f32[160,256]{1,0:T(8,128)S(1)}, f32[160,256]{1,0:T(8,128)S(1)}, u32[]{:S(2)}, u32[]{:S(2)}) %collective-permute-start.15) | collective-permute-done | bytes 163872 | tf_op jit(solution)/shard_map/ppermute | solution.py:359
  66.3 4.5 %collective-permute-start.19 = (f32[160,256]{1,0:T(8,128)S(1)}, f32[160,256]{1,0:T(8,128)S(1)}, u32[]{:S(2)}, u32[]{:S(2)}) collective-permute-start(f32[160,256]{1,0:T(8,128)S(1)} %add.75.refs_0_), channel_id=1, source_target_pairs={{0,8},{4,12},{8,0},{12,4},{16,24},{20,28},{24,16},{28,20},{1,9},{5... | collective-permute-start | bytes 491528 | tf_op jit(solution)/shard_map/ppermute | solution.py:359
  70.9 1.5 collective-permute-start.22
  72.4 1.7 %collective-permute-done.21.refs_6_ = f32[160,256]{1,0:T(8,128)S(1)} collective-permute-done((f32[160,256]{1,0:T(8,128)S(1)}, f32[160,256]{1,0:T(8,128)S(1)}, u32[]{:S(2)}, u32[]{:S(2)}) %collective-permute-start.21) | collective-permute-done | bytes 163872 | tf_op jit(solution)/shard_map/ppermute | solution.py:359
  74.1 1.7 %collective-permute-start.20 = (f32[160,256]{1,0:T(8,128)S(1)}, f32[160,256]{1,0:T(8,128)S(1)}, u32[]{:S(2)}, u32[]{:S(2)}) collective-permute-start(f32[160,256]{1,0:T(8,128)S(1)} %add.79.refs_1_), channel_id=1, source_target_pairs={{0,8},{4,12},{8,0},{12,4},{16,24},{20,28},{24,16},{28,20},{1,9},{5... | collective-permute-start | bytes 491528 | tf_op jit(solution)/shard_map/ppermute | solution.py:359
  75.9 1.5 collective-permute-start.18
  77.4 1.7 %copy-done.2 = bf16[1024,1280]{1,0:T(8,128)(2,1)S(1)} copy-done((bf16[1024,1280]{1,0:T(8,128)(2,1)S(1)}, bf16[1024,1280]{1,0:T(8,128)(2,1)}, u32[]{:S(2)}) %copy-start.2) | copy-done | bytes 2621464
  79.1 9.8 %shard_map.72 = (bf16[1280,2048]{1,0:T(8,128)(2,1)S(1)}, bf16[1280,2048]{1,0:T(8,128)(2,1)S(1)}) custom-call(s32[2]{0:T(128)S(1)} %copy-done.6, bf16[1024,1280]{1,0:T(8,128)(2,1)S(1)} %copy-done.2, f32[1280,2048]{1,0:T(8,128)} %momentum_ref.5, bf16[256,2048]{1,0:T(8,128)(2,1)S(1)} %copy-done.1, bf16[256,2048]{1,0:T(8,128)(2,1)} %collective-permute-done.refs_1_, ...), custom_call_target="tpu_custom_call" | custom-call | flops 5368709120 | bytes 27787272 | tf_op jit(solution)/shard_map/pallas_call | solution.py:126
  88.9 2.0 %shard_map.73 = f32[256,256]{1,0:T(8,128)S(1)} custom-call(f32[160,256]{1,0:T(8,128)S(1)} %add.75.refs_0_, f32[160,256]{1,0:T(8,128)S(1)} %add.79.refs_1_, f32[160,256]{1,0:T(8,128)S(1)} %collective-permute-done.17.refs_2_, f32[160,256]{1,0:T(8,128)S(1)} %collective-permute-done.18.refs_3_, f32[160,256]{1,0:T(8,128)S(1)} %collective-permute-done.19.refs_4_, ...), custom_call_target="tpu_custom_call" | custom-call | flops 1006632960 | bytes 1572864 | tf_op jit(solution)/shard_map/pallas_call | solution.py:126
  91.0 4.0 %shard_map.75 = f32[2,1,512,256]{3,2,1,0:T(8,128)S(1)} custom-call(s32[3]{0:T(128)S(1)} %get-tuple-element.143.where_ref, bf16[1280,2048]{1,0:T(8,128)(2,1)S(1)} %get-tuple-element.92.high_ref, bf16[1280,2048]{1,0:T(8,128)(2,1)S(1)} %get-tuple-element.93.low_ref, f32[160,256]{1,0:T(8,128)S(1)} %add.75.refs_0_, f32[160,256]{1,0:T(8,128)S(1)} %add.79.refs_1_, ...), custom_call_target="tpu_custom_call" | custom-call | flops 2013265920 | bytes 12845068 | tf_op jit(solution)/shard_map/pallas_call | solution.py:126
  95.6 4.2 %shard_map.74 = f32[2,1,512,256]{3,2,1,0:T(8,128)S(1)} custom-call(s32[3]{0:T(128)S(1)} %get-tuple-element.142.where_ref, bf16[1280,2048]{1,0:T(8,128)(2,1)S(1)} %get-tuple-element.92.high_ref, bf16[1280,2048]{1,0:T(8,128)(2,1)S(1)} %get-tuple-element.93.low_ref, f32[160,256]{1,0:T(8,128)S(1)} %add.75.refs_0_, f32[160,256]{1,0:T(8,128)S(1)} %add.79.refs_1_, ...), custom_call_target="tpu_custom_call" | custom-call | flops 2013265920 | bytes 12845068 | tf_op jit(solution)/shard_map/pallas_call | solution.py:126
  100.4 2.8 %collective-permute-start.30 = (f32[128,256]{1,0:T(8,128)S(1)}, f32[128,256]{1,0:T(8,128)S(1)}, u32[]{:S(2)}, u32[]{:S(2)}) collective-permute-start(f32[128,256]{1,0:T(8,128)S(1)} %get-tuple-element.135), channel_id=1, source_target_pairs={{0,14},{1,15},{2,12},{3,13},{4,10},{5,11},{6,8},{7,9},{8,6},{9,7},... | collective-permute-start | bytes 393224 | tf_op jit(solution)/shard_map/ppermute | solution.py:362
  104.1 2.0 %collective-permute-start.28 = (f32[128,256]{1,0:T(8,128)S(1)}, f32[128,256]{1,0:T(8,128)S(1)}, u32[]{:S(2)}, u32[]{:S(2)}) collective-permute-start(f32[128,256]{1,0:T(8,128)S(1)} %get-tuple-element.137), channel_id=1, source_target_pairs={{0,6},{1,7},{2,4},{3,5},{4,2},{5,3},{6,0},{7,1},{8,14},{9,15},{10,... | collective-permute-start | bytes 393224 | tf_op jit(solution)/shard_map/ppermute | solution.py:362
  106.6 8.1 %collective-permute-done.32 = f32[256,256]{1,0:T(8,128)S(1)} collective-permute-done((f32[256,256]{1,0:T(8,128)S(1)}, f32[256,256]{1,0:T(8,128)S(1)}, u32[]{:S(2)}, u32[]{:S(2)}) %collective-permute-start.32) | collective-permute-done | bytes 262176 | tf_op jit(solution)/shard_map/ppermute | solution.py:357
  114.7 1.5 collective-permute-start.26
  116.7 1.6 %collective-permute-start.24 = (f32[128,256]{1,0:T(8,128)S(1)}, f32[128,256]{1,0:T(8,128)S(1)}, u32[]{:S(2)}, u32[]{:S(2)}) collective-permute-start(f32[128,256]{1,0:T(8,128)S(1)} %get-tuple-element.141), channel_id=1, source_target_pairs={{0,4},{4,0},{8,12},{12,8},{16,20},{20,16},{24,28},{28,24},{1,5},{5... | collective-permute-start | bytes 393224 | tf_op jit(solution)/shard_map/ppermute | solution.py:359
  118.3 4.0 %shard_map.76.gram_ref = f32[256,256]{1,0:T(8,128)S(1)} custom-call(f32[256,256]{1,0:T(8,128)S(1)} %add.85.gram_ref), custom_call_target="tpu_custom_call" | custom-call | flops 2000000000 | bytes 524288 | tf_op jit(solution)/shard_map/pallas_call | solution.py:126
  122.7 3.9 %collective-permute-start.33 = (f32[128,256]{1,0:T(8,128)S(1)}, f32[128,256]{1,0:T(8,128)S(1)}, u32[]{:S(2)}, u32[]{:S(2)}) collective-permute-start(f32[128,256]{1,0:T(8,128)S(1)} %fusion.6), channel_id=1, source_target_pairs={{0,24},{4,28},{8,16},{12,20},{16,8},{20,12},{24,0},{28,4},{1,25},{... | collective-permute-start | bytes 393224 | tf_op jit(solution)/shard_map/ppermute | solution.py:359
  126.6 3.8 %shard_map.77.inverse_ref = f32[256,256]{1,0:T(8,128)S(1)} custom-call(f32[256,256]{1,0:T(8,128)S(1)} %shard_map.76.gram_ref), custom_call_target="tpu_custom_call" | custom-call | flops 2000000000 | bytes 524288 | tf_op jit(solution)/shard_map/pallas_call | solution.py:126
  130.8 2.8 %collective-permute-start.40 = (bf16[144,256]{1,0:T(8,128)(2,1)S(1)}, bf16[144,256]{1,0:T(8,128)(2,1)S(1)}, u32[]{:S(2)}, u32[]{:S(2)}) collective-permute-start(bf16[144,256]{1,0:T(8,128)(2,1)S(1)} %get-tuple-element.122), channel_id=1, source_target_pairs={{0,14},{1,15},{2,12},{3,13},{4,10},{5,11},{6,8},{7,9},{8,6},{9,7},... | collective-permute-start | bytes 221192 | tf_op jit(solution)/shard_map/ppermute | solution.py:362
  134.5 1.6 %collective-permute-start.36 = (f32[128,256]{1,0:T(8,128)S(1)}, f32[128,256]{1,0:T(8,128)S(1)}, u32[]{:S(2)}, u32[]{:S(2)}) collective-permute-start(f32[128,256]{1,0:T(8,128)S(1)} %get-tuple-element.119.refs_0_), channel_id=1, source_target_pairs={{0,12},{4,8},{8,4},{12,0},{16,28},{20,24},{24,20},{28,16},{1,13},{... | collective-permute-start | bytes 393224 | tf_op jit(solution)/shard_map/ppermute | solution.py:359
  137.0 1.5 collective-permute-start.34
  139.6 1.9 %collective-permute-start.37 = (bf16[144,256]{1,0:T(8,128)(2,1)S(1)}, bf16[144,256]{1,0:T(8,128)(2,1)S(1)}, u32[]{:S(2)}, u32[]{:S(2)}) collective-permute-start(bf16[144,256]{1,0:T(8,128)(2,1)S(1)} %get-tuple-element.122), channel_id=1, source_target_pairs={{0,2},{1,3},{2,0},{3,1},{4,6},{5,7},{6,4},{7,5},{8,10},{9,11},{10,... | collective-permute-start | bytes 221192 | tf_op jit(solution)/shard_map/ppermute | solution.py:357
  141.6 3.9 %shard_map.79 = (f32[1280,256]{1,0:T(8,128)}, bf16[1280,256]{1,0:T(8,128)(2,1)S(1)}) custom-call(s32[2]{0:T(128)S(1)} %copy-done.6, f32[256,256]{1,0:T(8,128)S(1)} %shard_map.77.inverse_ref, f32[160,256]{1,0:T(8,128)S(1)} %add.75.refs_0_, f32[160,256]{1,0:T(8,128)S(1)} %add.79.refs_1_, f32[160,256]{1,0:T(8,128)S(1)} %collective-permute-done.17.refs_2_, ...), custom_call_target="tpu_custom_call" | custom-call | flops 1006632960 | bytes 3538952 | tf_op jit(solution)/shard_map/pallas_call | solution.py:126
  146.2 1.9 %collective-permute-done.41.other_ref = bf16[1040,256]{1,0:T(8,128)(2,1)S(1)} collective-permute-done((bf16[1040,256]{1,0:T(8,128)(2,1)S(1)}, bf16[1040,256]{1,0:T(8,128)(2,1)S(1)}, u32[]{:S(2)}, u32[]{:S(2)}) %collective-permute-start.41) | collective-permute-done | bytes 532512 | tf_op jit(solution)/shard_map/ppermute | solution.py:357
  148.1 6.3 %shard_map.81 = (f32[1280,2048]{1,0:T(8,128)}, f32[512,256]{1,0:T(8,128)}) custom-call(s32[2]{0:T(128)S(1)} %copy-done.6, bf16[1280,2048]{1,0:T(8,128)(2,1)S(1)} %get-tuple-element.92.high_ref, bf16[1280,2048]{1,0:T(8,128)(2,1)S(1)} %get-tuple-element.93.low_ref, bf16[1280,256]{1,0:T(8,128)(2,1)S(1)} %get-tuple-element.121.ortho_ref, ...), custom_call_target="tpu_custom_call" | custom-call | flops 1342177280 | bytes 23740424 | tf_op jit(solution)/shard_map/pallas_call | solution.py:126
  (84 shorter events, 13.1 us)
Async XLA Ops:
  0.6 3.3 %collective-permute-start.2 = (f32[512,256]{1,0:T(8,128)}, f32[512,256]{1,0:T(8,128)S(1)}, u32[]{:S(2)}, u32[]{:S(2)}) collective-permute-start(f32[512,256]{1,0:T(8,128)} %refs_0_.2), channel_id=1, source_target_pairs={{0,1},{1,0},{2,3},{3,2},{4,5},{5,4},{6,7},{7,6},{8,9},{9,8},{10,11... | collective-permute-start | bytes 1572872 | tf_op jit(solution)/shard_map/ppermute | solution.py:357
  1.2 15.3 %collective-permute-start.1 = (f32[512,256]{1,0:T(8,128)}, f32[512,256]{1,0:T(8,128)S(1)}, u32[]{:S(2)}, u32[]{:S(2)}) collective-permute-start(f32[512,256]{1,0:T(8,128)} %refs_0_.2), channel_id=1, source_target_pairs={{0,2},{1,3},{2,0},{3,1},{4,6},{5,7},{6,4},{7,5},{8,10},{9,11},{10,... | collective-permute-start | bytes 1572872 | tf_op jit(solution)/shard_map/ppermute | solution.py:357
  3.8 14.6 %copy-start.5 = (s32[2]{0:T(128)}, s32[2]{0:T(128)S(1)}, u32[]{:S(2)}) copy-start(s32[2]{0:T(128)S(1)} %pad_add_fusion.where_ref) | copy-start | bytes 28
  7.4 11.0 %copy-start.1 = (bf16[256,2048]{1,0:T(8,128)(2,1)S(1)}, bf16[256,2048]{1,0:T(8,128)(2,1)}, u32[]{:S(2)}) copy-start(bf16[256,2048]{1,0:T(8,128)(2,1)} %refs_0_.3) | copy-start | bytes 3145732
  16.5 1.9 %collective-permute-start.3 = (f32[512,256]{1,0:T(8,128)S(1)}, f32[512,256]{1,0:T(8,128)S(1)}, u32[]{:S(2)}, u32[]{:S(2)}) collective-permute-start(f32[512,256]{1,0:T(8,128)S(1)} %collective-permute-done.1.refs_0_), channel_id=1, source_target_pairs={{0,1},{1,0},{2,3},{3,2},{4,5},{5,4},{6,7},{7,6},{8,9},{9,8},{10,11... | collective-permute-start | bytes 1572872 | tf_op jit(solution)/shard_map/ppermute | solution.py:357
  19.6 7.5 %copy-start.4 = (f32[256,256]{1,0:T(8,128)}, f32[256,256]{1,0:T(8,128)S(1)}, u32[]{:S(2)}) copy-start(f32[256,256]{1,0:T(8,128)S(1)} %get-tuple-element.72.refs_0_) | copy-start | bytes 786436
  19.6 8.4 %collective-permute-start.5 = (f32[256,256]{1,0:T(8,128)S(1)}, f32[256,256]{1,0:T(8,128)S(1)}, u32[]{:S(2)}, u32[]{:S(2)}) collective-permute-start(f32[256,256]{1,0:T(8,128)S(1)} %get-tuple-element.72.refs_0_), channel_id=1, source_target_pairs={{0,2},{1,3},{2,0},{3,1},{4,6},{5,7},{6,4},{7,5},{8,10},{9,11},{10,... | collective-permute-start | bytes 786440 | tf_op jit(solution)/shard_map/ppermute | solution.py:357
  21.4 6.6 %collective-permute-start.4 = (f32[256,256]{1,0:T(8,128)S(1)}, f32[256,256]{1,0:T(8,128)S(1)}, u32[]{:S(2)}, u32[]{:S(2)}) collective-permute-start(f32[256,256]{1,0:T(8,128)S(1)} %get-tuple-element.72.refs_0_), channel_id=1, source_target_pairs={{0,1},{1,0},{2,3},{3,2},{4,5},{5,4},{6,7},{7,6},{8,9},{9,8},{10,11... | collective-permute-start | bytes 786440 | tf_op jit(solution)/shard_map/ppermute | solution.py:357
  27.1 50.3 %copy-start.6 = (s32[2]{0:T(128)S(1)}, s32[2]{0:T(128)}, u32[]{:S(2)}) copy-start(s32[2]{0:T(128)} %copy-done.5) | copy-start | bytes 28
  28.0 3.3 %copy-start.7 = (f32[256,256]{1,0:T(8,128)}, f32[256,256]{1,0:T(8,128)S(1)}, u32[]{:S(2)}) copy-start(f32[256,256]{1,0:T(8,128)S(1)} %collective-permute-done.5.refs_2_) | copy-start | bytes 786436
  28.0 1.5 collective-permute-start.6
  28.1 3.3 %copy-start.8 = (f32[256,256]{1,0:T(8,128)}, f32[256,256]{1,0:T(8,128)S(1)}, u32[]{:S(2)}) copy-start(f32[256,256]{1,0:T(8,128)S(1)} %collective-permute-done.4.refs_1_) | copy-start | bytes 786436
  29.6 36.4 %collective-permute-start.7 = (bf16[256,2048]{1,0:T(8,128)(2,1)S(1)}, bf16[256,2048]{1,0:T(8,128)(2,1)S(1)}, u32[]{:S(2)}, u32[]{:S(2)}) collective-permute-start(bf16[256,2048]{1,0:T(8,128)(2,1)S(1)} %copy-done.1), channel_id=1, source_target_pairs={{0,2},{1,3},{2,0},{3,1},{4,6},{5,7},{6,4},{7,5},{8,10},{9,11},{10,... | collective-permute-start | bytes 3145736 | tf_op jit(solution)/shard_map/ppermute | solution.py:357
  36.5 8.0 %collective-permute-start.8 = (f32[160,256]{1,0:T(8,128)}, f32[160,256]{1,0:T(8,128)S(1)}, u32[]{:S(2)}, u32[]{:S(2)}) collective-permute-start(f32[160,256]{1,0:T(8,128)} %get-tuple-element.77), channel_id=1, source_target_pairs={{0,4},{4,0},{8,12},{12,8},{16,20},{20,16},{24,28},{28,24},{1,5},{5... | collective-permute-start | bytes 491528 | tf_op jit(solution)/shard_map/ppermute | solution.py:359
  38.1 8.2 %collective-permute-start.9 = (f32[160,256]{1,0:T(8,128)}, f32[160,256]{1,0:T(8,128)S(1)}, u32[]{:S(2)}, u32[]{:S(2)}) collective-permute-start(f32[160,256]{1,0:T(8,128)} %get-tuple-element.78), channel_id=1, source_target_pairs={{0,8},{4,12},{8,0},{12,4},{16,24},{20,28},{24,16},{28,20},{1,9},{5... | collective-permute-start | bytes 491528 | tf_op jit(solution)/shard_map/ppermute | solution.py:359
  39.6 9.1 %collective-permute-start.10 = (f32[160,256]{1,0:T(8,128)}, f32[160,256]{1,0:T(8,128)S(1)}, u32[]{:S(2)}, u32[]{:S(2)}) collective-permute-start(f32[160,256]{1,0:T(8,128)} %get-tuple-element.79), channel_id=1, source_target_pairs={{0,12},{4,8},{8,4},{12,0},{16,28},{20,24},{24,20},{28,16},{1,13},{... | collective-permute-start | bytes 491528 | tf_op jit(solution)/shard_map/ppermute | solution.py:359
  40.0 13.4 %collective-permute-start.12 = (f32[160,256]{1,0:T(8,128)}, f32[160,256]{1,0:T(8,128)S(1)}, u32[]{:S(2)}, u32[]{:S(2)}) collective-permute-start(f32[160,256]{1,0:T(8,128)} %get-tuple-element.84), channel_id=1, source_target_pairs={{0,4},{4,0},{8,12},{12,8},{16,20},{20,16},{24,28},{28,24},{1,5},{5... | collective-permute-start | bytes 491528 | tf_op jit(solution)/shard_map/ppermute | solution.py:359
  44.5 8.9 %collective-permute-start.13 = (f32[160,256]{1,0:T(8,128)}, f32[160,256]{1,0:T(8,128)S(1)}, u32[]{:S(2)}, u32[]{:S(2)}) collective-permute-start(f32[160,256]{1,0:T(8,128)} %get-tuple-element.85), channel_id=1, source_target_pairs={{0,8},{4,12},{8,0},{12,4},{16,24},{20,28},{24,16},{28,20},{1,9},{5... | collective-permute-start | bytes 491528 | tf_op jit(solution)/shard_map/ppermute | solution.py:359
  46.2 8.9 %collective-permute-start.14 = (f32[160,256]{1,0:T(8,128)}, f32[160,256]{1,0:T(8,128)S(1)}, u32[]{:S(2)}, u32[]{:S(2)}) collective-permute-start(f32[160,256]{1,0:T(8,128)} %get-tuple-element.86), channel_id=1, source_target_pairs={{0,12},{4,8},{8,4},{12,0},{16,28},{20,24},{24,20},{28,16},{1,13},{... | collective-permute-start | bytes 491528 | tf_op jit(solution)/shard_map/ppermute | solution.py:359
  49.7 12.9 %collective-permute-start.11 = (f32[160,256]{1,0:T(8,128)S(1)}, f32[160,256]{1,0:T(8,128)S(1)}, u32[]{:S(2)}, u32[]{:S(2)}) collective-permute-start(f32[160,256]{1,0:T(8,128)S(1)} %add_add_fusion.1), channel_id=1, source_target_pairs={{0,24},{4,28},{8,16},{12,20},{16,8},{20,12},{24,0},{28,4},{1,25},{... | collective-permute-start | bytes 491528 | tf_op jit(solution)/shard_map/ppermute | solution.py:359
  56.0 9.9 %collective-permute-start.15 = (f32[160,256]{1,0:T(8,128)S(1)}, f32[160,256]{1,0:T(8,128)S(1)}, u32[]{:S(2)}, u32[]{:S(2)}) collective-permute-start(f32[160,256]{1,0:T(8,128)S(1)} %add_add_fusion), channel_id=1, source_target_pairs={{0,24},{4,28},{8,16},{12,20},{16,8},{20,12},{24,0},{28,4},{1,25},{... | collective-permute-start | bytes 491528 | tf_op jit(solution)/shard_map/ppermute | solution.py:359
  62.6 8.3 %collective-permute-start = (bf16[256,2048]{1,0:T(8,128)(2,1)S(1)}, bf16[256,2048]{1,0:T(8,128)(2,1)}, u32[]{:S(2)}, u32[]{:S(2)}) collective-permute-start(bf16[256,2048]{1,0:T(8,128)(2,1)S(1)} %copy-done.1), channel_id=1, source_target_pairs={{0,1},{1,0},{2,3},{3,2},{4,5},{5,4},{6,7},{7,6},{8,9},{9,8},{10,11... | collective-permute-start | bytes 3145736 | tf_op jit(solution)/shard_map/ppermute | solution.py:357
  66.0 9.8 %collective-permute-start.16 = (bf16[256,2048]{1,0:T(8,128)(2,1)S(1)}, bf16[256,2048]{1,0:T(8,128)(2,1)}, u32[]{:S(2)}, u32[]{:S(2)}) collective-permute-start(bf16[256,2048]{1,0:T(8,128)(2,1)S(1)} %collective-permute-done.7.refs_2_), channel_id=1, source_target_pairs={{0,1},{1,0},{2,3},{3,2},{4,5},{5,4},{6,7},{7,6},{8,9},{9,8},{10,11... | collective-permute-start | bytes 3145736 | tf_op jit(solution)/shard_map/ppermute | solution.py:357
  66.1 8.0 %collective-permute-start.21 = (f32[160,256]{1,0:T(8,128)S(1)}, f32[160,256]{1,0:T(8,128)S(1)}, u32[]{:S(2)}, u32[]{:S(2)}) collective-permute-start(f32[160,256]{1,0:T(8,128)S(1)} %add.75.refs_0_), channel_id=1, source_target_pairs={{0,12},{4,8},{8,4},{12,0},{16,28},{20,24},{24,20},{28,16},{1,13},{... | collective-permute-start | bytes 491528 | tf_op jit(solution)/shard_map/ppermute | solution.py:359
  66.3 22.6 %collective-permute-start.19 = (f32[160,256]{1,0:T(8,128)S(1)}, f32[160,256]{1,0:T(8,128)S(1)}, u32[]{:S(2)}, u32[]{:S(2)}) collective-permute-start(f32[160,256]{1,0:T(8,128)S(1)} %add.75.refs_0_), channel_id=1, source_target_pairs={{0,8},{4,12},{8,0},{12,4},{16,24},{20,28},{24,16},{28,20},{1,9},{5... | collective-permute-start | bytes 491528 | tf_op jit(solution)/shard_map/ppermute | solution.py:359
  70.9 18.0 %collective-permute-start.17 = (f32[160,256]{1,0:T(8,128)S(1)}, f32[160,256]{1,0:T(8,128)S(1)}, u32[]{:S(2)}, u32[]{:S(2)}) collective-permute-start(f32[160,256]{1,0:T(8,128)S(1)} %add.75.refs_0_), channel_id=1, source_target_pairs={{0,4},{4,0},{8,12},{12,8},{16,20},{20,16},{24,28},{28,24},{1,5},{5... | collective-permute-start | bytes 491528 | tf_op jit(solution)/shard_map/ppermute | solution.py:359
  70.9 18.0 %collective-permute-start.22 = (f32[160,256]{1,0:T(8,128)S(1)}, f32[160,256]{1,0:T(8,128)S(1)}, u32[]{:S(2)}, u32[]{:S(2)}) collective-permute-start(f32[160,256]{1,0:T(8,128)S(1)} %add.79.refs_1_), channel_id=1, source_target_pairs={{0,12},{4,8},{8,4},{12,0},{16,28},{20,24},{24,20},{28,16},{1,13},{... | collective-permute-start | bytes 491528 | tf_op jit(solution)/shard_map/ppermute | solution.py:359
  74.1 14.8 %collective-permute-start.20 = (f32[160,256]{1,0:T(8,128)S(1)}, f32[160,256]{1,0:T(8,128)S(1)}, u32[]{:S(2)}, u32[]{:S(2)}) collective-permute-start(f32[160,256]{1,0:T(8,128)S(1)} %add.79.refs_1_), channel_id=1, source_target_pairs={{0,8},{4,12},{8,0},{12,4},{16,24},{20,28},{24,16},{28,20},{1,9},{5... | collective-permute-start | bytes 491528 | tf_op jit(solution)/shard_map/ppermute | solution.py:359
  75.9 13.1 %collective-permute-start.18 = (f32[160,256]{1,0:T(8,128)S(1)}, f32[160,256]{1,0:T(8,128)S(1)}, u32[]{:S(2)}, u32[]{:S(2)}) collective-permute-start(f32[160,256]{1,0:T(8,128)S(1)} %add.79.refs_1_), channel_id=1, source_target_pairs={{0,4},{4,0},{8,12},{12,8},{16,20},{20,16},{24,28},{28,24},{1,5},{5... | collective-permute-start | bytes 491528 | tf_op jit(solution)/shard_map/ppermute | solution.py:359
  95.0 5.1 %collective-permute-start.23 = (f32[8,128,256]{2,1,0:T(8,128)S(1)}, f32[8,128,256]{2,1,0:T(8,128)S(1)}, u32[]{:S(2)}, u32[]{:S(2)}) collective-permute-start(f32[8,128,256]{2,1,0:T(8,128)S(1)} %bitcast.40), channel_id=1, source_target_pairs={{0,1},{1,0},{2,3},{3,2},{4,5},{5,4},{6,7},{7,6},{8,9},{9,8},{10,11... | collective-permute-start | bytes 3145736 | tf_op jit(solution)/shard_map/ppermute | solution.py:357
  95.1 4.7 %collective-permute-start.31 = (f32[256,256]{1,0:T(8,128)S(1)}, f32[256,256]{1,0:T(8,128)S(1)}, u32[]{:S(2)}, u32[]{:S(2)}) collective-permute-start(f32[256,256]{1,0:T(8,128)S(1)} %shard_map.73), channel_id=1, source_target_pairs={{0,1},{1,0},{2,3},{3,2},{4,5},{5,4},{6,7},{7,6},{8,9},{9,8},{10,11... | collective-permute-start | bytes 786440 | tf_op jit(solution)/shard_map/ppermute | solution.py:357
  99.8 14.9 %collective-permute-start.32 = (f32[256,256]{1,0:T(8,128)S(1)}, f32[256,256]{1,0:T(8,128)S(1)}, u32[]{:S(2)}, u32[]{:S(2)}) collective-permute-start(f32[256,256]{1,0:T(8,128)S(1)} %add.84), channel_id=1, source_target_pairs={{0,2},{1,3},{2,0},{3,1},{4,6},{5,7},{6,4},{7,5},{8,10},{9,11},{10,... | collective-permute-start | bytes 786440 | tf_op jit(solution)/shard_map/ppermute | solution.py:357
  100.4 15.8 %collective-permute-start.30 = (f32[128,256]{1,0:T(8,128)S(1)}, f32[128,256]{1,0:T(8,128)S(1)}, u32[]{:S(2)}, u32[]{:S(2)}) collective-permute-start(f32[128,256]{1,0:T(8,128)S(1)} %get-tuple-element.135), channel_id=1, source_target_pairs={{0,14},{1,15},{2,12},{3,13},{4,10},{5,11},{6,8},{7,9},{8,6},{9,7},... | collective-permute-start | bytes 393224 | tf_op jit(solution)/shard_map/ppermute | solution.py:362
  103.1 13.6 %collective-permute-start.29 = (f32[128,256]{1,0:T(8,128)S(1)}, f32[128,256]{1,0:T(8,128)S(1)}, u32[]{:S(2)}, u32[]{:S(2)}) collective-permute-start(f32[128,256]{1,0:T(8,128)S(1)} %get-tuple-element.136), channel_id=1, source_target_pairs={{0,10},{1,11},{2,8},{3,9},{4,14},{5,15},{6,12},{7,13},{8,2},{9,3},... | collective-permute-start | bytes 393224 | tf_op jit(solution)/shard_map/ppermute | solution.py:362
  104.1 18.2 %collective-permute-start.28 = (f32[128,256]{1,0:T(8,128)S(1)}, f32[128,256]{1,0:T(8,128)S(1)}, u32[]{:S(2)}, u32[]{:S(2)}) collective-permute-start(f32[128,256]{1,0:T(8,128)S(1)} %get-tuple-element.137), channel_id=1, source_target_pairs={{0,6},{1,7},{2,4},{3,5},{4,2},{5,3},{6,0},{7,1},{8,14},{9,15},{10,... | collective-permute-start | bytes 393224 | tf_op jit(solution)/shard_map/ppermute | solution.py:362
  106.0 16.2 %collective-permute-start.27 = (f32[128,256]{1,0:T(8,128)S(1)}, f32[128,256]{1,0:T(8,128)S(1)}, u32[]{:S(2)}, u32[]{:S(2)}) collective-permute-start(f32[128,256]{1,0:T(8,128)S(1)} %get-tuple-element.138), channel_id=1, source_target_pairs={{0,2},{1,3},{2,0},{3,1},{4,6},{5,7},{6,4},{7,5},{8,10},{9,11},{10,... | collective-permute-start | bytes 393224 | tf_op jit(solution)/shard_map/ppermute | solution.py:357
  114.7 7.6 %collective-permute-start.26 = (f32[128,256]{1,0:T(8,128)S(1)}, f32[128,256]{1,0:T(8,128)S(1)}, u32[]{:S(2)}, u32[]{:S(2)}) collective-permute-start(f32[128,256]{1,0:T(8,128)S(1)} %get-tuple-element.139), channel_id=1, source_target_pairs={{0,12},{4,8},{8,4},{12,0},{16,28},{20,24},{24,20},{28,16},{1,13},{... | collective-permute-start | bytes 393224 | tf_op jit(solution)/shard_map/ppermute | solution.py:359
  116.2 6.1 %collective-permute-start.25 = (f32[128,256]{1,0:T(8,128)S(1)}, f32[128,256]{1,0:T(8,128)S(1)}, u32[]{:S(2)}, u32[]{:S(2)}) collective-permute-start(f32[128,256]{1,0:T(8,128)S(1)} %get-tuple-element.140), channel_id=1, source_target_pairs={{0,8},{4,12},{8,0},{12,4},{16,24},{20,28},{24,16},{28,20},{1,9},{5... | collective-permute-start | bytes 393224 | tf_op jit(solution)/shard_map/ppermute | solution.py:359
  116.7 5.9 %collective-permute-start.24 = (f32[128,256]{1,0:T(8,128)S(1)}, f32[128,256]{1,0:T(8,128)S(1)}, u32[]{:S(2)}, u32[]{:S(2)}) collective-permute-start(f32[128,256]{1,0:T(8,128)S(1)} %get-tuple-element.141), channel_id=1, source_target_pairs={{0,4},{4,0},{8,12},{12,8},{16,20},{20,16},{24,28},{28,24},{1,5},{5... | collective-permute-start | bytes 393224 | tf_op jit(solution)/shard_map/ppermute | solution.py:359
  122.7 7.7 %collective-permute-start.33 = (f32[128,256]{1,0:T(8,128)S(1)}, f32[128,256]{1,0:T(8,128)S(1)}, u32[]{:S(2)}, u32[]{:S(2)}) collective-permute-start(f32[128,256]{1,0:T(8,128)S(1)} %fusion.6), channel_id=1, source_target_pairs={{0,24},{4,28},{8,16},{12,20},{16,8},{20,12},{24,0},{28,4},{1,25},{... | collective-permute-start | bytes 393224 | tf_op jit(solution)/shard_map/ppermute | solution.py:359
  130.8 7.6 %collective-permute-start.40 = (bf16[144,256]{1,0:T(8,128)(2,1)S(1)}, bf16[144,256]{1,0:T(8,128)(2,1)S(1)}, u32[]{:S(2)}, u32[]{:S(2)}) collective-permute-start(bf16[144,256]{1,0:T(8,128)(2,1)S(1)} %get-tuple-element.122), channel_id=1, source_target_pairs={{0,14},{1,15},{2,12},{3,13},{4,10},{5,11},{6,8},{7,9},{8,6},{9,7},... | collective-permute-start | bytes 221192 | tf_op jit(solution)/shard_map/ppermute | solution.py:362
  133.6 6.0 %collective-permute-start.39 = (bf16[144,256]{1,0:T(8,128)(2,1)S(1)}, bf16[144,256]{1,0:T(8,128)(2,1)S(1)}, u32[]{:S(2)}, u32[]{:S(2)}) collective-permute-start(bf16[144,256]{1,0:T(8,128)(2,1)S(1)} %get-tuple-element.122), channel_id=1, source_target_pairs={{0,10},{1,11},{2,8},{3,9},{4,14},{5,15},{6,12},{7,13},{8,2},{9,3},... | collective-permute-start | bytes 221192 | tf_op jit(solution)/shard_map/ppermute | solution.py:362
  134.5 11.0 %collective-permute-start.36 = (f32[128,256]{1,0:T(8,128)S(1)}, f32[128,256]{1,0:T(8,128)S(1)}, u32[]{:S(2)}, u32[]{:S(2)}) collective-permute-start(f32[128,256]{1,0:T(8,128)S(1)} %get-tuple-element.119.refs_0_), channel_id=1, source_target_pairs={{0,12},{4,8},{8,4},{12,0},{16,28},{20,24},{24,20},{28,16},{1,13},{... | collective-permute-start | bytes 393224 | tf_op jit(solution)/shard_map/ppermute | solution.py:359
  136.1 9.3 %collective-permute-start.35 = (f32[128,256]{1,0:T(8,128)S(1)}, f32[128,256]{1,0:T(8,128)S(1)}, u32[]{:S(2)}, u32[]{:S(2)}) collective-permute-start(f32[128,256]{1,0:T(8,128)S(1)} %get-tuple-element.119.refs_0_), channel_id=1, source_target_pairs={{0,8},{4,12},{8,0},{12,4},{16,24},{20,28},{24,16},{28,20},{1,9},{5... | collective-permute-start | bytes 393224 | tf_op jit(solution)/shard_map/ppermute | solution.py:359
  137.0 8.5 %collective-permute-start.34 = (f32[128,256]{1,0:T(8,128)S(1)}, f32[128,256]{1,0:T(8,128)S(1)}, u32[]{:S(2)}, u32[]{:S(2)}) collective-permute-start(f32[128,256]{1,0:T(8,128)S(1)} %get-tuple-element.119.refs_0_), channel_id=1, source_target_pairs={{0,4},{4,0},{8,12},{12,8},{16,20},{20,16},{24,28},{28,24},{1,5},{5... | collective-permute-start | bytes 393224 | tf_op jit(solution)/shard_map/ppermute | solution.py:359
  138.5 7.0 %collective-permute-start.38 = (bf16[144,256]{1,0:T(8,128)(2,1)S(1)}, bf16[144,256]{1,0:T(8,128)(2,1)S(1)}, u32[]{:S(2)}, u32[]{:S(2)}) collective-permute-start(bf16[144,256]{1,0:T(8,128)(2,1)S(1)} %get-tuple-element.122), channel_id=1, source_target_pairs={{0,6},{1,7},{2,4},{3,5},{4,2},{5,3},{6,0},{7,1},{8,14},{9,15},{10,... | collective-permute-start | bytes 221192 | tf_op jit(solution)/shard_map/ppermute | solution.py:362
  139.6 5.8 %collective-permute-start.37 = (bf16[144,256]{1,0:T(8,128)(2,1)S(1)}, bf16[144,256]{1,0:T(8,128)(2,1)S(1)}, u32[]{:S(2)}, u32[]{:S(2)}) collective-permute-start(bf16[144,256]{1,0:T(8,128)(2,1)S(1)} %get-tuple-element.122), channel_id=1, source_target_pairs={{0,2},{1,3},{2,0},{3,1},{4,6},{5,7},{6,4},{7,5},{8,10},{9,11},{10,... | collective-permute-start | bytes 221192 | tf_op jit(solution)/shard_map/ppermute | solution.py:357
  146.2 2.0 %collective-permute-start.41 = (bf16[1040,256]{1,0:T(8,128)(2,1)S(1)}, bf16[1040,256]{1,0:T(8,128)(2,1)S(1)}, u32[]{:S(2)}, u32[]{:S(2)}) collective-permute-start(bf16[1040,256]{1,0:T(8,128)(2,1)S(1)} %get-tuple-element.131.side_ref), channel_id=1, source_target_pairs={{0,1},{1,0},{2,3},{3,2},{4,5},{5,4},{6,7},{7,6},{8,9},{9,8},{10,11... | collective-permute-start | bytes 1597448 | tf_op jit(solution)/shard_map/ppermute | solution.py:357
  (4 other events, 5.8 us)
